TPU v7x, 128 devices: a whole 4x4x4 slice. The times are simulated.
128 devices in a mesh: lat: 8 (over z, y_hi), lon: 16 (over x, y_lo, core).
Axes of the slice: x: 4, y: 4 (y_hi: 2, y_lo: 2; y = y_hi * 2 + y_lo), z: 4, core: 2. Of those that a mesh axis runs over, the one named last changes fastest.
Arguments:
- grid_feats: float32 [8, 32, 128, 1024], P('lat', 'lon'), may hold values from -6 to 6
- lift_index: int32 [8, 48, 4], P('lat', 'lon'), may hold values from 0 to 255, as said below
- lift_weight: float32 [8, 48, 4, 128, 128], P('lat', 'lon'), may hold values from -0.25 to 0.25
- window_index: int32 [8, 48, 8], P('lat', 'lon'), may hold values from 0 to 383, as said below
- window_count: int32 [8, 48], P('lat', 'lon'), may hold values from 4 to 8
- norm_gains: float32 [2, 1024], replicated, may hold values from 0.5 to 1.5
- qkv_weight: bfloat16 [1024, 3072], replicated, may hold values from -6.5 to 6.5
- out_weight: bfloat16 [1024, 1024], replicated, may hold values from -0.1875 to 0.1875
- up_weight: bfloat16 [1024, 2048], replicated, may hold values from -0.1875 to 0.1875
- down_weight: bfloat16 [2048, 1024], replicated, may hold values from -0.125 to 0.125
- return_index: int32 [8, 32, 4], P('lat', 'lon'), may hold values from 0 to 383, as said below
- return_weight: float32 [8, 32, 4, 128, 128], P('lat', 'lon'), may hold values from -0.25 to 0.25
Outputs:
- grid_out: float32 [8, 32, 128, 1024], P('lat', 'lon')
Inputs may be any that keep to these rules, and one draw needn't show every extreme that they name: `lift_index`: entries name grid blocks a' * 32 + b'; the 4 entries of a row differ; for mesh block (a, c), |a' - a| <= 1 and b' lies among the 4 columns from c // 3 * 2 - 1 to c // 3 * 2 + 2, counted modulo 32. `window_index`: entries name mesh blocks a' * 48 + c'; slot 0 is the query block itself, the 8 entries of a row differ; |a' - a| <= 1 and c' lies among the 5 columns from c // 3 * 3 - 1 to c // 3 * 3 + 3, counted modulo 48. `return_index`: entries name mesh blocks a' * 48 + c'; the 4 entries of a row differ; for grid block (a, b), |a' - a| <= 1 and c' lies among the 5 columns from b // 2 * 3 - 1 to b // 2 * 3 + 3, counted modulo 48.
All inputs are finite; a program needn't handle non-finite values.
Results may differ from a plain program's by a relative error of at most 0.0035.
Values may be sent and summed in bfloat16 or wider, within the bound.
No kernel may reach another device: no remote copies, remote signals or barrier semaphores. Data moves between devices by JAX's collectives and lax.ppermute only.
A program may use at most 128 MiB of HBM per device.

v0:
```python
import jax
import jax.numpy as jnp
from jax import lax
from jax.experimental import pallas as pl
from jax.experimental.pallas import tpu as pltpu
from jax.sharding import PartitionSpec as P


HEADS = 16
EPSILON = 1e-05
AXES = ("lat", "lon")
GRID_SCALE = 8192.0


def far_band(band):
    return band - 1 if band % 2 == 0 else band + 1


def relay_band(band):
    return band + 2 if band % 2 == 0 else band - 2


def outer_sector(sector):
    return sector - 1 if sector % 2 == 0 else sector + 1


def move(values, band_of, sector_of):
    bands, sectors = lax.axis_size("lat"), lax.axis_size("lon")
    pairs = []
    for band in range(bands):
        for sector in range(sectors):
            target = band_of(band)
            if 0 <= target < bands:
                pairs.append((band * sectors + sector, target * sectors + sector_of(sector) % sectors))
    return lax.ppermute(values, AXES, pairs)


def same(index):
    return index


def pair(index):
    return index ^ 1


def exchange(blocks, even_sector):
    last = blocks.shape[0] - 1
    parts = (blocks[:last], blocks[last:])

    def inner_edge(halves):
        return jnp.where(even_sector, halves[1], halves[0][:1])

    edge_out = jnp.where(even_sector, parts[0][:1], parts[1])
    near = [move(part, pair, same) for part in parts]
    outer = [
        move(edge_out, same, outer_sector), move(edge_out, pair, outer_sector), move(edge_out, far_band, outer_sector)
    ]
    far = [move(part, relay_band, same) for part in near]
    inner = [
        move(jnp.concatenate([inner_edge(parts), inner_edge(near)], axis=0), same, pair),
        move(inner_edge(far), same, pair),
    ]
    return near, far, outer, inner


def table_slots(global_ids, total_lon, blocks_here):
    band_here = lax.axis_index("lat")
    sector_here = lax.axis_index("lon")
    band_step = global_ids // total_lon - band_here
    column = (global_ids % total_lon - sector_here * blocks_here + 1) % total_lon
    near_step = jnp.where(band_here % 2 == 0, 1, -1)
    group = jnp.where(band_step == 0, 0, jnp.where(band_step == near_step, 1, 2))
    outer_column = jnp.where(sector_here % 2 == 0, 0, blocks_here + 1)
    inside = group * blocks_here + column - 1
    outside = 3 * blocks_here + jnp.where(column == outer_column, 0, 3) + group
    own_column = jnp.logical_and(column >= 1, column <= blocks_here)
    return jnp.where(own_column, inside, outside)


def fill_table(pieces, table, sems):
    copies = []
    start = 0
    for place, piece in enumerate(pieces):
        count = piece.shape[0]
        copies.append(pltpu.make_async_copy(piece, table.at[pl.ds(start, count)], sems.at[place]))
        start += count
    return copies


def normalise(values, gain):
    centred = values - jnp.mean(values, axis=-1, keepdims=True)
    spread = jnp.mean(centred * centred, axis=-1, keepdims=True)
    return (centred * lax.rsqrt(spread + EPSILON) * gain).astype(jnp.bfloat16)


def split_weights(weight, split):
    count, rows, width = weight.shape
    for k in range(count):
        full = weight[k]
        upper = full.astype(jnp.bfloat16)
        split[0:rows, k * width:(k + 1) * width] = upper
        split[rows:2 * rows, k * width:(k + 1) * width] = (full - upper.astype(jnp.float32)).astype(jnp.bfloat16)


def mix_blocks(slots, place, weight, table, upper, lower, split):
    count, rows, width = weight.shape
    split_weights(weight, split)
    for k in range(count):
        block = table[slots[place * count + k]]
        high = block.astype(jnp.bfloat16)
        upper[k * width:(k + 1) * width, :] = high
        if lower is not None:
            lower[k * width:(k + 1) * width, :] = (block - high.astype(jnp.float32)).astype(jnp.bfloat16)
    both = jnp.dot(split[...], upper[...], preferred_element_type=jnp.float32)
    total = both[:rows] + both[rows:]
    if lower is not None:
        total = total + jnp.dot(split[0:rows, :], lower[...], preferred_element_type=jnp.float32)
    return total


def lift_kernel(slots, *refs, piece_count):
    pieces = refs[:piece_count]
    weight, gains, mesh_in, normed, table, upper, lower, split, sems = refs[piece_count:]
    copies = fill_table(pieces, table, sems)
    for copy in copies:
        copy.start()
    for copy in copies:
        copy.wait()
    for m in range(weight.shape[0]):
        mixed = mix_blocks(slots, m, weight.at[m], table, upper, lower, split)
        mesh_in[m] = mixed
        normed[m] = normalise(mixed, gains[0:1, :])


def return_kernel(slots, *refs, piece_count):
    pieces = refs[:piece_count]
    weight, out, table, upper, split, sems = refs[piece_count:]
    copies = fill_table(pieces, table, sems)
    for copy in copies:
        copy.start()
    for copy in copies:
        copy.wait()
    for g in range(weight.shape[0]):
        out[g] = mix_blocks(slots, g, weight.at[g], table, upper, None, split)


def layer_kernel(slots, counts, *refs, piece_count):
    pieces = refs[:piece_count]
    (
        queries, mesh_in, gains, out_hbm, up_hbm, down_hbm, mesh_out,
        table, keys, values, mixed, out_weight, up_weight, down_weight, sems,
    ) = refs[piece_count:]
    copies = fill_table(pieces, table, sems)
    weights = [
        pltpu.make_async_copy(out_hbm, out_weight, sems.at[piece_count]),
        pltpu.make_async_copy(up_hbm, up_weight, sems.at[piece_count + 1]),
        pltpu.make_async_copy(down_hbm, down_weight, sems.at[piece_count + 2]),
    ]
    for copy in copies + weights:
        copy.start()
    for copy in copies:
        copy.wait()
    mesh_blocks, rows, width = mesh_in.shape
    neighbours = keys.shape[0] // rows
    head_size = width // HEADS
    wide = 2 * head_size
    certain = neighbours // 2 * rows
    low_half = lax.broadcasted_iota(jnp.int32, (rows, wide), 1) < head_size
    key_block = lax.broadcasted_iota(jnp.int32, (1, neighbours * rows - certain), 1) // rows + neighbours // 2
    values[:, :, wide:] = jnp.ones((HEADS // 2, neighbours * rows, wide), jnp.bfloat16)

    def attend(m, carry):
        for j in range(neighbours):
            slot = slots[m * neighbours + j]
            keys[j * rows:(j + 1) * rows, :] = table[slot, :, 0:width]
            for h in range(HEADS // 2):
                at = width + h * wide
                values[h, j * rows:(j + 1) * rows, 0:wide] = table[slot, :, at:at + wide]
        bias = jnp.where(key_block < counts[m], 0.0, -1e30)
        for h in range(HEADS // 2):
            at = h * wide
            query = queries[m, :, at:at + wide] * jnp.asarray(head_size ** (-0.5), jnp.bfloat16)
            none = jnp.zeros_like(query)
            pair_rows = jnp.concatenate(
                [jnp.where(low_half, query, none), jnp.where(low_half, none, query)], axis=0
            )
            scores = lax.dot_general(
                pair_rows, keys[:, at:at + wide], (((1,), (1,)), ((), ())), preferred_element_type=jnp.float32
            )
            first, second = scores[:, :certain], scores[:, certain:] + bias
            highest = jnp.maximum(
                jnp.max(first, axis=-1, keepdims=True), jnp.max(second, axis=-1, keepdims=True)
            )
            raw = jnp.concatenate(
                [jnp.exp(first - highest).astype(jnp.bfloat16), jnp.exp(second - highest).astype(jnp.bfloat16)],
                axis=1,
            )
            summed = jnp.dot(raw, values[h], preferred_element_type=jnp.float32)
            part = summed[:, :wide] / summed[:, wide:]
            mixed[pl.ds(m * rows, rows), at:at + wide] = jnp.where(
                low_half, part[:rows], part[rows:]
            ).astype(jnp.bfloat16)
        return carry

    lax.fori_loop(0, mesh_blocks, attend, 0)
    for copy in weights:
        copy.wait()
    after = mesh_in[...].reshape(mesh_blocks * rows, width) + jnp.dot(
        mixed[...], out_weight[...], preferred_element_type=jnp.float32
    )
    again = normalise(after, gains[1:2, :])
    hidden = jnp.dot(again, up_weight[...], preferred_element_type=jnp.float32)
    hidden = (0.5 * hidden * (1.0 + lax.erf(hidden * 0.7071067811865476))).astype(jnp.bfloat16)
    result = after + jnp.dot(hidden, down_weight[...], preferred_element_type=jnp.float32)
    mesh_out[...] = result.astype(jnp.bfloat16).reshape(mesh_blocks, rows, width)


def any_specs(count):
    return [pl.BlockSpec(memory_space=pl.ANY)] * count


VMEM_SPEC = pl.BlockSpec(memory_space=pltpu.MemorySpace.VMEM)


def shards(
    grid_feats, lift_index, lift_weight, window_index, window_count, norm_gains,
    qkv_weight, out_weight, up_weight, down_weight, return_index, return_weight,
):
    even_sector = lax.axis_index("lon") % 2 == 0
    lon_count = lax.axis_size("lon")
    grid_blocks = grid_feats.shape[1]
    mesh_blocks = lift_index.shape[1]
    rows, width = grid_feats.shape[2:]
    grid_lon = grid_blocks * lon_count
    mesh_lon = mesh_blocks * lon_count
    bf16, f32 = jnp.bfloat16, jnp.float32
    mesh_table = 3 * mesh_blocks + 6
    grid_table = 3 * grid_blocks + 6

    own_grid = grid_feats[0]
    sent = (own_grid * GRID_SCALE).astype(jnp.float16)
    near, far, outer, inner = exchange(sent, even_sector)
    grid_pieces = [own_grid] + [
        piece.astype(f32) * (1.0 / GRID_SCALE) for piece in near + far + outer + inner
    ]
    lift_slots = table_slots(lift_index[0], grid_lon, grid_blocks).reshape(-1)
    picks = lift_weight.shape[2]
    mesh_in, normed = pl.pallas_call(
        lambda *refs: lift_kernel(*refs, piece_count=len(grid_pieces)),
        grid_spec=pltpu.PrefetchScalarGridSpec(
            num_scalar_prefetch=1,
            in_specs=any_specs(len(grid_pieces)) + [VMEM_SPEC, VMEM_SPEC],
            out_specs=[VMEM_SPEC, VMEM_SPEC],
            scratch_shapes=[
                pltpu.VMEM((grid_table, rows, width), f32),
                pltpu.VMEM((picks * rows, width), bf16),
                pltpu.VMEM((picks * rows, width), bf16),
                pltpu.VMEM((2 * rows, picks * rows), bf16),
                pltpu.SemaphoreType.DMA((len(grid_pieces),)),
            ],
        ),
        out_shape=[
            jax.ShapeDtypeStruct((mesh_blocks, rows, width), f32),
            jax.ShapeDtypeStruct((mesh_blocks, rows, width), bf16),
        ],
        name="lift",
    )(lift_slots, *grid_pieces, lift_weight[0], norm_gains)

    near, far, outer, inner = exchange(normed, even_sector)
    own = jnp.dot(normed.reshape(-1, width), qkv_weight, preferred_element_type=f32).astype(bf16)
    queries = own[:, :width].reshape(mesh_blocks, rows, width)
    kv_weight = qkv_weight[:, width:]
    kv_pieces = [own[:, width:].reshape(mesh_blocks, rows, 2 * width)]

    def project(group):
        stacked = jnp.concatenate(group, axis=0) if len(group) > 1 else group[0]
        return (
            jnp.dot(stacked.reshape(-1, width), kv_weight, preferred_element_type=f32)
            .astype(bf16)
            .reshape(-1, rows, 2 * width)
        )

    kv_pieces.append(project(near))
    side = project(outer + inner[:1])
    kv_pieces.append(project(far))
    kv_pieces.append(side)
    kv_pieces.append(project(inner[1:]))
    window_slots = table_slots(window_index[0], mesh_lon, mesh_blocks).reshape(-1)
    neighbours = window_index.shape[2]
    hidden_width = up_weight.shape[1]
    mesh_out = pl.pallas_call(
        lambda *refs: layer_kernel(*refs, piece_count=len(kv_pieces)),
        grid_spec=pltpu.PrefetchScalarGridSpec(
            num_scalar_prefetch=2,
            in_specs=any_specs(len(kv_pieces)) + [VMEM_SPEC] * 3 + any_specs(3),
            out_specs=VMEM_SPEC,
            scratch_shapes=[
                pltpu.VMEM((mesh_table, rows, 2 * width), bf16),
                pltpu.VMEM((neighbours * rows, width), bf16),
                pltpu.VMEM((HEADS // 2, neighbours * rows, 4 * (width // HEADS)), bf16),
                pltpu.VMEM((mesh_blocks * rows, width), bf16),
                pltpu.VMEM((width, width), bf16),
                pltpu.VMEM((width, hidden_width), bf16),
                pltpu.VMEM((hidden_width, width), bf16),
                pltpu.SemaphoreType.DMA((len(kv_pieces) + 3,)),
            ],
        ),
        out_shape=jax.ShapeDtypeStruct((mesh_blocks, rows, width), bf16),
        name="layer",
    )(
        window_slots, window_count[0], *kv_pieces, queries, mesh_in, norm_gains,
        out_weight, up_weight, down_weight,
    )

    near, far, outer, inner = exchange(mesh_out, even_sector)
    mesh_pieces = [mesh_out] + near + far + outer + inner
    return_slots = table_slots(return_index[0], mesh_lon, mesh_blocks).reshape(-1)
    grid_out = pl.pallas_call(
        lambda *refs: return_kernel(*refs, piece_count=len(mesh_pieces)),
        grid_spec=pltpu.PrefetchScalarGridSpec(
            num_scalar_prefetch=1,
            in_specs=any_specs(len(mesh_pieces)) + [VMEM_SPEC],
            out_specs=VMEM_SPEC,
            scratch_shapes=[
                pltpu.VMEM((mesh_table, rows, width), bf16),
                pltpu.VMEM((picks * rows, width), bf16),
                pltpu.VMEM((2 * rows, picks * rows), bf16),
                pltpu.SemaphoreType.DMA((len(mesh_pieces),)),
            ],
        ),
        out_shape=jax.ShapeDtypeStruct((grid_blocks, rows, width), f32),
        name="give_back",
    )(return_slots, *mesh_pieces, return_weight[0])
    return grid_out.reshape(1, grid_blocks, rows, width)


def solution(mesh):
    placed = (
        P("lat", "lon", None, None),
        P("lat", "lon", None),
        P("lat", "lon", None, None, None),
        P("lat", "lon", None),
        P("lat", "lon"),
        P(),
        P(),
        P(),
        P(),
        P(),
        P("lat", "lon", None),
        P("lat", "lon", None, None, None),
    )

    return jax.shard_map(shards, mesh=mesh, in_specs=placed, out_specs=P("lat", "lon", None, None), check_vma=False)
```

profile of v0, /device:TPU:21, one launch (start us, length us, event | category | flops | bytes accessed | tf_op | source)
XLA Modules:
  0.0 193.6 jit_solution(12143424303278596462)
XLA Ops:
  0.0 1.3 multiply_convert_fusion
  1.3 0.2 broadcast_select_fusion.6
  1.5 4.0 %collective-permute-start.6 = (f16[1,128,1024]{2,1,0:T(8,128)(2,1)S(1)}, f16[1,128,1024]{2,1,0:T(8,128)(2,1)S(1)}, u32[]{:S(2)}, u32[]{:S(2)}) collective-permute-start(f16[1,128,1024]{2,1,0:T(8,128)(2,1)S(1)} %get-tuple-element.20), channel_id=1, source_target_pairs={{16,47},{17,34},{18,33},{19,36},{20,35},{21,38},{22,37},{23,40},{2... | collective-permute-start | bytes 786440 | tf_op jit(solution)/shard_map/ppermute | solution.py:35
  5.6 0.6 collective-permute-start.4
  6.2 2.3 %collective-permute-start.1 = (f16[1,128,1024]{2,1,0:T(8,128)(2,1)S(1)}, f16[1,128,1024]{2,1,0:T(8,128)(2,1)S(1)}, u32[]{:S(2)}, u32[]{:S(2)}) collective-permute-start(f16[1,128,1024]{2,1,0:T(8,128)(2,1)S(1)} %get-tuple-element.18), channel_id=1, source_target_pairs={{0,16},{1,17},{2,18},{3,19},{4,20},{5,21},{6,22},{7,23},{8,24},{9,... | collective-permute-start | bytes 786440 | tf_op jit(solution)/shard_map/ppermute | solution.py:35
  8.6 0.6 collective-permute-start
  9.2 0.7 reduce.3
  10.0 0.7 divide_reduce_fusion
  10.7 0.6 and_select_fusion.1.refs_0_
  11.3 0.7 compare_reduce_fusion
  12.2 0.6 and_select_fusion.5.refs_0_
  12.8 8.4 %collective-permute-done.1 = f16[1,128,1024]{2,1,0:T(8,128)(2,1)S(1)} collective-permute-done((f16[1,128,1024]{2,1,0:T(8,128)(2,1)S(1)}, f16[1,128,1024]{2,1,0:T(8,128)(2,1)S(1)}, u32[]{:S(2)}, u32[]{:S(2)}) %collective-permute-start.1) | collective-permute-done | bytes 262176 | tf_op jit(solution)/shard_map/ppermute | solution.py:35
  21.2 5.3 %collective-permute-done = f16[1,128,1024]{2,1,0:T(8,128)(2,1)S(1)} collective-permute-done((f16[1,128,1024]{2,1,0:T(8,128)(2,1)S(1)}, f16[1,128,1024]{2,1,0:T(8,128)(2,1)S(1)}, u32[]{:S(2)}, u32[]{:S(2)}) %collective-permute-start) | collective-permute-done | bytes 262176 | tf_op jit(solution)/shard_map/ppermute | solution.py:35
  26.8 0.5 collective-permute-start.7
  27.2 1.3 collective-permute-start.3
  28.5 0.9 convert_multiply_fusion.7.refs_3_
  29.4 0.9 convert_multiply_fusion.8.refs_2_
  30.3 1.3 collective-permute-start.2
  31.6 0.9 convert_multiply_fusion.2.refs_8_
  32.4 0.9 convert_multiply_fusion.3.refs_7_
  33.3 0.9 convert_multiply_fusion.4.refs_6_
  34.2 3.7 %collective-permute-done.3 = f16[1,128,1024]{2,1,0:T(8,128)(2,1)S(1)} collective-permute-done((f16[1,128,1024]{2,1,0:T(8,128)(2,1)S(1)}, f16[1,128,1024]{2,1,0:T(8,128)(2,1)S(1)}, u32[]{:S(2)}, u32[]{:S(2)}) %collective-permute-start.3) | collective-permute-done | bytes 262176 | tf_op jit(solution)/shard_map/ppermute | solution.py:35
  37.8 5.6 %collective-permute-done.2 = f16[1,128,1024]{2,1,0:T(8,128)(2,1)S(1)} collective-permute-done((f16[1,128,1024]{2,1,0:T(8,128)(2,1)S(1)}, f16[1,128,1024]{2,1,0:T(8,128)(2,1)S(1)}, u32[]{:S(2)}, u32[]{:S(2)}) %collective-permute-start.2) | collective-permute-done | bytes 262176 | tf_op jit(solution)/shard_map/ppermute | solution.py:35
  43.6 0.7 collective-permute-start.8
  44.2 0.9 convert_multiply_fusion.6.refs_4_
  45.1 0.9 convert_multiply_fusion.5.refs_5_
  46.0 0.9 convert_multiply_fusion.1.refs_10_
  46.8 1.1 convert_multiply_fusion.refs_9_
  47.9 7.7 %lift.1 = (f32[3,128,1024]{2,1,0:T(8,128)}, bf16[3,128,1024]{2,1,0:T(8,128)(2,1)}) custom-call(s32[12]{0:T(128)} %and_select_fusion.1.refs_0_, f32[2,128,1024]{2,1,0:T(8,128)} %bitcast.26, f32[1,128,1024]{2,1,0:T(8,128)} %convert_multiply_fusion.8.refs_2_, f32[1,128,1024]{2,1,0:T(8,128)} %convert_multiply_fusion.7.refs_3_, ...), custom_call_target="tpu_custom_call" | custom-call | tf_op jit(solution)/shard_map/lift/pallas_call | solution.py:248
  55.6 1.1 slice.52
  56.7 1.2 broadcast_select_fusion.3
  57.9 3.6 %collective-permute-start.15 = (bf16[1,128,1024]{2,1,0:T(8,128)(2,1)S(1)}, bf16[1,128,1024]{2,1,0:T(8,128)(2,1)S(1)}, u32[]{:S(2)}, u32[]{:S(2)}) collective-permute-start(bf16[1,128,1024]{2,1,0:T(8,128)(2,1)S(1)} %get-tuple-element.14), channel_id=1, source_target_pairs={{16,47},{17,34},{18,33},{19,36},{20,35},{21,38},{22,37},{23,40},{2... | collective-permute-start | bytes 786440 | tf_op jit(solution)/shard_map/ppermute | solution.py:35
  61.7 2.8 %collective-permute-start.13 = (bf16[1,128,1024]{2,1,0:T(8,128)(2,1)S(1)}, bf16[1,128,1024]{2,1,0:T(8,128)(2,1)S(1)}, u32[]{:S(2)}, u32[]{:S(2)}) collective-permute-start(bf16[1,128,1024]{2,1,0:T(8,128)(2,1)S(1)} %get-tuple-element.14), channel_id=1, source_target_pairs={{0,15},{1,2},{2,1},{3,4},{4,3},{5,6},{6,5},{7,8},{8,7},{9,10},{10,... | collective-permute-start | bytes 786440 | tf_op jit(solution)/shard_map/ppermute | solution.py:35
  64.5 1.7 collective-permute-start.9
  66.2 1.3 collective-permute-start.10
  67.4 5.8 %convolution_convert_fusion = bf16[384,3072]{1,0:T(8,128)(2,1)S(1)} fusion(bf16[384,1024]{1,0:T(8,128)(2,1)} %bitcast.31, bf16[1024,3072]{1,0:T(8,128)(2,1)} %param.18), kind=kOutput, calls=%fused_computation | convolution fusion | flops 2417098752 | bytes 9437184 | tf_op jit(solution)/shard_map/dot_general | solution.py:270
  73.2 0.9 slice.69
  74.2 1.3 slice.66
  75.5 14.3 %collective-permute-done.10 = bf16[1,128,1024]{2,1,0:T(8,128)(2,1)S(1)} collective-permute-done((bf16[1,128,1024]{2,1,0:T(8,128)(2,1)S(1)}, bf16[1,128,1024]{2,1,0:T(8,128)(2,1)S(1)}, u32[]{:S(2)}, u32[]{:S(2)}) %collective-permute-start.10) | collective-permute-done | bytes 262176 | tf_op jit(solution)/shard_map/ppermute | solution.py:35
  89.8 1.3 collective-permute-start.12
  91.1 1.3 collective-permute-start.11
  92.5 6.6 %collective-permute-done.12 = bf16[1,128,1024]{2,1,0:T(8,128)(2,1)S(1)} collective-permute-done((bf16[1,128,1024]{2,1,0:T(8,128)(2,1)S(1)}, bf16[1,128,1024]{2,1,0:T(8,128)(2,1)S(1)}, u32[]{:S(2)}, u32[]{:S(2)}) %collective-permute-start.12) | collective-permute-done | bytes 262176 | tf_op jit(solution)/shard_map/ppermute | solution.py:35
  99.1 2.1 %collective-permute-start.16 = (bf16[2,128,1024]{2,1,0:T(8,128)(2,1)S(1)}, bf16[2,128,1024]{2,1,0:T(8,128)(2,1)S(1)}, u32[]{:S(2)}, u32[]{:S(2)}) collective-permute-start(bf16[2,128,1024]{2,1,0:T(8,128)(2,1)S(1)} %pad_maximum_fusion.4), channel_id=1, source_target_pairs={{0,1},{1,0},{2,3},{3,2},{4,5},{5,4},{6,7},{7,6},{8,9},{9,8},{10,11... | collective-permute-start | bytes 1572872 | tf_op jit(solution)/shard_map/ppermute | solution.py:35
  101.2 3.0 %convolution_convert_fusion.3 = bf16[384,2048]{1,0:T(8,128)(2,1)} fusion(bf16[384,1024]{1,0:T(8,128)(2,1)S(1)} %bitcast.33, bf16[1024,3072]{1,0:T(8,128)(2,1)S(1)} %bitcast.39), kind=kOutput, calls=%fused_computation.3 | convolution fusion | flops 1611399168 | bytes 6553600 | tf_op jit(solution)/shard_map/dot_general | solution.py:278
  104.2 6.2 %collective-permute-done.11 = bf16[2,128,1024]{2,1,0:T(8,128)(2,1)S(1)} collective-permute-done((bf16[2,128,1024]{2,1,0:T(8,128)(2,1)S(1)}, bf16[2,128,1024]{2,1,0:T(8,128)(2,1)S(1)}, u32[]{:S(2)}, u32[]{:S(2)}) %collective-permute-start.11) | collective-permute-done | bytes 524320 | tf_op jit(solution)/shard_map/ppermute | solution.py:35
  110.4 1.5 collective-permute-start.17
  112.1 4.2 %convolution_convert_fusion.1 = bf16[640,2048]{1,0:T(8,128)(2,1)} fusion(bf16[640,1024]{1,0:T(8,128)(2,1)S(1)} %bitcast.32, bf16[1024,3072]{1,0:T(8,128)(2,1)S(1)} %bitcast.39), kind=kOutput, calls=%fused_computation.1 | convolution fusion | flops 2685665280 | bytes 8126464 | tf_op jit(solution)/shard_map/dot_general | solution.py:278
  116.3 3.0 %convolution_convert_fusion.2 = bf16[384,2048]{1,0:T(8,128)(2,1)} fusion(bf16[384,1024]{1,0:T(8,128)(2,1)S(1)} %bitcast.34, bf16[1024,3072]{1,0:T(8,128)(2,1)S(1)} %bitcast.39), kind=kOutput, calls=%fused_computation.2 | convolution fusion | flops 1611399168 | bytes 6553600 | tf_op jit(solution)/shard_map/dot_general | solution.py:278
  119.4 1.5 fusion.8.refs_6_
  120.9 20.6 %layer.1.refs_1_ = bf16[3,128,1024]{2,1,0:T(8,128)(2,1)} custom-call(s32[24]{0:T(128)} %and_select_fusion.5.refs_0_, s32[3]{0:T(128)} %bitcast.37, bf16[3,128,2048]{2,1,0:T(8,128)(2,1)} %bitcast.25, bf16[3,128,2048]{2,1,0:T(8,128)(2,1)} %bitcast.29, bf16[3,128,2048]{2,1,0:T(8,128)(2,1)} %bitcast.30, bf16[5,128,2048]{2,1,0:T(8,128)(2,1)} %bitcast.28, ...), custom_call_target="tpu_custom_call" | custom-call | tf_op jit(solution)/shard_map/layer/pallas_call | solution.py:291
  141.5 1.1 slice.70
  142.6 1.0 collective-permute-start.18
  143.5 1.1 broadcast_select_fusion
  144.6 2.1 %collective-permute-start.19 = (bf16[1,128,1024]{2,1,0:T(8,128)(2,1)S(1)}, bf16[1,128,1024]{2,1,0:T(8,128)(2,1)S(1)}, u32[]{:S(2)}, u32[]{:S(2)}) collective-permute-start(bf16[1,128,1024]{2,1,0:T(8,128)(2,1)S(1)} %get-tuple-element.12), channel_id=1, source_target_pairs={{0,16},{1,17},{2,18},{3,19},{4,20},{5,21},{6,22},{7,23},{8,24},{9,... | collective-permute-start | bytes 786440 | tf_op jit(solution)/shard_map/ppermute | solution.py:35
  146.8 10.8 %collective-permute-done.18.refs_2_ = bf16[2,128,1024]{2,1,0:T(8,128)(2,1)S(1)} collective-permute-done((bf16[2,128,1024]{2,1,0:T(8,128)(2,1)S(1)}, bf16[2,128,1024]{2,1,0:T(8,128)(2,1)S(1)}, u32[]{:S(2)}, u32[]{:S(2)}) %collective-permute-start.18) | collective-permute-done | bytes 524320 | tf_op jit(solution)/shard_map/ppermute | solution.py:35
  157.6 1.3 collective-permute-start.20
  158.9 7.8 %collective-permute-start.24 = (bf16[1,128,1024]{2,1,0:T(8,128)(2,1)S(1)}, bf16[1,128,1024]{2,1,0:T(8,128)(2,1)S(1)}, u32[]{:S(2)}, u32[]{:S(2)}) collective-permute-start(bf16[1,128,1024]{2,1,0:T(8,128)(2,1)S(1)} %get-tuple-element.13), channel_id=1, source_target_pairs={{16,47},{17,34},{18,33},{19,36},{20,35},{21,38},{22,37},{23,40},{2... | collective-permute-start | bytes 786440 | tf_op jit(solution)/shard_map/ppermute | solution.py:35
  167.0 1.3 collective-permute-start.21
  168.4 14.5 %collective-permute-done.21.refs_5_ = bf16[1,128,1024]{2,1,0:T(8,128)(2,1)S(1)} collective-permute-done((bf16[1,128,1024]{2,1,0:T(8,128)(2,1)S(1)}, bf16[1,128,1024]{2,1,0:T(8,128)(2,1)S(1)}, u32[]{:S(2)}, u32[]{:S(2)}) %collective-permute-start.21) | collective-permute-done | bytes 262176 | tf_op jit(solution)/shard_map/ppermute | solution.py:35
  182.8 2.2 %collective-permute-start.25 = (bf16[2,128,1024]{2,1,0:T(8,128)(2,1)S(1)}, bf16[2,128,1024]{2,1,0:T(8,128)(2,1)S(1)}, u32[]{:S(2)}, u32[]{:S(2)}) collective-permute-start(bf16[2,128,1024]{2,1,0:T(8,128)(2,1)S(1)} %pad_maximum_fusion.5), channel_id=1, source_target_pairs={{0,1},{1,0},{2,3},{3,2},{4,5},{5,4},{6,7},{7,6},{8,9},{9,8},{10,11... | collective-permute-start | bytes 1572872 | tf_op jit(solution)/shard_map/ppermute | solution.py:35
  185.1 0.8 slice_select_fusion
  186.2 0.6 and_select_fusion.9.refs_0_
  186.8 0.9 collective-permute-done.26.refs_10_
  187.8 5.6 %give_back.1 = f32[2,128,1024]{2,1,0:T(8,128)} custom-call(s32[8]{0:T(128)} %and_select_fusion.9.refs_0_, bf16[3,128,1024]{2,1,0:T(8,128)(2,1)} %layer.1.refs_1_, bf16[2,128,1024]{2,1,0:T(8,128)(2,1)} %copy-done, bf16[1,128,1024]{2,1,0:T(8,128)(2,1)} %copy-done.2, bf16[2,128,1024]{2,1,0:T(8,128)(2,1)} %copy-done.1, bf16[1,128,1024]{2,1,0:T(8,128)(2,1)} %copy-done.3, ...), custom_call_target="tpu_custom_call" | custom-call | tf_op jit(solution)/shard_map/give_back/pallas_call | solution.py:318
  (63 shorter events, 1.9 us)
Async XLA Ops:
  1.5 28.7 %collective-permute-start.6 = (f16[1,128,1024]{2,1,0:T(8,128)(2,1)S(1)}, f16[1,128,1024]{2,1,0:T(8,128)(2,1)S(1)}, u32[]{:S(2)}, u32[]{:S(2)}) collective-permute-start(f16[1,128,1024]{2,1,0:T(8,128)(2,1)S(1)} %get-tuple-element.20), channel_id=1, source_target_pairs={{16,47},{17,34},{18,33},{19,36},{20,35},{21,38},{22,37},{23,40},{2... | collective-permute-start | bytes 786440 | tf_op jit(solution)/shard_map/ppermute | solution.py:35
  5.5 26.9 %collective-permute-start.5 = (f16[1,128,1024]{2,1,0:T(8,128)(2,1)S(1)}, f16[1,128,1024]{2,1,0:T(8,128)(2,1)S(1)}, u32[]{:S(2)}, u32[]{:S(2)}) collective-permute-start(f16[1,128,1024]{2,1,0:T(8,128)(2,1)S(1)} %get-tuple-element.20), channel_id=1, source_target_pairs={{0,31},{1,18},{2,17},{3,20},{4,19},{5,22},{6,21},{7,24},{8,23},{9,... | collective-permute-start | bytes 786440 | tf_op jit(solution)/shard_map/ppermute | solution.py:35
  5.6 27.6 %collective-permute-start.4 = (f16[1,128,1024]{2,1,0:T(8,128)(2,1)S(1)}, f16[1,128,1024]{2,1,0:T(8,128)(2,1)S(1)}, u32[]{:S(2)}, u32[]{:S(2)}) collective-permute-start(f16[1,128,1024]{2,1,0:T(8,128)(2,1)S(1)} %get-tuple-element.20), channel_id=1, source_target_pairs={{0,15},{1,2},{2,1},{3,4},{4,3},{5,6},{6,5},{7,8},{8,7},{9,10},{10,... | collective-permute-start | bytes 786440 | tf_op jit(solution)/shard_map/ppermute | solution.py:35
  6.2 15.0 %collective-permute-start.1 = (f16[1,128,1024]{2,1,0:T(8,128)(2,1)S(1)}, f16[1,128,1024]{2,1,0:T(8,128)(2,1)S(1)}, u32[]{:S(2)}, u32[]{:S(2)}) collective-permute-start(f16[1,128,1024]{2,1,0:T(8,128)(2,1)S(1)} %get-tuple-element.18), channel_id=1, source_target_pairs={{0,16},{1,17},{2,18},{3,19},{4,20},{5,21},{6,22},{7,23},{8,24},{9,... | collective-permute-start | bytes 786440 | tf_op jit(solution)/shard_map/ppermute | solution.py:35
  8.6 18.0 %collective-permute-start = (f16[1,128,1024]{2,1,0:T(8,128)(2,1)S(1)}, f16[1,128,1024]{2,1,0:T(8,128)(2,1)S(1)}, u32[]{:S(2)}, u32[]{:S(2)}) collective-permute-start(f16[1,128,1024]{2,1,0:T(8,128)(2,1)S(1)} %get-tuple-element.19), channel_id=1, source_target_pairs={{0,16},{1,17},{2,18},{3,19},{4,20},{5,21},{6,22},{7,23},{8,24},{9,... | collective-permute-start | bytes 786440 | tf_op jit(solution)/shard_map/ppermute | solution.py:35
  26.8 20.1 %collective-permute-start.7 = (f16[2,128,1024]{2,1,0:T(8,128)(2,1)S(1)}, f16[2,128,1024]{2,1,0:T(8,128)(2,1)S(1)}, u32[]{:S(2)}, u32[]{:S(2)}) collective-permute-start(f16[2,128,1024]{2,1,0:T(8,128)(2,1)S(1)} %pad_maximum_fusion.3), channel_id=1, source_target_pairs={{0,1},{1,0},{2,3},{3,2},{4,5},{5,4},{6,7},{7,6},{8,9},{9,8},{10,11... | collective-permute-start | bytes 1572872 | tf_op jit(solution)/shard_map/ppermute | solution.py:35
  27.2 10.6 %collective-permute-start.3 = (f16[1,128,1024]{2,1,0:T(8,128)(2,1)S(1)}, f16[1,128,1024]{2,1,0:T(8,128)(2,1)S(1)}, u32[]{:S(2)}, u32[]{:S(2)}) collective-permute-start(f16[1,128,1024]{2,1,0:T(8,128)(2,1)S(1)} %collective-permute-done.1), channel_id=1, source_target_pairs={{0,32},{1,33},{2,34},{3,35},{4,36},{5,37},{6,38},{7,39},{8,40},{9,... | collective-permute-start | bytes 786440 | tf_op jit(solution)/shard_map/ppermute | solution.py:35
  30.3 13.2 %collective-permute-start.2 = (f16[1,128,1024]{2,1,0:T(8,128)(2,1)S(1)}, f16[1,128,1024]{2,1,0:T(8,128)(2,1)S(1)}, u32[]{:S(2)}, u32[]{:S(2)}) collective-permute-start(f16[1,128,1024]{2,1,0:T(8,128)(2,1)S(1)} %collective-permute-done), channel_id=1, source_target_pairs={{0,32},{1,33},{2,34},{3,35},{4,36},{5,37},{6,38},{7,39},{8,40},{9,... | collective-permute-start | bytes 786440 | tf_op jit(solution)/shard_map/ppermute | solution.py:35
  43.6 2.4 %collective-permute-start.8 = (f16[1,128,1024]{2,1,0:T(8,128)(2,1)S(1)}, f16[1,128,1024]{2,1,0:T(8,128)(2,1)S(1)}, u32[]{:S(2)}, u32[]{:S(2)}) collective-permute-start(f16[1,128,1024]{2,1,0:T(8,128)(2,1)S(1)} %broadcast_select_fusion.4), channel_id=1, source_target_pairs={{0,1},{1,0},{2,3},{3,2},{4,5},{5,4},{6,7},{7,6},{8,9},{9,8},{10,11... | collective-permute-start | bytes 786440 | tf_op jit(solution)/shard_map/ppermute | solution.py:35
  56.7 44.5 %slice-start = ((s8[6291456]{0:T(1024)(128)(4,1)}), s8[4194304]{0:T(1024)(128)(4,1)S(1)}, s32[]{:S(2)}) async-start(s8[6291456]{0:T(1024)(128)(4,1)} %bitcast.38), calls=%async_computation | async-start | bytes 8388608
  57.9 54.0 %collective-permute-start.15 = (bf16[1,128,1024]{2,1,0:T(8,128)(2,1)S(1)}, bf16[1,128,1024]{2,1,0:T(8,128)(2,1)S(1)}, u32[]{:S(2)}, u32[]{:S(2)}) collective-permute-start(bf16[1,128,1024]{2,1,0:T(8,128)(2,1)S(1)} %get-tuple-element.14), channel_id=1, source_target_pairs={{16,47},{17,34},{18,33},{19,36},{20,35},{21,38},{22,37},{23,40},{2... | collective-permute-start | bytes 786440 | tf_op jit(solution)/shard_map/ppermute | solution.py:35
  61.6 50.3 %collective-permute-start.14 = (bf16[1,128,1024]{2,1,0:T(8,128)(2,1)S(1)}, bf16[1,128,1024]{2,1,0:T(8,128)(2,1)S(1)}, u32[]{:S(2)}, u32[]{:S(2)}) collective-permute-start(bf16[1,128,1024]{2,1,0:T(8,128)(2,1)S(1)} %get-tuple-element.14), channel_id=1, source_target_pairs={{0,31},{1,18},{2,17},{3,20},{4,19},{5,22},{6,21},{7,24},{8,23},{9,... | collective-permute-start | bytes 786440 | tf_op jit(solution)/shard_map/ppermute | solution.py:35
  61.7 50.2 %collective-permute-start.13 = (bf16[1,128,1024]{2,1,0:T(8,128)(2,1)S(1)}, bf16[1,128,1024]{2,1,0:T(8,128)(2,1)S(1)}, u32[]{:S(2)}, u32[]{:S(2)}) collective-permute-start(bf16[1,128,1024]{2,1,0:T(8,128)(2,1)S(1)} %get-tuple-element.14), channel_id=1, source_target_pairs={{0,15},{1,2},{2,1},{3,4},{4,3},{5,6},{6,5},{7,8},{8,7},{9,10},{10,... | collective-permute-start | bytes 786440 | tf_op jit(solution)/shard_map/ppermute | solution.py:35
  64.5 26.6 %collective-permute-start.9 = (bf16[2,128,1024]{2,1,0:T(8,128)(2,1)S(1)}, bf16[2,128,1024]{2,1,0:T(8,128)(2,1)S(1)}, u32[]{:S(2)}, u32[]{:S(2)}) collective-permute-start(bf16[2,128,1024]{2,1,0:T(8,128)(2,1)S(1)} %slice.52), channel_id=1, source_target_pairs={{0,16},{1,17},{2,18},{3,19},{4,20},{5,21},{6,22},{7,23},{8,24},{9,... | collective-permute-start | bytes 1572872 | tf_op jit(solution)/shard_map/ppermute | solution.py:35
  66.2 23.6 %collective-permute-start.10 = (bf16[1,128,1024]{2,1,0:T(8,128)(2,1)S(1)}, bf16[1,128,1024]{2,1,0:T(8,128)(2,1)S(1)}, u32[]{:S(2)}, u32[]{:S(2)}) collective-permute-start(bf16[1,128,1024]{2,1,0:T(8,128)(2,1)S(1)} %get-tuple-element.15), channel_id=1, source_target_pairs={{0,16},{1,17},{2,18},{3,19},{4,20},{5,21},{6,22},{7,23},{8,24},{9,... | collective-permute-start | bytes 786440 | tf_op jit(solution)/shard_map/ppermute | solution.py:35
  67.4 33.8 %slice-start.1 = ((s8[6291456]{0:T(1024)(128)(4,1)}), s8[2097152]{0:T(1024)(128)(4,1)S(1)}, s32[]{:S(2)}) async-start(s8[6291456]{0:T(1024)(128)(4,1)} %bitcast.38), calls=%async_computation.1 | async-start | bytes 4194304
  89.8 9.4 %collective-permute-start.12 = (bf16[1,128,1024]{2,1,0:T(8,128)(2,1)S(1)}, bf16[1,128,1024]{2,1,0:T(8,128)(2,1)S(1)}, u32[]{:S(2)}, u32[]{:S(2)}) collective-permute-start(bf16[1,128,1024]{2,1,0:T(8,128)(2,1)S(1)} %collective-permute-done.10), channel_id=1, source_target_pairs={{0,32},{1,33},{2,34},{3,35},{4,36},{5,37},{6,38},{7,39},{8,40},{9,... | collective-permute-start | bytes 786440 | tf_op jit(solution)/shard_map/ppermute | solution.py:35
  91.1 19.3 %collective-permute-start.11 = (bf16[2,128,1024]{2,1,0:T(8,128)(2,1)S(1)}, bf16[2,128,1024]{2,1,0:T(8,128)(2,1)S(1)}, u32[]{:S(2)}, u32[]{:S(2)}) collective-permute-start(bf16[2,128,1024]{2,1,0:T(8,128)(2,1)S(1)} %collective-permute-done.9), channel_id=1, source_target_pairs={{0,32},{1,33},{2,34},{3,35},{4,36},{5,37},{6,38},{7,39},{8,40},{9,... | collective-permute-start | bytes 1572872 | tf_op jit(solution)/shard_map/ppermute | solution.py:35
  99.1 12.8 %collective-permute-start.16 = (bf16[2,128,1024]{2,1,0:T(8,128)(2,1)S(1)}, bf16[2,128,1024]{2,1,0:T(8,128)(2,1)S(1)}, u32[]{:S(2)}, u32[]{:S(2)}) collective-permute-start(bf16[2,128,1024]{2,1,0:T(8,128)(2,1)S(1)} %pad_maximum_fusion.4), channel_id=1, source_target_pairs={{0,1},{1,0},{2,3},{3,2},{4,5},{5,4},{6,7},{7,6},{8,9},{9,8},{10,11... | collective-permute-start | bytes 1572872 | tf_op jit(solution)/shard_map/ppermute | solution.py:35
  110.4 9.0 %collective-permute-start.17 = (bf16[1,128,1024]{2,1,0:T(8,128)(2,1)S(1)}, bf16[1,128,1024]{2,1,0:T(8,128)(2,1)S(1)}, u32[]{:S(2)}, u32[]{:S(2)}) collective-permute-start(bf16[1,128,1024]{2,1,0:T(8,128)(2,1)S(1)} %slice_select_fusion.2), channel_id=1, source_target_pairs={{0,1},{1,0},{2,3},{3,2},{4,5},{5,4},{6,7},{7,6},{8,9},{9,8},{10,11... | collective-permute-start | bytes 786440 | tf_op jit(solution)/shard_map/ppermute | solution.py:35
  120.9 38.0 %copy-start.7 = (s32[1,2,4]{2,1,0:T(2,128)S(1)}, s32[1,2,4]{2,1,0:T(2,128)}, u32[]{:S(2)}) copy-start(s32[1,2,4]{2,1,0:T(2,128)} %param.22) | copy-start | bytes 100
  142.6 15.0 %collective-permute-start.18 = (bf16[2,128,1024]{2,1,0:T(8,128)(2,1)S(1)}, bf16[2,128,1024]{2,1,0:T(8,128)(2,1)S(1)}, u32[]{:S(2)}, u32[]{:S(2)}) collective-permute-start(bf16[2,128,1024]{2,1,0:T(8,128)(2,1)S(1)} %slice.70), channel_id=1, source_target_pairs={{0,16},{1,17},{2,18},{3,19},{4,20},{5,21},{6,22},{7,23},{8,24},{9,... | collective-permute-start | bytes 1572872 | tf_op jit(solution)/shard_map/ppermute | solution.py:35
  144.6 22.3 %collective-permute-start.19 = (bf16[1,128,1024]{2,1,0:T(8,128)(2,1)S(1)}, bf16[1,128,1024]{2,1,0:T(8,128)(2,1)S(1)}, u32[]{:S(2)}, u32[]{:S(2)}) collective-permute-start(bf16[1,128,1024]{2,1,0:T(8,128)(2,1)S(1)} %get-tuple-element.12), channel_id=1, source_target_pairs={{0,16},{1,17},{2,18},{3,19},{4,20},{5,21},{6,22},{7,23},{8,24},{9,... | collective-permute-start | bytes 786440 | tf_op jit(solution)/shard_map/ppermute | solution.py:35
  157.6 30.1 %copy-start = (bf16[2,128,1024]{2,1,0:T(8,128)(2,1)}, bf16[2,128,1024]{2,1,0:T(8,128)(2,1)S(1)}, u32[]{:S(2)}) copy-start(bf16[2,128,1024]{2,1,0:T(8,128)(2,1)S(1)} %collective-permute-done.18.refs_2_) | copy-start | bytes 1572868
  157.6 27.5 %collective-permute-start.20 = (bf16[2,128,1024]{2,1,0:T(8,128)(2,1)S(1)}, bf16[2,128,1024]{2,1,0:T(8,128)(2,1)S(1)}, u32[]{:S(2)}, u32[]{:S(2)}) collective-permute-start(bf16[2,128,1024]{2,1,0:T(8,128)(2,1)S(1)} %collective-permute-done.18.refs_2_), channel_id=1, source_target_pairs={{0,32},{1,33},{2,34},{3,35},{4,36},{5,37},{6,38},{7,39},{8,40},{9,... | collective-permute-start | bytes 1572872 | tf_op jit(solution)/shard_map/ppermute | solution.py:35
  158.9 27.9 %collective-permute-start.24 = (bf16[1,128,1024]{2,1,0:T(8,128)(2,1)S(1)}, bf16[1,128,1024]{2,1,0:T(8,128)(2,1)S(1)}, u32[]{:S(2)}, u32[]{:S(2)}) collective-permute-start(bf16[1,128,1024]{2,1,0:T(8,128)(2,1)S(1)} %get-tuple-element.13), channel_id=1, source_target_pairs={{16,47},{17,34},{18,33},{19,36},{20,35},{21,38},{22,37},{23,40},{2... | collective-permute-start | bytes 786440 | tf_op jit(solution)/shard_map/ppermute | solution.py:35
  166.7 20.0 %collective-permute-start.23 = (bf16[1,128,1024]{2,1,0:T(8,128)(2,1)S(1)}, bf16[1,128,1024]{2,1,0:T(8,128)(2,1)S(1)}, u32[]{:S(2)}, u32[]{:S(2)}) collective-permute-start(bf16[1,128,1024]{2,1,0:T(8,128)(2,1)S(1)} %get-tuple-element.13), channel_id=1, source_target_pairs={{0,31},{1,18},{2,17},{3,20},{4,19},{5,22},{6,21},{7,24},{8,23},{9,... | collective-permute-start | bytes 786440 | tf_op jit(solution)/shard_map/ppermute | solution.py:35
  166.8 20.0 %collective-permute-start.22 = (bf16[1,128,1024]{2,1,0:T(8,128)(2,1)S(1)}, bf16[1,128,1024]{2,1,0:T(8,128)(2,1)}, u32[]{:S(2)}, u32[]{:S(2)}) collective-permute-start(bf16[1,128,1024]{2,1,0:T(8,128)(2,1)S(1)} %get-tuple-element.13), channel_id=1, source_target_pairs={{0,15},{1,2},{2,1},{3,4},{4,3},{5,6},{6,5},{7,8},{8,7},{9,10},{10,... | collective-permute-start | bytes 786440 | tf_op jit(solution)/shard_map/ppermute | solution.py:35
  166.9 20.8 %copy-start.2 = (bf16[1,128,1024]{2,1,0:T(8,128)(2,1)}, bf16[1,128,1024]{2,1,0:T(8,128)(2,1)S(1)}, u32[]{:S(2)}) copy-start(bf16[1,128,1024]{2,1,0:T(8,128)(2,1)S(1)} %collective-permute-done.19.refs_3_) | copy-start | bytes 786436
  167.0 15.9 %collective-permute-start.21 = (bf16[1,128,1024]{2,1,0:T(8,128)(2,1)S(1)}, bf16[1,128,1024]{2,1,0:T(8,128)(2,1)S(1)}, u32[]{:S(2)}, u32[]{:S(2)}) collective-permute-start(bf16[1,128,1024]{2,1,0:T(8,128)(2,1)S(1)} %collective-permute-done.19.refs_3_), channel_id=1, source_target_pairs={{0,32},{1,33},{2,34},{3,35},{4,36},{5,37},{6,38},{7,39},{8,40},{9,... | collective-permute-start | bytes 786440 | tf_op jit(solution)/shard_map/ppermute | solution.py:35
  182.8 4.9 %copy-start.3 = (bf16[1,128,1024]{2,1,0:T(8,128)(2,1)}, bf16[1,128,1024]{2,1,0:T(8,128)(2,1)S(1)}, u32[]{:S(2)}) copy-start(bf16[1,128,1024]{2,1,0:T(8,128)(2,1)S(1)} %collective-permute-done.21.refs_5_) | copy-start | bytes 786436
  182.8 4.0 %collective-permute-start.25 = (bf16[2,128,1024]{2,1,0:T(8,128)(2,1)S(1)}, bf16[2,128,1024]{2,1,0:T(8,128)(2,1)S(1)}, u32[]{:S(2)}, u32[]{:S(2)}) collective-permute-start(bf16[2,128,1024]{2,1,0:T(8,128)(2,1)S(1)} %pad_maximum_fusion.5), channel_id=1, source_target_pairs={{0,1},{1,0},{2,3},{3,2},{4,5},{5,4},{6,7},{7,6},{8,9},{9,8},{10,11... | collective-permute-start | bytes 1572872 | tf_op jit(solution)/shard_map/ppermute | solution.py:35
  185.1 2.7 %copy-start.1 = (bf16[2,128,1024]{2,1,0:T(8,128)(2,1)}, bf16[2,128,1024]{2,1,0:T(8,128)(2,1)S(1)}, u32[]{:S(2)}) copy-start(bf16[2,128,1024]{2,1,0:T(8,128)(2,1)S(1)} %collective-permute-done.20.refs_4_) | copy-start | bytes 1572868
  185.9 1.9 collective-permute-start.26
  186.8 1.0 copy-start.5
  186.8 1.0 copy-start.6
  186.8 1.0 copy-start.4
where the time goes:
time: 196 us; the launch traced here: 194 us
  waiting for transfers between devices  76.3 us (39%)
  starting transfers between devices  43 us (22%)
  Pallas kernels  33.8 us (17%)
  matrix products  17.5 us (9%)
  other arithmetic  17.3 us (9%)
  local copies, waits for them, and re-layouts  5.01 us (3%)
    ppermute x27, waiting for transfers between devices, move(): return lax.ppermute(values, AXES, pairs)  76.3 us
    ppermute x27, starting transfers between devices, move(): return lax.ppermute(values, AXES, pairs)  43 us
    pallas_call x1, Pallas kernels, shards(): pl.pallas_call(lambda *refs: layer_kernel(*refs, piece_count=len(kv_piece...  20.6 us
    dot_general x4, matrix products, project(): jnp.dot(stacked.reshape(-1, width), kv_weight, preferred_element_type=f32)  11.7 us
    mul x9, other arithmetic, shards(): piece.astype(f32) * (1.0 / GRID_SCALE)  8.01 us
    pallas_call x1, Pallas kernels, shards(): pl.pallas_call(lambda *refs: lift_kernel(*refs, piece_count=len(grid_piec...  7.68 us
    dot_general x1, matrix products, shards(): jnp.dot(normed.reshape(-1, width), qkv_weight, preferred_element_type=f32)  5.77 us
    pallas_call x1, Pallas kernels, shards(): pl.pallas_call(lambda *refs: return_kernel(*refs, piece_count=len(mesh_pi...  5.6 us
  transfers between devices with their start and end apart: 27, of which 10 were waited for; matrix products, arithmetic and copies ran while one was open for 17% of the time, Pallas kernels for 0%

commit v1 on v0

--- a/solution.py
+++ b/solution.py
@@ -43,14 +43,10 @@
     return index ^ 1
 
 
-def exchange(blocks, even_sector):
-    last = blocks.shape[0] - 1
-    parts = (blocks[:last], blocks[last:])
-
+def exchange(parts, edge_out, even_sector):
     def inner_edge(halves):
         return jnp.where(even_sector, halves[1], halves[0][:1])
 
-    edge_out = jnp.where(even_sector, parts[0][:1], parts[1])
     near = [move(part, pair, same) for part in parts]
     outer = [
         move(edge_out, same, outer_sector), move(edge_out, pair, outer_sector), move(edge_out, far_band, outer_sector)
@@ -118,9 +114,20 @@
     return total
 
 
-def lift_kernel(slots, *refs, piece_count):
+def store_part(place, count, even, value, head, tail, edge):
+    if place < count - 1:
+        head[place] = value
+    else:
+        tail[0] = value
+    if place in (0, count - 1):
+        @pl.when(even == (1 if place == 0 else 0))
+        def _():
+            edge[0] = value
+
+
+def lift_kernel(slots, even, *refs, piece_count):
     pieces = refs[:piece_count]
-    weight, gains, mesh_in, normed, table, upper, lower, split, sems = refs[piece_count:]
+    weight, gains, mesh_in, normed, head, tail, edge, table, upper, lower, split, sems = refs[piece_count:]
     copies = fill_table(pieces, table, sems)
     for copy in copies:
         copy.start()
@@ -129,7 +136,9 @@
     for m in range(weight.shape[0]):
         mixed = mix_blocks(slots, m, weight.at[m], table, upper, lower, split)
         mesh_in[m] = mixed
-        normed[m] = normalise(mixed, gains[0:1, :])
+        result = normalise(mixed, gains[0:1, :])
+        normed[m] = result
+        store_part(m, weight.shape[0], even[0], result, head, tail, edge)
 
 
 def return_kernel(slots, *refs, piece_count):
@@ -144,10 +153,10 @@
         out[g] = mix_blocks(slots, g, weight.at[g], table, upper, None, split)
 
 
-def layer_kernel(slots, counts, *refs, piece_count):
+def layer_kernel(slots, counts, even, *refs, piece_count):
     pieces = refs[:piece_count]
     (
-        queries, mesh_in, gains, out_hbm, up_hbm, down_hbm, mesh_out,
+        queries, mesh_in, gains, out_hbm, up_hbm, down_hbm, head, tail, edge,
         table, keys, values, mixed, out_weight, up_weight, down_weight, sems,
     ) = refs[piece_count:]
     copies = fill_table(pieces, table, sems)
@@ -212,7 +221,15 @@
     hidden = jnp.dot(again, up_weight[...], preferred_element_type=jnp.float32)
     hidden = (0.5 * hidden * (1.0 + lax.erf(hidden * 0.7071067811865476))).astype(jnp.bfloat16)
     result = after + jnp.dot(hidden, down_weight[...], preferred_element_type=jnp.float32)
-    mesh_out[...] = result.astype(jnp.bfloat16).reshape(mesh_blocks, rows, width)
+    result = result.astype(jnp.bfloat16).reshape(mesh_blocks, rows, width)
+    for m in range(mesh_blocks):
+        store_part(m, mesh_blocks, even[0], result[m], head, tail, edge)
+
+
+def part_shapes(count, rows, width):
+    return [
+        jax.ShapeDtypeStruct((size, rows, width), jnp.bfloat16) for size in (count - 1, 1, 1)
+    ]
 
 
 def any_specs(count):
@@ -239,18 +256,20 @@
 
     own_grid = grid_feats[0]
     sent = (own_grid * GRID_SCALE).astype(jnp.float16)
-    near, far, outer, inner = exchange(sent, even_sector)
+    sent_edge = (jnp.where(even_sector, own_grid[:1], own_grid[-1:]) * GRID_SCALE).astype(jnp.float16)
+    even = even_sector.astype(jnp.int32).reshape(1)
+    near, far, outer, inner = exchange((sent[:-1], sent[-1:]), sent_edge, even_sector)
     grid_pieces = [own_grid] + [
         piece.astype(f32) * (1.0 / GRID_SCALE) for piece in near + far + outer + inner
     ]
     lift_slots = table_slots(lift_index[0], grid_lon, grid_blocks).reshape(-1)
     picks = lift_weight.shape[2]
-    mesh_in, normed = pl.pallas_call(
+    mesh_in, normed, head, tail, edge = pl.pallas_call(
         lambda *refs: lift_kernel(*refs, piece_count=len(grid_pieces)),
         grid_spec=pltpu.PrefetchScalarGridSpec(
-            num_scalar_prefetch=1,
+            num_scalar_prefetch=2,
             in_specs=any_specs(len(grid_pieces)) + [VMEM_SPEC, VMEM_SPEC],
-            out_specs=[VMEM_SPEC, VMEM_SPEC],
+            out_specs=[VMEM_SPEC] * 5,
             scratch_shapes=[
                 pltpu.VMEM((grid_table, rows, width), f32),
                 pltpu.VMEM((picks * rows, width), bf16),
@@ -262,11 +281,11 @@
         out_shape=[
             jax.ShapeDtypeStruct((mesh_blocks, rows, width), f32),
             jax.ShapeDtypeStruct((mesh_blocks, rows, width), bf16),
-        ],
+        ] + part_shapes(mesh_blocks, rows, width),
         name="lift",
-    )(lift_slots, *grid_pieces, lift_weight[0], norm_gains)
-
-    near, far, outer, inner = exchange(normed, even_sector)
+    )(lift_slots, even, *grid_pieces, lift_weight[0], norm_gains)
+
+    near, far, outer, inner = exchange((head, tail), edge, even_sector)
     own = jnp.dot(normed.reshape(-1, width), qkv_weight, preferred_element_type=f32).astype(bf16)
     queries = own[:, :width].reshape(mesh_blocks, rows, width)
     kv_weight = qkv_weight[:, width:]
@@ -288,12 +307,12 @@
     window_slots = table_slots(window_index[0], mesh_lon, mesh_blocks).reshape(-1)
     neighbours = window_index.shape[2]
     hidden_width = up_weight.shape[1]
-    mesh_out = pl.pallas_call(
+    head, tail, edge = pl.pallas_call(
         lambda *refs: layer_kernel(*refs, piece_count=len(kv_pieces)),
         grid_spec=pltpu.PrefetchScalarGridSpec(
-            num_scalar_prefetch=2,
+            num_scalar_prefetch=3,
             in_specs=any_specs(len(kv_pieces)) + [VMEM_SPEC] * 3 + any_specs(3),
-            out_specs=VMEM_SPEC,
+            out_specs=[VMEM_SPEC] * 3,
             scratch_shapes=[
                 pltpu.VMEM((mesh_table, rows, 2 * width), bf16),
                 pltpu.VMEM((neighbours * rows, width), bf16),
@@ -305,15 +324,15 @@
                 pltpu.SemaphoreType.DMA((len(kv_pieces) + 3,)),
             ],
         ),
-        out_shape=jax.ShapeDtypeStruct((mesh_blocks, rows, width), bf16),
+        out_shape=part_shapes(mesh_blocks, rows, width),
         name="layer",
     )(
-        window_slots, window_count[0], *kv_pieces, queries, mesh_in, norm_gains,
+        window_slots, window_count[0], even, *kv_pieces, queries, mesh_in, norm_gains,
         out_weight, up_weight, down_weight,
     )
 
-    near, far, outer, inner = exchange(mesh_out, even_sector)
-    mesh_pieces = [mesh_out] + near + far + outer + inner
+    near, far, outer, inner = exchange((head, tail), edge, even_sector)
+    mesh_pieces = [head, tail] + near + far + outer + inner
     return_slots = table_slots(return_index[0], mesh_lon, mesh_blocks).reshape(-1)
     grid_out = pl.pallas_call(
         lambda *refs: return_kernel(*refs, piece_count=len(mesh_pieces)),

time: 196 us -> 191 us (0.974)
  the two profiles are of different devices: /device:TPU:21 before, /device:TPU:41 now
where the time goes in v1:
time: 191 us
  waiting for transfers between devices  62 us (32%)
  starting transfers between devices  57.4 us (30%)
  Pallas kernels  35.3 us (18%)
  matrix products  17.4 us (9%)
  other arithmetic  15.1 us (8%)
  local copies, waits for them, and re-layouts  2.88 us (2%)
    ppermute x27, waiting for transfers between devices, move(): return lax.ppermute(values, AXES, pairs)  62 us
    ppermute x27, starting transfers between devices, move(): return lax.ppermute(values, AXES, pairs)  57.4 us
    pallas_call x1, Pallas kernels, shards(): pl.pallas_call(lambda *refs: layer_kernel(*refs, piece_count=len(kv_piece...  20.7 us
    dot_general x4, matrix products, project(): jnp.dot(stacked.reshape(-1, width), kv_weight, preferred_element_type=f32)  11.7 us
    pallas_call x1, Pallas kernels, shards(): pl.pallas_call(lambda *refs: lift_kernel(*refs, piece_count=len(grid_piec...  8.98 us
    mul x9, other arithmetic, shards(): piece.astype(f32) * (1.0 / GRID_SCALE)  7.92 us
    dot_general x1, matrix products, shards(): jnp.dot(normed.reshape(-1, width), qkv_weight, preferred_element_type=f32)  5.77 us
    pallas_call x1, Pallas kernels, shards(): pl.pallas_call(lambda *refs: return_kernel(*refs, piece_count=len(mesh_pi...  5.6 us
  transfers between devices with their start and end apart: 27, of which 10 were waited for; matrix products, arithmetic and copies ran while one was open for 16% of the time, Pallas kernels for 0%

profile of v1, /device:TPU:41, one launch (start us, length us, event | category | flops | bytes accessed | tf_op | source)
XLA Modules:
  0.0 190.7 jit_solution(16287262663400144146)
XLA Ops:
  0.0 1.3 fusion.11
  1.3 4.2 %collective-permute-start.6 = (f16[1,128,1024]{2,1,0:T(8,128)(2,1)S(1)}, f16[1,128,1024]{2,1,0:T(8,128)(2,1)S(1)}, u32[]{:S(2)}, u32[]{:S(2)}) collective-permute-start(f16[1,128,1024]{2,1,0:T(8,128)(2,1)S(1)} %fusion.11), channel_id=1, source_target_pairs={{16,47},{17,34},{18,33},{19,36},{20,35},{21,38},{22,37},{23,40},{2... | collective-permute-start | bytes 786440 | tf_op jit(solution)/shard_map/ppermute | solution.py:35
  5.6 1.7 collective-permute-start.5
  7.3 2.9 %collective-permute-start.4 = (f16[1,128,1024]{2,1,0:T(8,128)(2,1)S(1)}, f16[1,128,1024]{2,1,0:T(8,128)(2,1)S(1)}, u32[]{:S(2)}, u32[]{:S(2)}) collective-permute-start(f16[1,128,1024]{2,1,0:T(8,128)(2,1)S(1)} %fusion.11), channel_id=1, source_target_pairs={{0,15},{1,2},{2,1},{3,4},{4,3},{5,6},{6,5},{7,8},{8,7},{9,10},{10,... | collective-permute-start | bytes 786440 | tf_op jit(solution)/shard_map/ppermute | solution.py:35
  10.2 1.3 multiply_convert_fusion
  11.5 0.2 broadcast_select_fusion.2
  11.7 0.1 collective-permute-start.1
  11.8 3.0 %collective-permute-start = (f16[1,128,1024]{2,1,0:T(8,128)(2,1)S(1)}, f16[1,128,1024]{2,1,0:T(8,128)(2,1)S(1)}, u32[]{:S(2)}, u32[]{:S(2)}) collective-permute-start(f16[1,128,1024]{2,1,0:T(8,128)(2,1)S(1)} %get-tuple-element.25), channel_id=1, source_target_pairs={{0,16},{1,17},{2,18},{3,19},{4,20},{5,21},{6,22},{7,23},{8,24},{9,... | collective-permute-start | bytes 786440 | tf_op jit(solution)/shard_map/ppermute | solution.py:35
  14.9 0.5 and_select_fusion.1.refs_0_
  15.7 0.5 and_select_fusion.5.refs_0_
  16.2 8.2 %collective-permute-done.1 = f16[1,128,1024]{2,1,0:T(8,128)(2,1)S(1)} collective-permute-done((f16[1,128,1024]{2,1,0:T(8,128)(2,1)S(1)}, f16[1,128,1024]{2,1,0:T(8,128)(2,1)S(1)}, u32[]{:S(2)}, u32[]{:S(2)}) %collective-permute-start.1) | collective-permute-done | bytes 262176 | tf_op jit(solution)/shard_map/ppermute | solution.py:35
  24.4 3.8 %collective-permute-done = f16[1,128,1024]{2,1,0:T(8,128)(2,1)S(1)} collective-permute-done((f16[1,128,1024]{2,1,0:T(8,128)(2,1)S(1)}, f16[1,128,1024]{2,1,0:T(8,128)(2,1)S(1)}, u32[]{:S(2)}, u32[]{:S(2)}) %collective-permute-start) | collective-permute-done | bytes 262176 | tf_op jit(solution)/shard_map/ppermute | solution.py:35
  28.4 0.1 pad_maximum_fusion.3
  28.6 3.3 %collective-permute-start.3 = (f16[1,128,1024]{2,1,0:T(8,128)(2,1)S(1)}, f16[1,128,1024]{2,1,0:T(8,128)(2,1)S(1)}, u32[]{:S(2)}, u32[]{:S(2)}) collective-permute-start(f16[1,128,1024]{2,1,0:T(8,128)(2,1)S(1)} %collective-permute-done.1), channel_id=1, source_target_pairs={{0,32},{1,33},{2,34},{3,35},{4,36},{5,37},{6,38},{7,39},{8,40},{9,... | collective-permute-start | bytes 786440 | tf_op jit(solution)/shard_map/ppermute | solution.py:35
  31.9 0.8 convert_multiply_fusion.7.refs_4_
  32.7 0.9 convert_multiply_fusion.8.refs_3_
  33.6 2.8 %collective-permute-start.2 = (f16[1,128,1024]{2,1,0:T(8,128)(2,1)S(1)}, f16[1,128,1024]{2,1,0:T(8,128)(2,1)S(1)}, u32[]{:S(2)}, u32[]{:S(2)}) collective-permute-start(f16[1,128,1024]{2,1,0:T(8,128)(2,1)S(1)} %collective-permute-done), channel_id=1, source_target_pairs={{0,32},{1,33},{2,34},{3,35},{4,36},{5,37},{6,38},{7,39},{8,40},{9,... | collective-permute-start | bytes 786440 | tf_op jit(solution)/shard_map/ppermute | solution.py:35
  36.4 0.9 convert_multiply_fusion.2.refs_9_
  37.2 0.9 convert_multiply_fusion.3.refs_8_
  38.1 0.8 convert_multiply_fusion.4.refs_7_
  38.9 4.9 %collective-permute-done.2 = f16[1,128,1024]{2,1,0:T(8,128)(2,1)S(1)} collective-permute-done((f16[1,128,1024]{2,1,0:T(8,128)(2,1)S(1)}, f16[1,128,1024]{2,1,0:T(8,128)(2,1)S(1)}, u32[]{:S(2)}, u32[]{:S(2)}) %collective-permute-start.2) | collective-permute-done | bytes 262176 | tf_op jit(solution)/shard_map/ppermute | solution.py:35
  43.9 1.1 collective-permute-start.8
  45.0 0.9 convert_multiply_fusion.6.refs_5_
  45.9 0.9 convert_multiply_fusion.5.refs_6_
  46.7 0.8 convert_multiply_fusion.1.refs_11_
  47.6 1.1 convert_multiply_fusion.refs_10_
  48.6 9.0 %lift.1 = (f32[3,128,1024]{2,1,0:T(8,128)}, bf16[3,128,1024]{2,1,0:T(8,128)(2,1)}, bf16[2,128,1024]{2,1,0:T(8,128)(2,1)}, bf16[1,128,1024]{2,1,0:T(8,128)(2,1)}, bf16[1,128,1024]{2,1,0:T(8,128)(2,1)}) custom-call(s32[12]{0:T(128)} %and_select_fusion.1.refs_0_, s32[1]{0:T(128)} %bitcast.1.refs_1_.refs_2_, f32[2,128,1024]{2,1,0:T(8,128)} %bitcast.28, ...), custom_call_target="tpu_custom_call" | custom-call | tf_op jit(solution)/shard_map/lift/pallas_call | solution.py:267
  57.6 3.2 %collective-permute-start.15 = (bf16[1,128,1024]{2,1,0:T(8,128)(2,1)}, bf16[1,128,1024]{2,1,0:T(8,128)(2,1)S(1)}, u32[]{:S(2)}, u32[]{:S(2)}) collective-permute-start(bf16[1,128,1024]{2,1,0:T(8,128)(2,1)} %get-tuple-element.16), channel_id=1, source_target_pairs={{16,47},{17,34},{18,33},{19,36},{20,35},{21,38},{22,37},{23,40},{2... | collective-permute-start | bytes 786440 | tf_op jit(solution)/shard_map/ppermute | solution.py:35
  60.8 2.5 %collective-permute-start.14 = (bf16[1,128,1024]{2,1,0:T(8,128)(2,1)}, bf16[1,128,1024]{2,1,0:T(8,128)(2,1)S(1)}, u32[]{:S(2)}, u32[]{:S(2)}) collective-permute-start(bf16[1,128,1024]{2,1,0:T(8,128)(2,1)} %get-tuple-element.16), channel_id=1, source_target_pairs={{0,31},{1,18},{2,17},{3,20},{4,19},{5,22},{6,21},{7,24},{8,23},{9,... | collective-permute-start | bytes 786440 | tf_op jit(solution)/shard_map/ppermute | solution.py:35
  63.3 3.3 %collective-permute-start.13 = (bf16[1,128,1024]{2,1,0:T(8,128)(2,1)}, bf16[1,128,1024]{2,1,0:T(8,128)(2,1)S(1)}, u32[]{:S(2)}, u32[]{:S(2)}) collective-permute-start(bf16[1,128,1024]{2,1,0:T(8,128)(2,1)} %get-tuple-element.16), channel_id=1, source_target_pairs={{0,15},{1,2},{2,1},{3,4},{4,3},{5,6},{6,5},{7,8},{8,7},{9,10},{10,... | collective-permute-start | bytes 786440 | tf_op jit(solution)/shard_map/ppermute | solution.py:35
  66.6 3.0 %collective-permute-start.9 = (bf16[2,128,1024]{2,1,0:T(8,128)(2,1)}, bf16[2,128,1024]{2,1,0:T(8,128)(2,1)S(1)}, u32[]{:S(2)}, u32[]{:S(2)}) collective-permute-start(bf16[2,128,1024]{2,1,0:T(8,128)(2,1)} %get-tuple-element.14), channel_id=1, source_target_pairs={{0,16},{1,17},{2,18},{3,19},{4,20},{5,21},{6,22},{7,23},{8,24},{9,... | collective-permute-start | bytes 1572872 | tf_op jit(solution)/shard_map/ppermute | solution.py:35
  69.6 5.8 %convolution_convert_fusion = bf16[384,3072]{1,0:T(8,128)(2,1)S(1)} fusion(bf16[384,1024]{1,0:T(8,128)(2,1)} %bitcast.42, bf16[1024,3072]{1,0:T(8,128)(2,1)} %param.18), kind=kOutput, calls=%fused_computation | convolution fusion | flops 2417098752 | bytes 9437184 | tf_op jit(solution)/shard_map/dot_general | solution.py:289
  75.4 0.9 slice.59
  76.3 1.3 slice.56
  77.7 2.4 %collective-permute-done.10 = bf16[1,128,1024]{2,1,0:T(8,128)(2,1)S(1)} collective-permute-done((bf16[1,128,1024]{2,1,0:T(8,128)(2,1)}, bf16[1,128,1024]{2,1,0:T(8,128)(2,1)S(1)}, u32[]{:S(2)}, u32[]{:S(2)}) %collective-permute-start.10) | collective-permute-done | bytes 262176 | tf_op jit(solution)/shard_map/ppermute | solution.py:35
  80.1 2.3 %collective-permute-start.12 = (bf16[1,128,1024]{2,1,0:T(8,128)(2,1)S(1)}, bf16[1,128,1024]{2,1,0:T(8,128)(2,1)S(1)}, u32[]{:S(2)}, u32[]{:S(2)}) collective-permute-start(bf16[1,128,1024]{2,1,0:T(8,128)(2,1)S(1)} %collective-permute-done.10), channel_id=1, source_target_pairs={{0,32},{1,33},{2,34},{3,35},{4,36},{5,37},{6,38},{7,39},{8,40},{9,... | collective-permute-start | bytes 786440 | tf_op jit(solution)/shard_map/ppermute | solution.py:35
  82.4 7.7 %collective-permute-done.9 = bf16[2,128,1024]{2,1,0:T(8,128)(2,1)S(1)} collective-permute-done((bf16[2,128,1024]{2,1,0:T(8,128)(2,1)}, bf16[2,128,1024]{2,1,0:T(8,128)(2,1)S(1)}, u32[]{:S(2)}, u32[]{:S(2)}) %collective-permute-start.9) | collective-permute-done | bytes 524320 | tf_op jit(solution)/shard_map/ppermute | solution.py:35
  90.1 2.8 %collective-permute-start.11 = (bf16[2,128,1024]{2,1,0:T(8,128)(2,1)S(1)}, bf16[2,128,1024]{2,1,0:T(8,128)(2,1)S(1)}, u32[]{:S(2)}, u32[]{:S(2)}) collective-permute-start(bf16[2,128,1024]{2,1,0:T(8,128)(2,1)S(1)} %collective-permute-done.9), channel_id=1, source_target_pairs={{0,32},{1,33},{2,34},{3,35},{4,36},{5,37},{6,38},{7,39},{8,40},{9,... | collective-permute-start | bytes 1572872 | tf_op jit(solution)/shard_map/ppermute | solution.py:35
  93.1 0.5 collective-permute-start.16
  93.6 3.0 %convolution_convert_fusion.3 = bf16[384,2048]{1,0:T(8,128)(2,1)} fusion(bf16[384,1024]{1,0:T(8,128)(2,1)S(1)} %bitcast.36, bf16[1024,3072]{1,0:T(8,128)(2,1)S(1)} %bitcast.41), kind=kOutput, calls=%fused_computation.3 | convolution fusion | flops 1611399168 | bytes 6553600 | tf_op jit(solution)/shard_map/dot_general | solution.py:297
  96.6 9.2 %collective-permute-done.11 = bf16[2,128,1024]{2,1,0:T(8,128)(2,1)S(1)} collective-permute-done((bf16[2,128,1024]{2,1,0:T(8,128)(2,1)S(1)}, bf16[2,128,1024]{2,1,0:T(8,128)(2,1)S(1)}, u32[]{:S(2)}, u32[]{:S(2)}) %collective-permute-start.11) | collective-permute-done | bytes 524320 | tf_op jit(solution)/shard_map/ppermute | solution.py:35
  105.8 0.8 collective-permute-start.17
  106.7 0.2 pad_maximum_fusion
  106.8 4.2 %convolution_convert_fusion.1 = bf16[640,2048]{1,0:T(8,128)(2,1)} fusion(bf16[640,1024]{1,0:T(8,128)(2,1)S(1)} %bitcast.34, bf16[1024,3072]{1,0:T(8,128)(2,1)S(1)} %bitcast.41), kind=kOutput, calls=%fused_computation.1 | convolution fusion | flops 2685665280 | bytes 8126464 | tf_op jit(solution)/shard_map/dot_general | solution.py:297
  111.1 3.0 %convolution_convert_fusion.2 = bf16[384,2048]{1,0:T(8,128)(2,1)} fusion(bf16[384,1024]{1,0:T(8,128)(2,1)S(1)} %bitcast.37, bf16[1024,3072]{1,0:T(8,128)(2,1)S(1)} %bitcast.41), kind=kOutput, calls=%fused_computation.2 | convolution fusion | flops 1611399168 | bytes 6553600 | tf_op jit(solution)/shard_map/dot_general | solution.py:297
  114.1 1.5 fusion.8.refs_7_
  115.7 20.7 %layer.1 = (bf16[2,128,1024]{2,1,0:T(8,128)(2,1)}, bf16[1,128,1024]{2,1,0:T(8,128)(2,1)}, bf16[1,128,1024]{2,1,0:T(8,128)(2,1)}) custom-call(s32[24]{0:T(128)} %and_select_fusion.5.refs_0_, s32[3]{0:T(128)} %bitcast.39, s32[1]{0:T(128)} %bitcast.1.refs_1_.refs_2_, bf16[3,128,2048]{2,1,0:T(8,128)(2,1)} %bitcast.29, bf16[3,128,2048]{2,1,0:T(8,128)(2,1)} %bitcast.32, ...), custom_call_target="tpu_custom_call" | custom-call | tf_op jit(solution)/shard_map/layer/pallas_call | solution.py:310
  136.4 0.7 collective-permute-start.18
  137.1 2.3 %collective-permute-start.19 = (bf16[1,128,1024]{2,1,0:T(8,128)(2,1)}, bf16[1,128,1024]{2,1,0:T(8,128)(2,1)S(1)}, u32[]{:S(2)}, u32[]{:S(2)}) collective-permute-start(bf16[1,128,1024]{2,1,0:T(8,128)(2,1)} %get-tuple-element.19.refs_2_), channel_id=1, source_target_pairs={{0,16},{1,17},{2,18},{3,19},{4,20},{5,21},{6,22},{7,23},{8,24},{9,... | collective-permute-start | bytes 786440 | tf_op jit(solution)/shard_map/ppermute | solution.py:35
  139.4 2.9 %collective-permute-start.24 = (bf16[1,128,1024]{2,1,0:T(8,128)(2,1)}, bf16[1,128,1024]{2,1,0:T(8,128)(2,1)S(1)}, u32[]{:S(2)}, u32[]{:S(2)}) collective-permute-start(bf16[1,128,1024]{2,1,0:T(8,128)(2,1)} %get-tuple-element.20), channel_id=1, source_target_pairs={{16,47},{17,34},{18,33},{19,36},{20,35},{21,38},{22,37},{23,40},{2... | collective-permute-start | bytes 786440 | tf_op jit(solution)/shard_map/ppermute | solution.py:35
  142.4 2.3 %collective-permute-start.23 = (bf16[1,128,1024]{2,1,0:T(8,128)(2,1)}, bf16[1,128,1024]{2,1,0:T(8,128)(2,1)S(1)}, u32[]{:S(2)}, u32[]{:S(2)}) collective-permute-start(bf16[1,128,1024]{2,1,0:T(8,128)(2,1)} %get-tuple-element.20), channel_id=1, source_target_pairs={{0,31},{1,18},{2,17},{3,20},{4,19},{5,22},{6,21},{7,24},{8,23},{9,... | collective-permute-start | bytes 786440 | tf_op jit(solution)/shard_map/ppermute | solution.py:35
  144.7 3.1 %collective-permute-start.22 = (bf16[1,128,1024]{2,1,0:T(8,128)(2,1)}, bf16[1,128,1024]{2,1,0:T(8,128)(2,1)S(1)}, u32[]{:S(2)}, u32[]{:S(2)}) collective-permute-start(bf16[1,128,1024]{2,1,0:T(8,128)(2,1)} %get-tuple-element.20), channel_id=1, source_target_pairs={{0,15},{1,2},{2,1},{3,4},{4,3},{5,6},{6,5},{7,8},{8,7},{9,10},{10,... | collective-permute-start | bytes 786440 | tf_op jit(solution)/shard_map/ppermute | solution.py:35
  147.8 10.7 %collective-permute-done.18.refs_3_ = bf16[2,128,1024]{2,1,0:T(8,128)(2,1)S(1)} collective-permute-done((bf16[2,128,1024]{2,1,0:T(8,128)(2,1)}, bf16[2,128,1024]{2,1,0:T(8,128)(2,1)S(1)}, u32[]{:S(2)}, u32[]{:S(2)}) %collective-permute-start.18) | collective-permute-done | bytes 524320 | tf_op jit(solution)/shard_map/ppermute | solution.py:35
  158.5 3.9 %collective-permute-start.20 = (bf16[2,128,1024]{2,1,0:T(8,128)(2,1)S(1)}, bf16[2,128,1024]{2,1,0:T(8,128)(2,1)S(1)}, u32[]{:S(2)}, u32[]{:S(2)}) collective-permute-start(bf16[2,128,1024]{2,1,0:T(8,128)(2,1)S(1)} %collective-permute-done.18.refs_3_), channel_id=1, source_target_pairs={{0,32},{1,33},{2,34},{3,35},{4,36},{5,37},{6,38},{7,39},{8,40},{9,... | collective-permute-start | bytes 1572872 | tf_op jit(solution)/shard_map/ppermute | solution.py:35
  162.4 1.0 slice_select_fusion.4
  163.4 0.8 collective-permute-done.19.refs_4_
  164.2 3.9 %collective-permute-start.21 = (bf16[1,128,1024]{2,1,0:T(8,128)(2,1)S(1)}, bf16[1,128,1024]{2,1,0:T(8,128)(2,1)S(1)}, u32[]{:S(2)}, u32[]{:S(2)}) collective-permute-start(bf16[1,128,1024]{2,1,0:T(8,128)(2,1)S(1)} %collective-permute-done.19.refs_4_), channel_id=1, source_target_pairs={{0,32},{1,33},{2,34},{3,35},{4,36},{5,37},{6,38},{7,39},{8,40},{9,... | collective-permute-start | bytes 786440 | tf_op jit(solution)/shard_map/ppermute | solution.py:35
  168.1 13.3 %collective-permute-done.21.refs_6_ = bf16[1,128,1024]{2,1,0:T(8,128)(2,1)S(1)} collective-permute-done((bf16[1,128,1024]{2,1,0:T(8,128)(2,1)S(1)}, bf16[1,128,1024]{2,1,0:T(8,128)(2,1)S(1)}, u32[]{:S(2)}, u32[]{:S(2)}) %collective-permute-start.21) | collective-permute-done | bytes 262176 | tf_op jit(solution)/shard_map/ppermute | solution.py:35
  181.4 0.7 collective-permute-start.25
  182.1 0.8 slice_select_fusion
  183.0 0.1 ne.110
  183.2 0.6 and_select_fusion.9.refs_0_
  183.9 0.9 collective-permute-done.26.refs_11_
  184.9 5.6 %give_back.1 = f32[2,128,1024]{2,1,0:T(8,128)} custom-call(s32[8]{0:T(128)} %and_select_fusion.9.refs_0_, bf16[2,128,1024]{2,1,0:T(8,128)(2,1)} %get-tuple-element.18.refs_1_, bf16[1,128,1024]{2,1,0:T(8,128)(2,1)} %get-tuple-element.19.refs_2_, bf16[2,128,1024]{2,1,0:T(8,128)(2,1)} %copy-done, bf16[1,128,1024]{2,1,0:T(8,128)(2,1)} %copy-done.2, ...), custom_call_target="tpu_custom_call" | custom-call | tf_op jit(solution)/shard_map/give_back/pallas_call | solution.py:337
  (72 shorter events, 1.3 us)
Async XLA Ops:
  0.0 14.7 %copy-start.11 = (s32[1,3,4]{2,0,1:T(1,128)S(1)}, s32[1,3,4]{2,0,1:T(1,128)}, u32[]{:S(2)}) copy-start(s32[1,3,4]{2,0,1:T(1,128)} %param.13) | copy-start | bytes 148
  0.0 14.8 %copy-start.10 = (s32[1,3,8]{2,0,1:T(1,128)S(1)}, s32[1,3,8]{2,0,1:T(1,128)}, u32[]{:S(2)}) copy-start(s32[1,3,8]{2,0,1:T(1,128)} %param.15) | copy-start | bytes 292
  1.3 32.3 %collective-permute-start.6 = (f16[1,128,1024]{2,1,0:T(8,128)(2,1)S(1)}, f16[1,128,1024]{2,1,0:T(8,128)(2,1)S(1)}, u32[]{:S(2)}, u32[]{:S(2)}) collective-permute-start(f16[1,128,1024]{2,1,0:T(8,128)(2,1)S(1)} %fusion.11), channel_id=1, source_target_pairs={{16,47},{17,34},{18,33},{19,36},{20,35},{21,38},{22,37},{23,40},{2... | collective-permute-start | bytes 786440 | tf_op jit(solution)/shard_map/ppermute | solution.py:35
  5.6 31.7 %collective-permute-start.5 = (f16[1,128,1024]{2,1,0:T(8,128)(2,1)S(1)}, f16[1,128,1024]{2,1,0:T(8,128)(2,1)S(1)}, u32[]{:S(2)}, u32[]{:S(2)}) collective-permute-start(f16[1,128,1024]{2,1,0:T(8,128)(2,1)S(1)} %fusion.11), channel_id=1, source_target_pairs={{0,31},{1,18},{2,17},{3,20},{4,19},{5,22},{6,21},{7,24},{8,23},{9,... | collective-permute-start | bytes 786440 | tf_op jit(solution)/shard_map/ppermute | solution.py:35
  7.3 30.8 %collective-permute-start.4 = (f16[1,128,1024]{2,1,0:T(8,128)(2,1)S(1)}, f16[1,128,1024]{2,1,0:T(8,128)(2,1)S(1)}, u32[]{:S(2)}, u32[]{:S(2)}) collective-permute-start(f16[1,128,1024]{2,1,0:T(8,128)(2,1)S(1)} %fusion.11), channel_id=1, source_target_pairs={{0,15},{1,2},{2,1},{3,4},{4,3},{5,6},{6,5},{7,8},{8,7},{9,10},{10,... | collective-permute-start | bytes 786440 | tf_op jit(solution)/shard_map/ppermute | solution.py:35
  11.7 12.8 %collective-permute-start.1 = (f16[1,128,1024]{2,1,0:T(8,128)(2,1)S(1)}, f16[1,128,1024]{2,1,0:T(8,128)(2,1)S(1)}, u32[]{:S(2)}, u32[]{:S(2)}) collective-permute-start(f16[1,128,1024]{2,1,0:T(8,128)(2,1)S(1)} %get-tuple-element.24), channel_id=1, source_target_pairs={{0,16},{1,17},{2,18},{3,19},{4,20},{5,21},{6,22},{7,23},{8,24},{9,... | collective-permute-start | bytes 786440 | tf_op jit(solution)/shard_map/ppermute | solution.py:35
  11.8 16.5 %collective-permute-start = (f16[1,128,1024]{2,1,0:T(8,128)(2,1)S(1)}, f16[1,128,1024]{2,1,0:T(8,128)(2,1)S(1)}, u32[]{:S(2)}, u32[]{:S(2)}) collective-permute-start(f16[1,128,1024]{2,1,0:T(8,128)(2,1)S(1)} %get-tuple-element.25), channel_id=1, source_target_pairs={{0,16},{1,17},{2,18},{3,19},{4,20},{5,21},{6,22},{7,23},{8,24},{9,... | collective-permute-start | bytes 786440 | tf_op jit(solution)/shard_map/ppermute | solution.py:35
  28.5 19.1 %collective-permute-start.7 = (f16[2,128,1024]{2,1,0:T(8,128)(2,1)S(1)}, f16[2,128,1024]{2,1,0:T(8,128)(2,1)S(1)}, u32[]{:S(2)}, u32[]{:S(2)}) collective-permute-start(f16[2,128,1024]{2,1,0:T(8,128)(2,1)S(1)} %pad_maximum_fusion.3), channel_id=1, source_target_pairs={{0,1},{1,0},{2,3},{3,2},{4,5},{5,4},{6,7},{7,6},{8,9},{9,8},{10,11... | collective-permute-start | bytes 1572872 | tf_op jit(solution)/shard_map/ppermute | solution.py:35
  28.6 10.3 %collective-permute-start.3 = (f16[1,128,1024]{2,1,0:T(8,128)(2,1)S(1)}, f16[1,128,1024]{2,1,0:T(8,128)(2,1)S(1)}, u32[]{:S(2)}, u32[]{:S(2)}) collective-permute-start(f16[1,128,1024]{2,1,0:T(8,128)(2,1)S(1)} %collective-permute-done.1), channel_id=1, source_target_pairs={{0,32},{1,33},{2,34},{3,35},{4,36},{5,37},{6,38},{7,39},{8,40},{9,... | collective-permute-start | bytes 786440 | tf_op jit(solution)/shard_map/ppermute | solution.py:35
  33.6 10.2 %collective-permute-start.2 = (f16[1,128,1024]{2,1,0:T(8,128)(2,1)S(1)}, f16[1,128,1024]{2,1,0:T(8,128)(2,1)S(1)}, u32[]{:S(2)}, u32[]{:S(2)}) collective-permute-start(f16[1,128,1024]{2,1,0:T(8,128)(2,1)S(1)} %collective-permute-done), channel_id=1, source_target_pairs={{0,32},{1,33},{2,34},{3,35},{4,36},{5,37},{6,38},{7,39},{8,40},{9,... | collective-permute-start | bytes 786440 | tf_op jit(solution)/shard_map/ppermute | solution.py:35
  43.9 2.9 %collective-permute-start.8 = (f16[1,128,1024]{2,1,0:T(8,128)(2,1)S(1)}, f16[1,128,1024]{2,1,0:T(8,128)(2,1)S(1)}, u32[]{:S(2)}, u32[]{:S(2)}) collective-permute-start(f16[1,128,1024]{2,1,0:T(8,128)(2,1)S(1)} %broadcast_select_fusion), channel_id=1, source_target_pairs={{0,1},{1,0},{2,3},{3,2},{4,5},{5,4},{6,7},{7,6},{8,9},{9,8},{10,11... | collective-permute-start | bytes 786440 | tf_op jit(solution)/shard_map/ppermute | solution.py:35
  57.6 49.0 %collective-permute-start.15 = (bf16[1,128,1024]{2,1,0:T(8,128)(2,1)}, bf16[1,128,1024]{2,1,0:T(8,128)(2,1)S(1)}, u32[]{:S(2)}, u32[]{:S(2)}) collective-permute-start(bf16[1,128,1024]{2,1,0:T(8,128)(2,1)} %get-tuple-element.16), channel_id=1, source_target_pairs={{16,47},{17,34},{18,33},{19,36},{20,35},{21,38},{22,37},{23,40},{2... | collective-permute-start | bytes 786440 | tf_op jit(solution)/shard_map/ppermute | solution.py:35
  60.8 45.8 %collective-permute-start.14 = (bf16[1,128,1024]{2,1,0:T(8,128)(2,1)}, bf16[1,128,1024]{2,1,0:T(8,128)(2,1)S(1)}, u32[]{:S(2)}, u32[]{:S(2)}) collective-permute-start(bf16[1,128,1024]{2,1,0:T(8,128)(2,1)} %get-tuple-element.16), channel_id=1, source_target_pairs={{0,31},{1,18},{2,17},{3,20},{4,19},{5,22},{6,21},{7,24},{8,23},{9,... | collective-permute-start | bytes 786440 | tf_op jit(solution)/shard_map/ppermute | solution.py:35
  63.3 43.3 %collective-permute-start.13 = (bf16[1,128,1024]{2,1,0:T(8,128)(2,1)}, bf16[1,128,1024]{2,1,0:T(8,128)(2,1)S(1)}, u32[]{:S(2)}, u32[]{:S(2)}) collective-permute-start(bf16[1,128,1024]{2,1,0:T(8,128)(2,1)} %get-tuple-element.16), channel_id=1, source_target_pairs={{0,15},{1,2},{2,1},{3,4},{4,3},{5,6},{6,5},{7,8},{8,7},{9,10},{10,... | collective-permute-start | bytes 786440 | tf_op jit(solution)/shard_map/ppermute | solution.py:35
  66.6 13.5 %collective-permute-start.10 = (bf16[1,128,1024]{2,1,0:T(8,128)(2,1)}, bf16[1,128,1024]{2,1,0:T(8,128)(2,1)S(1)}, u32[]{:S(2)}, u32[]{:S(2)}) collective-permute-start(bf16[1,128,1024]{2,1,0:T(8,128)(2,1)} %get-tuple-element.15), channel_id=1, source_target_pairs={{0,16},{1,17},{2,18},{3,19},{4,20},{5,21},{6,22},{7,23},{8,24},{9,... | collective-permute-start | bytes 786440 | tf_op jit(solution)/shard_map/ppermute | solution.py:35
  66.6 23.5 %collective-permute-start.9 = (bf16[2,128,1024]{2,1,0:T(8,128)(2,1)}, bf16[2,128,1024]{2,1,0:T(8,128)(2,1)S(1)}, u32[]{:S(2)}, u32[]{:S(2)}) collective-permute-start(bf16[2,128,1024]{2,1,0:T(8,128)(2,1)} %get-tuple-element.14), channel_id=1, source_target_pairs={{0,16},{1,17},{2,18},{3,19},{4,20},{5,21},{6,22},{7,23},{8,24},{9,... | collective-permute-start | bytes 1572872 | tf_op jit(solution)/shard_map/ppermute | solution.py:35
  69.6 24.0 %slice-start = ((s8[6291456]{0:T(1024)(128)(4,1)}), s8[4194304]{0:T(1024)(128)(4,1)S(1)}, s32[]{:S(2)}) async-start(s8[6291456]{0:T(1024)(128)(4,1)} %bitcast.40), calls=%async_computation | async-start | bytes 8388608
  69.6 24.0 %slice-start.1 = ((s8[6291456]{0:T(1024)(128)(4,1)}), s8[2097152]{0:T(1024)(128)(4,1)S(1)}, s32[]{:S(2)}) async-start(s8[6291456]{0:T(1024)(128)(4,1)} %bitcast.40), calls=%async_computation.1 | async-start | bytes 4194304
  75.4 2.3 %copy-start.8 = (bf16[1,128,1024]{2,1,0:T(8,128)(2,1)S(1)}, bf16[1,128,1024]{2,1,0:T(8,128)(2,1)}, u32[]{:S(2)}) copy-start(bf16[1,128,1024]{2,1,0:T(8,128)(2,1)} %get-tuple-element.15) | copy-start | bytes 786436
  75.4 2.2 %copy-start.9 = (bf16[2,128,1024]{2,1,0:T(8,128)(2,1)S(1)}, bf16[2,128,1024]{2,1,0:T(8,128)(2,1)}, u32[]{:S(2)}) copy-start(bf16[2,128,1024]{2,1,0:T(8,128)(2,1)} %get-tuple-element.14) | copy-start | bytes 1572868
  80.1 13.0 %collective-permute-start.12 = (bf16[1,128,1024]{2,1,0:T(8,128)(2,1)S(1)}, bf16[1,128,1024]{2,1,0:T(8,128)(2,1)S(1)}, u32[]{:S(2)}, u32[]{:S(2)}) collective-permute-start(bf16[1,128,1024]{2,1,0:T(8,128)(2,1)S(1)} %collective-permute-done.10), channel_id=1, source_target_pairs={{0,32},{1,33},{2,34},{3,35},{4,36},{5,37},{6,38},{7,39},{8,40},{9,... | collective-permute-start | bytes 786440 | tf_op jit(solution)/shard_map/ppermute | solution.py:35
  90.1 15.7 %collective-permute-start.11 = (bf16[2,128,1024]{2,1,0:T(8,128)(2,1)S(1)}, bf16[2,128,1024]{2,1,0:T(8,128)(2,1)S(1)}, u32[]{:S(2)}, u32[]{:S(2)}) collective-permute-start(bf16[2,128,1024]{2,1,0:T(8,128)(2,1)S(1)} %collective-permute-done.9), channel_id=1, source_target_pairs={{0,32},{1,33},{2,34},{3,35},{4,36},{5,37},{6,38},{7,39},{8,40},{9,... | collective-permute-start | bytes 1572872 | tf_op jit(solution)/shard_map/ppermute | solution.py:35
  93.1 13.6 %collective-permute-start.16 = (bf16[2,128,1024]{2,1,0:T(8,128)(2,1)S(1)}, bf16[2,128,1024]{2,1,0:T(8,128)(2,1)S(1)}, u32[]{:S(2)}, u32[]{:S(2)}) collective-permute-start(bf16[2,128,1024]{2,1,0:T(8,128)(2,1)S(1)} %pad_maximum_fusion.4), channel_id=1, source_target_pairs={{0,1},{1,0},{2,3},{3,2},{4,5},{5,4},{6,7},{7,6},{8,9},{9,8},{10,11... | collective-permute-start | bytes 1572872 | tf_op jit(solution)/shard_map/ppermute | solution.py:35
  105.8 8.3 %collective-permute-start.17 = (bf16[1,128,1024]{2,1,0:T(8,128)(2,1)S(1)}, bf16[1,128,1024]{2,1,0:T(8,128)(2,1)S(1)}, u32[]{:S(2)}, u32[]{:S(2)}) collective-permute-start(bf16[1,128,1024]{2,1,0:T(8,128)(2,1)S(1)} %slice_select_fusion.2), channel_id=1, source_target_pairs={{0,1},{1,0},{2,3},{3,2},{4,5},{5,4},{6,7},{7,6},{8,9},{9,8},{10,11... | collective-permute-start | bytes 786440 | tf_op jit(solution)/shard_map/ppermute | solution.py:35
  115.6 23.8 %copy-start.12 = (s32[1,2,4]{2,1,0:T(2,128)S(1)}, s32[1,2,4]{2,1,0:T(2,128)}, u32[]{:S(2)}) copy-start(s32[1,2,4]{2,1,0:T(2,128)} %param.22) | copy-start | bytes 100
  136.4 22.1 %collective-permute-start.18 = (bf16[2,128,1024]{2,1,0:T(8,128)(2,1)}, bf16[2,128,1024]{2,1,0:T(8,128)(2,1)S(1)}, u32[]{:S(2)}, u32[]{:S(2)}) collective-permute-start(bf16[2,128,1024]{2,1,0:T(8,128)(2,1)} %get-tuple-element.18.refs_1_), channel_id=1, source_target_pairs={{0,16},{1,17},{2,18},{3,19},{4,20},{5,21},{6,22},{7,23},{8,24},{9,... | collective-permute-start | bytes 1572872 | tf_op jit(solution)/shard_map/ppermute | solution.py:35
  137.1 27.1 %collective-permute-start.19 = (bf16[1,128,1024]{2,1,0:T(8,128)(2,1)}, bf16[1,128,1024]{2,1,0:T(8,128)(2,1)S(1)}, u32[]{:S(2)}, u32[]{:S(2)}) collective-permute-start(bf16[1,128,1024]{2,1,0:T(8,128)(2,1)} %get-tuple-element.19.refs_2_), channel_id=1, source_target_pairs={{0,16},{1,17},{2,18},{3,19},{4,20},{5,21},{6,22},{7,23},{8,24},{9,... | collective-permute-start | bytes 786440 | tf_op jit(solution)/shard_map/ppermute | solution.py:35
  139.4 44.4 %collective-permute-start.24 = (bf16[1,128,1024]{2,1,0:T(8,128)(2,1)}, bf16[1,128,1024]{2,1,0:T(8,128)(2,1)S(1)}, u32[]{:S(2)}, u32[]{:S(2)}) collective-permute-start(bf16[1,128,1024]{2,1,0:T(8,128)(2,1)} %get-tuple-element.20), channel_id=1, source_target_pairs={{16,47},{17,34},{18,33},{19,36},{20,35},{21,38},{22,37},{23,40},{2... | collective-permute-start | bytes 786440 | tf_op jit(solution)/shard_map/ppermute | solution.py:35
  142.4 41.5 %collective-permute-start.23 = (bf16[1,128,1024]{2,1,0:T(8,128)(2,1)}, bf16[1,128,1024]{2,1,0:T(8,128)(2,1)S(1)}, u32[]{:S(2)}, u32[]{:S(2)}) collective-permute-start(bf16[1,128,1024]{2,1,0:T(8,128)(2,1)} %get-tuple-element.20), channel_id=1, source_target_pairs={{0,31},{1,18},{2,17},{3,20},{4,19},{5,22},{6,21},{7,24},{8,23},{9,... | collective-permute-start | bytes 786440 | tf_op jit(solution)/shard_map/ppermute | solution.py:35
  144.7 39.2 %collective-permute-start.22 = (bf16[1,128,1024]{2,1,0:T(8,128)(2,1)}, bf16[1,128,1024]{2,1,0:T(8,128)(2,1)S(1)}, u32[]{:S(2)}, u32[]{:S(2)}) collective-permute-start(bf16[1,128,1024]{2,1,0:T(8,128)(2,1)} %get-tuple-element.20), channel_id=1, source_target_pairs={{0,15},{1,2},{2,1},{3,4},{4,3},{5,6},{6,5},{7,8},{8,7},{9,10},{10,... | collective-permute-start | bytes 786440 | tf_op jit(solution)/shard_map/ppermute | solution.py:35
  158.5 26.3 %copy-start = (bf16[2,128,1024]{2,1,0:T(8,128)(2,1)}, bf16[2,128,1024]{2,1,0:T(8,128)(2,1)S(1)}, u32[]{:S(2)}) copy-start(bf16[2,128,1024]{2,1,0:T(8,128)(2,1)S(1)} %collective-permute-done.18.refs_3_) | copy-start | bytes 1572868
  158.5 23.6 %collective-permute-start.20 = (bf16[2,128,1024]{2,1,0:T(8,128)(2,1)S(1)}, bf16[2,128,1024]{2,1,0:T(8,128)(2,1)S(1)}, u32[]{:S(2)}, u32[]{:S(2)}) collective-permute-start(bf16[2,128,1024]{2,1,0:T(8,128)(2,1)S(1)} %collective-permute-done.18.refs_3_), channel_id=1, source_target_pairs={{0,32},{1,33},{2,34},{3,35},{4,36},{5,37},{6,38},{7,39},{8,40},{9,... | collective-permute-start | bytes 1572872 | tf_op jit(solution)/shard_map/ppermute | solution.py:35
  164.2 20.7 %copy-start.2 = (bf16[1,128,1024]{2,1,0:T(8,128)(2,1)}, bf16[1,128,1024]{2,1,0:T(8,128)(2,1)S(1)}, u32[]{:S(2)}) copy-start(bf16[1,128,1024]{2,1,0:T(8,128)(2,1)S(1)} %collective-permute-done.19.refs_4_) | copy-start | bytes 786436
  164.2 17.2 %collective-permute-start.21 = (bf16[1,128,1024]{2,1,0:T(8,128)(2,1)S(1)}, bf16[1,128,1024]{2,1,0:T(8,128)(2,1)S(1)}, u32[]{:S(2)}, u32[]{:S(2)}) collective-permute-start(bf16[1,128,1024]{2,1,0:T(8,128)(2,1)S(1)} %collective-permute-done.19.refs_4_), channel_id=1, source_target_pairs={{0,32},{1,33},{2,34},{3,35},{4,36},{5,37},{6,38},{7,39},{8,40},{9,... | collective-permute-start | bytes 786440 | tf_op jit(solution)/shard_map/ppermute | solution.py:35
  181.4 3.4 %copy-start.3 = (bf16[1,128,1024]{2,1,0:T(8,128)(2,1)}, bf16[1,128,1024]{2,1,0:T(8,128)(2,1)S(1)}, u32[]{:S(2)}) copy-start(bf16[1,128,1024]{2,1,0:T(8,128)(2,1)S(1)} %collective-permute-done.21.refs_6_) | copy-start | bytes 786436
  181.4 2.5 %collective-permute-start.25 = (bf16[2,128,1024]{2,1,0:T(8,128)(2,1)S(1)}, bf16[2,128,1024]{2,1,0:T(8,128)(2,1)S(1)}, u32[]{:S(2)}, u32[]{:S(2)}) collective-permute-start(bf16[2,128,1024]{2,1,0:T(8,128)(2,1)S(1)} %pad_maximum_fusion.5), channel_id=1, source_target_pairs={{0,1},{1,0},{2,3},{3,2},{4,5},{5,4},{6,7},{7,6},{8,9},{9,8},{10,11... | collective-permute-start | bytes 1572872 | tf_op jit(solution)/shard_map/ppermute | solution.py:35
  182.1 2.7 %copy-start.1 = (bf16[2,128,1024]{2,1,0:T(8,128)(2,1)}, bf16[2,128,1024]{2,1,0:T(8,128)(2,1)S(1)}, u32[]{:S(2)}) copy-start(bf16[2,128,1024]{2,1,0:T(8,128)(2,1)S(1)} %collective-permute-done.20.refs_5_) | copy-start | bytes 1572868
  183.0 1.9 collective-permute-start.26
  183.8 1.0 copy-start.5
  183.9 1.0 copy-start.6
  183.9 1.0 copy-start.7
  183.9 1.0 copy-start.4

commit v2 on v0

--- a/solution.py
+++ b/solution.py
@@ -10,10 +10,6 @@
 EPSILON = 1e-05
 AXES = ("lat", "lon")
 GRID_SCALE = 8192.0
-
-
-def far_band(band):
-    return band - 1 if band % 2 == 0 else band + 1
 
 
 def relay_band(band):
@@ -43,36 +39,37 @@
     return index ^ 1
 
 
-def exchange(blocks, even_sector):
-    last = blocks.shape[0] - 1
-    parts = (blocks[:last], blocks[last:])
-
-    def inner_edge(halves):
-        return jnp.where(even_sector, halves[1], halves[0][:1])
-
-    edge_out = jnp.where(even_sector, parts[0][:1], parts[1])
-    near = [move(part, pair, same) for part in parts]
+def exchange(blocks):
+    near = [move(block, pair, same) for block in blocks]
+    far = [move(block, relay_band, same) for block in near]
     outer = [
-        move(edge_out, same, outer_sector), move(edge_out, pair, outer_sector), move(edge_out, far_band, outer_sector)
+        move(blocks[0], same, outer_sector),
+        move(blocks[0], pair, outer_sector),
+        move(far[0], same, outer_sector),
     ]
-    far = [move(part, relay_band, same) for part in near]
     inner = [
-        move(jnp.concatenate([inner_edge(parts), inner_edge(near)], axis=0), same, pair),
-        move(inner_edge(far), same, pair),
+        move(jnp.concatenate([blocks[-1], near[-1]], axis=0), same, pair), move(far[-1], same, pair)
     ]
-    return near, far, outer, inner
-
-
-def table_slots(global_ids, total_lon, blocks_here):
+    return near, far, outer[:2] + inner[:1], outer[2:] + inner[1:]
+
+
+def table_slots(global_ids, total_lon, blocks_here, own_in_order):
     band_here = lax.axis_index("lat")
     sector_here = lax.axis_index("lon")
     band_step = global_ids // total_lon - band_here
     column = (global_ids % total_lon - sector_here * blocks_here + 1) % total_lon
     near_step = jnp.where(band_here % 2 == 0, 1, -1)
     group = jnp.where(band_step == 0, 0, jnp.where(band_step == near_step, 1, 2))
-    outer_column = jnp.where(sector_here % 2 == 0, 0, blocks_here + 1)
-    inside = group * blocks_here + column - 1
-    outside = 3 * blocks_here + jnp.where(column == outer_column, 0, 3) + group
+    even = sector_here % 2 == 0
+    outer_column = jnp.where(even, 0, blocks_here + 1)
+    outer_first = jnp.where(even, column - 1, blocks_here - column)
+    if own_in_order:
+        outer_first = jnp.where(group == 0, column - 1, outer_first)
+    inside = group * blocks_here + outer_first
+    is_outer = column == outer_column
+    outside = 3 * blocks_here + jnp.where(
+        group == 2, jnp.where(is_outer, 4, 5), jnp.where(is_outer, 0, 2) + group
+    )
     own_column = jnp.logical_and(column >= 1, column <= blocks_here)
     return jnp.where(own_column, inside, outside)
 
@@ -93,20 +90,22 @@
     return (centred * lax.rsqrt(spread + EPSILON) * gain).astype(jnp.bfloat16)
 
 
-def split_weights(weight, split):
-    count, rows, width = weight.shape
-    for k in range(count):
-        full = weight[k]
-        upper = full.astype(jnp.bfloat16)
-        split[0:rows, k * width:(k + 1) * width] = upper
-        split[rows:2 * rows, k * width:(k + 1) * width] = (full - upper.astype(jnp.float32)).astype(jnp.bfloat16)
-
-
-def mix_blocks(slots, place, weight, table, upper, lower, split):
-    count, rows, width = weight.shape
-    split_weights(weight, split)
-    for k in range(count):
-        block = table[slots[place * count + k]]
+def two_parts(values):
+    upper = lax.reduce_precision(values, 8, 7)
+    return upper.astype(jnp.bfloat16), (values - upper).astype(jnp.bfloat16)
+
+
+def stacked_weights(weight):
+    count, picks, rows, width = weight.shape
+    wide = weight.transpose(0, 2, 1, 3).reshape(count, rows, picks * width)
+    return jnp.concatenate(two_parts(wide), axis=1)
+
+
+def mix_blocks(slots, place, split, table, upper, lower):
+    width = table.shape[1]
+    rows = split.shape[0] // 2
+    for k in range(split.shape[1] // width):
+        block = table[slots[place, k]]
         high = block.astype(jnp.bfloat16)
         upper[k * width:(k + 1) * width, :] = high
         if lower is not None:
@@ -118,38 +117,44 @@
     return total
 
 
-def lift_kernel(slots, *refs, piece_count):
+def block_at(place, count, even):
+    return jnp.where(even[0] == 1, place, count - 1 - place)
+
+
+def lift_kernel(slots, even, *refs, piece_count):
     pieces = refs[:piece_count]
-    weight, gains, mesh_in, normed, table, upper, lower, split, sems = refs[piece_count:]
+    split, gains, mesh_in, *rest = refs[piece_count:]
+    table, upper, lower, sems = rest[-4:]
+    parts = rest[:-4]
     copies = fill_table(pieces, table, sems)
     for copy in copies:
         copy.start()
     for copy in copies:
         copy.wait()
-    for m in range(weight.shape[0]):
-        mixed = mix_blocks(slots, m, weight.at[m], table, upper, lower, split)
+    for m, part in enumerate(parts):
+        source = block_at(m, len(parts), even)
+        mixed = mix_blocks(slots, source, split.at[source], table, upper, lower)
         mesh_in[m] = mixed
-        normed[m] = normalise(mixed, gains[0:1, :])
+        part[0] = normalise(mixed, gains[0:1, :])
 
 
 def return_kernel(slots, *refs, piece_count):
     pieces = refs[:piece_count]
-    weight, out, table, upper, split, sems = refs[piece_count:]
+    split, out, table, upper, sems = refs[piece_count:]
     copies = fill_table(pieces, table, sems)
     for copy in copies:
         copy.start()
     for copy in copies:
         copy.wait()
-    for g in range(weight.shape[0]):
-        out[g] = mix_blocks(slots, g, weight.at[g], table, upper, None, split)
-
-
-def layer_kernel(slots, counts, *refs, piece_count):
+    for g in range(split.shape[0]):
+        out[g] = mix_blocks(slots, g, split.at[g], table, upper, None)
+
+
+def layer_kernel(slots, counts, even, *refs, piece_count):
     pieces = refs[:piece_count]
-    (
-        queries, mesh_in, gains, out_hbm, up_hbm, down_hbm, mesh_out,
-        table, keys, values, mixed, out_weight, up_weight, down_weight, sems,
-    ) = refs[piece_count:]
+    queries, mesh_in, gains, out_hbm, up_hbm, down_hbm, *rest = refs[piece_count:]
+    table, keys, values, mixed, out_weight, up_weight, down_weight, sems = rest[-8:]
+    parts = rest[:-8]
     copies = fill_table(pieces, table, sems)
     weights = [
         pltpu.make_async_copy(out_hbm, out_weight, sems.at[piece_count]),
@@ -170,13 +175,14 @@
     values[:, :, wide:] = jnp.ones((HEADS // 2, neighbours * rows, wide), jnp.bfloat16)
 
     def attend(m, carry):
+        source = block_at(m, mesh_blocks, even)
         for j in range(neighbours):
-            slot = slots[m * neighbours + j]
+            slot = slots[source, j]
             keys[j * rows:(j + 1) * rows, :] = table[slot, :, 0:width]
             for h in range(HEADS // 2):
                 at = width + h * wide
                 values[h, j * rows:(j + 1) * rows, 0:wide] = table[slot, :, at:at + wide]
-        bias = jnp.where(key_block < counts[m], 0.0, -1e30)
+        bias = jnp.where(key_block < counts[source], 0.0, -1e30)
         for h in range(HEADS // 2):
             at = h * wide
             query = queries[m, :, at:at + wide] * jnp.asarray(head_size ** (-0.5), jnp.bfloat16)
@@ -212,7 +218,9 @@
     hidden = jnp.dot(again, up_weight[...], preferred_element_type=jnp.float32)
     hidden = (0.5 * hidden * (1.0 + lax.erf(hidden * 0.7071067811865476))).astype(jnp.bfloat16)
     result = after + jnp.dot(hidden, down_weight[...], preferred_element_type=jnp.float32)
-    mesh_out[...] = result.astype(jnp.bfloat16).reshape(mesh_blocks, rows, width)
+    result = result.astype(jnp.bfloat16).reshape(mesh_blocks, rows, width)
+    for m in range(mesh_blocks):
+        parts[m][0] = result[m]
 
 
 def any_specs(count):
@@ -237,36 +245,44 @@
     mesh_table = 3 * mesh_blocks + 6
     grid_table = 3 * grid_blocks + 6
 
+    even = even_sector.astype(jnp.int32).reshape(1)
+    part_shapes = [jax.ShapeDtypeStruct((1, rows, width), bf16)] * mesh_blocks
     own_grid = grid_feats[0]
-    sent = (own_grid * GRID_SCALE).astype(jnp.float16)
-    near, far, outer, inner = exchange(sent, even_sector)
-    grid_pieces = [own_grid] + [
-        piece.astype(f32) * (1.0 / GRID_SCALE) for piece in near + far + outer + inner
-    ]
-    lift_slots = table_slots(lift_index[0], grid_lon, grid_blocks).reshape(-1)
+    sent = []
+    for i in range(grid_blocks):
+        mirror = grid_blocks - 1 - i
+        chosen = jnp.where(even_sector, own_grid[i:i + 1], own_grid[mirror:mirror + 1])
+        sent.append((chosen * GRID_SCALE).astype(jnp.float16))
+    near, far, side, last = exchange(sent)
+
+    def decode(pieces):
+        return [piece.astype(f32) * (1.0 / GRID_SCALE) for piece in pieces]
+
+    grid_pieces = [own_grid] + decode(near) + decode(far)
+    grid_pieces += decode(side) + decode(last)
+    lift_slots = table_slots(lift_index[0], grid_lon, grid_blocks, True)
     picks = lift_weight.shape[2]
-    mesh_in, normed = pl.pallas_call(
+    mesh_in, *parts = pl.pallas_call(
         lambda *refs: lift_kernel(*refs, piece_count=len(grid_pieces)),
         grid_spec=pltpu.PrefetchScalarGridSpec(
-            num_scalar_prefetch=1,
+            num_scalar_prefetch=2,
             in_specs=any_specs(len(grid_pieces)) + [VMEM_SPEC, VMEM_SPEC],
-            out_specs=[VMEM_SPEC, VMEM_SPEC],
+            out_specs=[VMEM_SPEC] * (1 + mesh_blocks),
             scratch_shapes=[
                 pltpu.VMEM((grid_table, rows, width), f32),
                 pltpu.VMEM((picks * rows, width), bf16),
                 pltpu.VMEM((picks * rows, width), bf16),
-                pltpu.VMEM((2 * rows, picks * rows), bf16),
                 pltpu.SemaphoreType.DMA((len(grid_pieces),)),
             ],
         ),
         out_shape=[
             jax.ShapeDtypeStruct((mesh_blocks, rows, width), f32),
-            jax.ShapeDtypeStruct((mesh_blocks, rows, width), bf16),
-        ],
+        ] + part_shapes,
         name="lift",
-    )(lift_slots, *grid_pieces, lift_weight[0], norm_gains)
-
-    near, far, outer, inner = exchange(normed, even_sector)
+    )(lift_slots, even, *grid_pieces, stacked_weights(lift_weight[0]), norm_gains)
+
+    near, far, side, last = exchange(parts)
+    normed = jnp.concatenate(parts, axis=0)
     own = jnp.dot(normed.reshape(-1, width), qkv_weight, preferred_element_type=f32).astype(bf16)
     queries = own[:, :width].reshape(mesh_blocks, rows, width)
     kv_weight = qkv_weight[:, width:]
@@ -281,19 +297,18 @@
         )
 
     kv_pieces.append(project(near))
-    side = project(outer + inner[:1])
+    side = project(side)
     kv_pieces.append(project(far))
-    kv_pieces.append(side)
-    kv_pieces.append(project(inner[1:]))
-    window_slots = table_slots(window_index[0], mesh_lon, mesh_blocks).reshape(-1)
+    kv_pieces += [side, project(last)]
+    window_slots = table_slots(window_index[0], mesh_lon, mesh_blocks, False)
     neighbours = window_index.shape[2]
     hidden_width = up_weight.shape[1]
-    mesh_out = pl.pallas_call(
+    parts = pl.pallas_call(
         lambda *refs: layer_kernel(*refs, piece_count=len(kv_pieces)),
         grid_spec=pltpu.PrefetchScalarGridSpec(
-            num_scalar_prefetch=2,
+            num_scalar_prefetch=3,
             in_specs=any_specs(len(kv_pieces)) + [VMEM_SPEC] * 3 + any_specs(3),
-            out_specs=VMEM_SPEC,
+            out_specs=[VMEM_SPEC] * mesh_blocks,
             scratch_shapes=[
                 pltpu.VMEM((mesh_table, rows, 2 * width), bf16),
                 pltpu.VMEM((neighbours * rows, width), bf16),
@@ -305,16 +320,16 @@
                 pltpu.SemaphoreType.DMA((len(kv_pieces) + 3,)),
             ],
         ),
-        out_shape=jax.ShapeDtypeStruct((mesh_blocks, rows, width), bf16),
+        out_shape=part_shapes,
         name="layer",
     )(
-        window_slots, window_count[0], *kv_pieces, queries, mesh_in, norm_gains,
+        window_slots, window_count[0], even, *kv_pieces, queries, mesh_in, norm_gains,
         out_weight, up_weight, down_weight,
     )
 
-    near, far, outer, inner = exchange(mesh_out, even_sector)
-    mesh_pieces = [mesh_out] + near + far + outer + inner
-    return_slots = table_slots(return_index[0], mesh_lon, mesh_blocks).reshape(-1)
+    near, far, side, last = exchange(parts)
+    mesh_pieces = list(parts) + near + far + side + last
+    return_slots = table_slots(return_index[0], mesh_lon, mesh_blocks, False)
     grid_out = pl.pallas_call(
         lambda *refs: return_kernel(*refs, piece_count=len(mesh_pieces)),
         grid_spec=pltpu.PrefetchScalarGridSpec(
@@ -324,13 +339,12 @@
             scratch_shapes=[
                 pltpu.VMEM((mesh_table, rows, width), bf16),
                 pltpu.VMEM((picks * rows, width), bf16),
-                pltpu.VMEM((2 * rows, picks * rows), bf16),
                 pltpu.SemaphoreType.DMA((len(mesh_pieces),)),
             ],
         ),
         out_shape=jax.ShapeDtypeStruct((grid_blocks, rows, width), f32),
         name="give_back",
-    )(return_slots, *mesh_pieces, return_weight[0])
+    )(return_slots, *mesh_pieces, stacked_weights(return_weight[0]))
     return grid_out.reshape(1, grid_blocks, rows, width)
 
 
@@ -350,4 +364,6 @@
         P("lat", "lon", None, None, None),
     )
 
-    return jax.shard_map(shards, mesh=mesh, in_specs=placed, out_specs=P("lat", "lon", None, None), check_vma=False)
+    return jax.shard_map(
+        shards, mesh=mesh, in_specs=placed, out_specs=P("lat", "lon", None, None), check_vma=False
+    )

time: 196 us -> 177 us (0.903)
  the two profiles are of different devices: /device:TPU:21 before, /device:TPU:1 now
where the time goes in v2:
time: 177 us; the launch traced here: 176 us
  starting transfers between devices  56.2 us (32%)
  waiting for transfers between devices  45.5 us (26%)
  Pallas kernels  33.9 us (19%)
  other arithmetic  18 us (10%)
  matrix products  17.7 us (10%)
  local copies, waits for them, and re-layouts  4.47 us (3%)
    ppermute x31, starting transfers between devices, move(): return lax.ppermute(values, AXES, pairs)  56.2 us
    ppermute x31, waiting for transfers between devices, move(): return lax.ppermute(values, AXES, pairs)  45.5 us
    pallas_call x1, Pallas kernels, shards(): pl.pallas_call(lambda *refs: layer_kernel(*refs, piece_count=len(kv_piece...  20.6 us
    dot_general x4, matrix products, project(): jnp.dot(stacked.reshape(-1, width), kv_weight, preferred_element_type=f32)  11.9 us
    mul x9, other arithmetic, decode(): return [piece.astype(f32) * (1.0 / GRID_SCALE) for piece in pieces]  7.91 us
    pallas_call x1, Pallas kernels, shards(): pl.pallas_call(lambda *refs: lift_kernel(*refs, piece_count=len(grid_piec...  7.73 us
    dot_general x1, matrix products, shards(): jnp.dot(normed.reshape(-1, width), qkv_weight, preferred_element_type=f32)  5.77 us
    pallas_call x1, Pallas kernels, shards(): pl.pallas_call(lambda *refs: return_kernel(*refs, piece_count=len(mesh_pi...  5.58 us
  transfers between devices with their start and end apart: 31, of which 10 were waited for; matrix products, arithmetic and copies ran while one was open for 19% of the time, Pallas kernels for 0%

profile of v2, /device:TPU:1, one launch (start us, length us, event | category | flops | bytes accessed | tf_op | source)
XLA Modules:
  0.0 176.3 jit_solution(4914361228454945114)
XLA Ops:
  0.0 1.4 fusion.11
  1.4 3.8 %collective-permute-start = (f16[1,128,1024]{2,1,0:T(8,128)(2,1)S(1)}, f16[1,128,1024]{2,1,0:T(8,128)(2,1)S(1)}, u32[]{:S(2)}, u32[]{:S(2)}) collective-permute-start(f16[1,128,1024]{2,1,0:T(8,128)(2,1)S(1)} %get-tuple-element.20), channel_id=1, source_target_pairs={{0,16},{1,17},{2,18},{3,19},{4,20},{5,21},{6,22},{7,23},{8,24},{9,... | collective-permute-start | bytes 786440 | tf_op jit(solution)/shard_map/ppermute | solution.py:31
  5.2 1.6 collective-permute-start.5
  6.8 2.5 %collective-permute-start.1 = (f16[1,128,1024]{2,1,0:T(8,128)(2,1)S(1)}, f16[1,128,1024]{2,1,0:T(8,128)(2,1)S(1)}, u32[]{:S(2)}, u32[]{:S(2)}) collective-permute-start(f16[1,128,1024]{2,1,0:T(8,128)(2,1)S(1)} %get-tuple-element.19), channel_id=1, source_target_pairs={{0,16},{1,17},{2,18},{3,19},{4,20},{5,21},{6,22},{7,23},{8,24},{9,... | collective-permute-start | bytes 786440 | tf_op jit(solution)/shard_map/ppermute | solution.py:31
  9.4 0.7 broadcast_remainder_fusion
  10.1 0.7 sign_compare_fusion
  10.9 1.3 fusion.21.refs_0_
  12.2 1.0 pad_maximum_fusion.1.refs_12_
  13.1 0.6 add_select_fusion.6.refs_0_
  13.7 11.6 %collective-permute-done.1 = f16[1,128,1024]{2,1,0:T(8,128)(2,1)S(1)} collective-permute-done((f16[1,128,1024]{2,1,0:T(8,128)(2,1)S(1)}, f16[1,128,1024]{2,1,0:T(8,128)(2,1)S(1)}, u32[]{:S(2)}, u32[]{:S(2)}) %collective-permute-start.1) | collective-permute-done | bytes 262176 | tf_op jit(solution)/shard_map/ppermute | solution.py:31
  25.4 3.5 %collective-permute-start.3 = (f16[1,128,1024]{2,1,0:T(8,128)(2,1)S(1)}, f16[1,128,1024]{2,1,0:T(8,128)(2,1)S(1)}, u32[]{:S(2)}, u32[]{:S(2)}) collective-permute-start(f16[1,128,1024]{2,1,0:T(8,128)(2,1)S(1)} %collective-permute-done.1), channel_id=1, source_target_pairs={{0,32},{1,33},{2,34},{3,35},{4,36},{5,37},{6,38},{7,39},{8,40},{9,... | collective-permute-start | bytes 786440 | tf_op jit(solution)/shard_map/ppermute | solution.py:31
  29.0 0.9 convert_multiply_fusion.7.refs_4_
  29.8 3.5 %collective-permute-start.2 = (f16[1,128,1024]{2,1,0:T(8,128)(2,1)S(1)}, f16[1,128,1024]{2,1,0:T(8,128)(2,1)S(1)}, u32[]{:S(2)}, u32[]{:S(2)}) collective-permute-start(f16[1,128,1024]{2,1,0:T(8,128)(2,1)S(1)} %collective-permute-done), channel_id=1, source_target_pairs={{0,32},{1,33},{2,34},{3,35},{4,36},{5,37},{6,38},{7,39},{8,40},{9,... | collective-permute-start | bytes 786440 | tf_op jit(solution)/shard_map/ppermute | solution.py:31
  33.4 0.9 convert_multiply_fusion.8.refs_3_
  34.2 0.9 convert_multiply_fusion.3.refs_8_
  35.1 0.9 convert_multiply_fusion.4.refs_7_
  35.9 1.0 collective-permute-start.8
  37.0 0.8 convert_multiply_fusion.5.refs_6_
  37.8 1.9 %collective-permute-done.2 = f16[1,128,1024]{2,1,0:T(8,128)(2,1)S(1)} collective-permute-done((f16[1,128,1024]{2,1,0:T(8,128)(2,1)S(1)}, f16[1,128,1024]{2,1,0:T(8,128)(2,1)S(1)}, u32[]{:S(2)}, u32[]{:S(2)}) %collective-permute-start.2) | collective-permute-done | bytes 262176 | tf_op jit(solution)/shard_map/ppermute | solution.py:31
  39.7 3.7 %collective-permute-start.7 = (f16[1,128,1024]{2,1,0:T(8,128)(2,1)S(1)}, f16[1,128,1024]{2,1,0:T(8,128)(2,1)S(1)}, u32[]{:S(2)}, u32[]{:S(2)}) collective-permute-start(f16[1,128,1024]{2,1,0:T(8,128)(2,1)S(1)} %collective-permute-done.2), channel_id=1, source_target_pairs={{0,15},{1,2},{2,1},{3,4},{4,3},{5,6},{6,5},{7,8},{8,7},{9,10},{10,... | collective-permute-start | bytes 786440 | tf_op jit(solution)/shard_map/ppermute | solution.py:31
  43.4 0.9 convert_multiply_fusion.6.refs_5_
  44.2 0.8 convert_multiply_fusion.1.refs_11_
  45.1 1.1 convert_multiply_fusion.refs_9_
  46.2 4.1 %collective-permute-done.7 = f16[1,128,1024]{2,1,0:T(8,128)(2,1)S(1)} collective-permute-done((f16[1,128,1024]{2,1,0:T(8,128)(2,1)S(1)}, f16[1,128,1024]{2,1,0:T(8,128)(2,1)S(1)}, u32[]{:S(2)}, u32[]{:S(2)}) %collective-permute-start.7) | collective-permute-done | bytes 262176 | tf_op jit(solution)/shard_map/ppermute | solution.py:31
  50.2 0.9 convert_multiply_fusion.2.refs_10_
  51.1 7.7 %lift.1 = (f32[3,128,1024]{2,1,0:T(8,128)}, bf16[1,128,1024]{2,1,0:T(8,128)(2,1)}, bf16[1,128,1024]{2,1,0:T(8,128)(2,1)}, bf16[1,128,1024]{2,1,0:T(8,128)(2,1)}) custom-call(s32[3,4]{1,0:T(4,128)} %fusion.21.refs_0_, s32[1]{0:T(128)} %bitcast.4.refs_1_.refs_2_, f32[2,128,1024]{2,1,0:T(8,128)} %bitcast.113, f32[1,128,1024]{2,1,0:T(8,128)} %convert_multiply_fusion.8.refs_3_, ...), custom_call_target="tpu_custom_call" | custom-call | tf_op jit(solution)/shard_map/lift/pallas_call | solution.py:265
  58.8 2.6 %collective-permute-start.9 = (bf16[1,128,1024]{2,1,0:T(8,128)(2,1)}, bf16[1,128,1024]{2,1,0:T(8,128)(2,1)S(1)}, u32[]{:S(2)}, u32[]{:S(2)}) collective-permute-start(bf16[1,128,1024]{2,1,0:T(8,128)(2,1)} %get-tuple-element.12), channel_id=1, source_target_pairs={{0,16},{1,17},{2,18},{3,19},{4,20},{5,21},{6,22},{7,23},{8,24},{9,... | collective-permute-start | bytes 786440 | tf_op jit(solution)/shard_map/ppermute | solution.py:31
  61.5 1.4 collective-permute-start.15
  63.3 1.6 collective-permute-start.11
  65.0 1.3 collective-permute-start.10
  66.3 1.3 pad_maximum_fusion.2
  67.7 5.8 %convolution_convert_fusion = bf16[384,3072]{1,0:T(8,128)(2,1)S(1)} fusion(bf16[384,1024]{1,0:T(8,128)(2,1)S(1)} %bitcast.121, bf16[1024,3072]{1,0:T(8,128)(2,1)} %param.18), kind=kOutput, calls=%fused_computation | convolution fusion | flops 2417098752 | bytes 9437184 | tf_op jit(solution)/shard_map/dot_general | solution.py:286
  73.5 1.3 slice.24
  74.8 0.9 slice.25
  75.7 4.1 %collective-permute-start.12 = (bf16[1,128,1024]{2,1,0:T(8,128)(2,1)S(1)}, bf16[1,128,1024]{2,1,0:T(8,128)(2,1)S(1)}, u32[]{:S(2)}, u32[]{:S(2)}) collective-permute-start(bf16[1,128,1024]{2,1,0:T(8,128)(2,1)S(1)} %collective-permute-done.9), channel_id=1, source_target_pairs={{0,32},{1,33},{2,34},{3,35},{4,36},{5,37},{6,38},{7,39},{8,40},{9,... | collective-permute-start | bytes 786440 | tf_op jit(solution)/shard_map/ppermute | solution.py:31
  79.8 5.2 %collective-permute-done.11 = bf16[1,128,1024]{2,1,0:T(8,128)(2,1)S(1)} collective-permute-done((bf16[1,128,1024]{2,1,0:T(8,128)(2,1)}, bf16[1,128,1024]{2,1,0:T(8,128)(2,1)S(1)}, u32[]{:S(2)}, u32[]{:S(2)}) %collective-permute-start.11) | collective-permute-done | bytes 262176 | tf_op jit(solution)/shard_map/ppermute | solution.py:31
  85.0 4.3 %collective-permute-start.14 = (bf16[1,128,1024]{2,1,0:T(8,128)(2,1)S(1)}, bf16[1,128,1024]{2,1,0:T(8,128)(2,1)S(1)}, u32[]{:S(2)}, u32[]{:S(2)}) collective-permute-start(bf16[1,128,1024]{2,1,0:T(8,128)(2,1)S(1)} %collective-permute-done.11), channel_id=1, source_target_pairs={{0,32},{1,33},{2,34},{3,35},{4,36},{5,37},{6,38},{7,39},{8,40},{9,... | collective-permute-start | bytes 786440 | tf_op jit(solution)/shard_map/ppermute | solution.py:31
  89.3 3.4 %collective-permute-start.13 = (bf16[1,128,1024]{2,1,0:T(8,128)(2,1)S(1)}, bf16[1,128,1024]{2,1,0:T(8,128)(2,1)S(1)}, u32[]{:S(2)}, u32[]{:S(2)}) collective-permute-start(bf16[1,128,1024]{2,1,0:T(8,128)(2,1)S(1)} %collective-permute-done.10), channel_id=1, source_target_pairs={{0,32},{1,33},{2,34},{3,35},{4,36},{5,37},{6,38},{7,39},{8,40},{9,... | collective-permute-start | bytes 786440 | tf_op jit(solution)/shard_map/ppermute | solution.py:31
  92.8 3.0 %convolution_convert_fusion.3 = bf16[384,2048]{1,0:T(8,128)(2,1)} fusion(bf16[384,1024]{1,0:T(8,128)(2,1)S(1)} %bitcast.122, bf16[1024,3072]{1,0:T(8,128)(2,1)S(1)} %bitcast.126), kind=kOutput, calls=%fused_computation.3 | convolution fusion | flops 1611399168 | bytes 6553600 | tf_op jit(solution)/shard_map/dot_general | solution.py:294
  96.1 2.1 %collective-permute-done.13 = bf16[1,128,1024]{2,1,0:T(8,128)(2,1)S(1)} collective-permute-done((bf16[1,128,1024]{2,1,0:T(8,128)(2,1)S(1)}, bf16[1,128,1024]{2,1,0:T(8,128)(2,1)S(1)}, u32[]{:S(2)}, u32[]{:S(2)}) %collective-permute-start.13) | collective-permute-done | bytes 262176 | tf_op jit(solution)/shard_map/ppermute | solution.py:31
  98.2 1.9 %collective-permute-start.19 = (bf16[1,128,1024]{2,1,0:T(8,128)(2,1)S(1)}, bf16[1,128,1024]{2,1,0:T(8,128)(2,1)S(1)}, u32[]{:S(2)}, u32[]{:S(2)}) collective-permute-start(bf16[1,128,1024]{2,1,0:T(8,128)(2,1)S(1)} %collective-permute-done.14), channel_id=1, source_target_pairs={{0,1},{1,0},{2,3},{3,2},{4,5},{5,4},{6,7},{7,6},{8,9},{9,8},{10,11... | collective-permute-start | bytes 786440 | tf_op jit(solution)/shard_map/ppermute | solution.py:31
  100.2 3.0 %convolution_convert_fusion.2 = bf16[384,2048]{1,0:T(8,128)(2,1)} fusion(bf16[384,1024]{1,0:T(8,128)(2,1)S(1)} %bitcast.120, bf16[1024,3072]{1,0:T(8,128)(2,1)S(1)} %bitcast.126), kind=kOutput, calls=%fused_computation.2 | convolution fusion | flops 1611399168 | bytes 6553600 | tf_op jit(solution)/shard_map/dot_general | solution.py:294
  103.3 3.7 %convolution_convert_fusion.1 = bf16[512,2048]{1,0:T(8,128)(2,1)} fusion(bf16[512,1024]{1,0:T(8,128)(2,1)S(1)} %bitcast.119, bf16[1024,3072]{1,0:T(8,128)(2,1)S(1)} %bitcast.126), kind=kOutput, calls=%fused_computation.1 | convolution fusion | flops 2148532224 | bytes 7340032 | tf_op jit(solution)/shard_map/dot_general | solution.py:294
  107.1 2.2 %fusion.5 = bf16[256,2048]{1,0:T(8,128)(2,1)} fusion(bf16[256,1024]{1,0:T(8,128)(2,1)S(1)} %bitcast.123, bf16[1024,3072]{1,0:T(8,128)(2,1)S(1)} %bitcast.126), kind=kOutput, calls=%fused_computation.9 | convolution fusion | flops 1074266112 | bytes 5767168 | tf_op jit(solution)/shard_map/dot_general | solution.py:294
  109.3 20.6 %layer.1 = (bf16[1,128,1024]{2,1,0:T(8,128)(2,1)}, bf16[1,128,1024]{2,1,0:T(8,128)(2,1)}, bf16[1,128,1024]{2,1,0:T(8,128)(2,1)}) custom-call(s32[3,8]{1,0:T(4,128)} %add_select_fusion.6.refs_0_, s32[3]{0:T(128)} %bitcast.124, s32[1]{0:T(128)} %bitcast.4.refs_1_.refs_2_, bf16[3,128,2048]{2,1,0:T(8,128)(2,1)} %bitcast.112, bf16[3,128,2048]{2,1,0:T(8,128)(2,1)} %bitcast.116, ...), custom_call_target="tpu_custom_call" | custom-call | tf_op jit(solution)/shard_map/layer/pallas_call | solution.py:306
  130.0 3.0 %collective-permute-start.22 = (bf16[1,128,1024]{2,1,0:T(8,128)(2,1)}, bf16[1,128,1024]{2,1,0:T(8,128)(2,1)S(1)}, u32[]{:S(2)}, u32[]{:S(2)}) collective-permute-start(bf16[1,128,1024]{2,1,0:T(8,128)(2,1)} %get-tuple-element.18.refs_3_), channel_id=1, source_target_pairs={{0,16},{1,17},{2,18},{3,19},{4,20},{5,21},{6,22},{7,23},{8,24},{9,... | collective-permute-start | bytes 786440 | tf_op jit(solution)/shard_map/ppermute | solution.py:31
  133.0 0.6 collective-permute-start.21
  133.6 8.8 %collective-permute-done.20.refs_4_ = bf16[1,128,1024]{2,1,0:T(8,128)(2,1)S(1)} collective-permute-done((bf16[1,128,1024]{2,1,0:T(8,128)(2,1)}, bf16[1,128,1024]{2,1,0:T(8,128)(2,1)S(1)}, u32[]{:S(2)}, u32[]{:S(2)}) %collective-permute-start.20) | collective-permute-done | bytes 262176 | tf_op jit(solution)/shard_map/ppermute | solution.py:31
  142.4 2.9 %collective-permute-start.23 = (bf16[1,128,1024]{2,1,0:T(8,128)(2,1)S(1)}, bf16[1,128,1024]{2,1,0:T(8,128)(2,1)S(1)}, u32[]{:S(2)}, u32[]{:S(2)}) collective-permute-start(bf16[1,128,1024]{2,1,0:T(8,128)(2,1)S(1)} %collective-permute-done.20.refs_4_), channel_id=1, source_target_pairs={{0,32},{1,33},{2,34},{3,35},{4,36},{5,37},{6,38},{7,39},{8,40},{9,... | collective-permute-start | bytes 786440 | tf_op jit(solution)/shard_map/ppermute | solution.py:31
  145.3 2.7 %collective-permute-done.22.refs_6_ = bf16[1,128,1024]{2,1,0:T(8,128)(2,1)S(1)} collective-permute-done((bf16[1,128,1024]{2,1,0:T(8,128)(2,1)}, bf16[1,128,1024]{2,1,0:T(8,128)(2,1)S(1)}, u32[]{:S(2)}, u32[]{:S(2)}) %collective-permute-start.22) | collective-permute-done | bytes 262176 | tf_op jit(solution)/shard_map/ppermute | solution.py:31
  148.0 2.9 %collective-permute-start.25 = (bf16[1,128,1024]{2,1,0:T(8,128)(2,1)S(1)}, bf16[1,128,1024]{2,1,0:T(8,128)(2,1)S(1)}, u32[]{:S(2)}, u32[]{:S(2)}) collective-permute-start(bf16[1,128,1024]{2,1,0:T(8,128)(2,1)S(1)} %collective-permute-done.22.refs_6_), channel_id=1, source_target_pairs={{0,32},{1,33},{2,34},{3,35},{4,36},{5,37},{6,38},{7,39},{8,40},{9,... | collective-permute-start | bytes 786440 | tf_op jit(solution)/shard_map/ppermute | solution.py:31
  150.9 1.0 pad_maximum_fusion.8
  151.9 1.7 collective-permute-start.28
  153.6 3.0 %collective-permute-done.21.refs_5_ = bf16[1,128,1024]{2,1,0:T(8,128)(2,1)S(1)} collective-permute-done((bf16[1,128,1024]{2,1,0:T(8,128)(2,1)}, bf16[1,128,1024]{2,1,0:T(8,128)(2,1)S(1)}, u32[]{:S(2)}, u32[]{:S(2)}) %collective-permute-start.21) | collective-permute-done | bytes 262176 | tf_op jit(solution)/shard_map/ppermute | solution.py:31
  156.6 3.0 %collective-permute-start.24 = (bf16[1,128,1024]{2,1,0:T(8,128)(2,1)S(1)}, bf16[1,128,1024]{2,1,0:T(8,128)(2,1)S(1)}, u32[]{:S(2)}, u32[]{:S(2)}) collective-permute-start(bf16[1,128,1024]{2,1,0:T(8,128)(2,1)S(1)} %collective-permute-done.21.refs_5_), channel_id=1, source_target_pairs={{0,32},{1,33},{2,34},{3,35},{4,36},{5,37},{6,38},{7,39},{8,40},{9,... | collective-permute-start | bytes 786440 | tf_op jit(solution)/shard_map/ppermute | solution.py:31
  159.9 0.7 collective-permute-start.30
  160.6 0.8 pad_maximum_fusion.9.refs_15_
  161.4 0.6 and_select_fusion.refs_0_
  162.1 4.6 %collective-permute-done.27.refs_11_ = bf16[1,128,1024]{2,1,0:T(8,128)(2,1)S(1)} collective-permute-done((bf16[1,128,1024]{2,1,0:T(8,128)(2,1)}, bf16[1,128,1024]{2,1,0:T(8,128)(2,1)S(1)}, u32[]{:S(2)}, u32[]{:S(2)}) %collective-permute-start.27) | collective-permute-done | bytes 262176 | tf_op jit(solution)/shard_map/ppermute | solution.py:31
  166.7 1.6 collective-permute-done.29.refs_13_
  168.3 0.7 copy-done.12
  169.0 0.7 copy-done.13
  169.7 0.8 copy-done.3
  170.5 5.6 %give_back.1 = f32[2,128,1024]{2,1,0:T(8,128)} custom-call(s32[2,4]{1,0:T(2,128)} %and_select_fusion.refs_0_, bf16[1,128,1024]{2,1,0:T(8,128)(2,1)} %get-tuple-element.16.refs_1_, bf16[1,128,1024]{2,1,0:T(8,128)(2,1)} %get-tuple-element.17.refs_2_, bf16[1,128,1024]{2,1,0:T(8,128)(2,1)} %get-tuple-element.18.refs_3_, bf16[1,128,1024]{2,1,0:T(8,128)(2,1)} %copy-done.5, ...), custom_call_target="tpu_custom_call" | custom-call | tf_op jit(solution)/shard_map/give_back/pallas_call | solution.py:333
  (70 shorter events, 1.9 us)
Async XLA Ops:
  0.0 10.8 %copy-start = (f32[1,3,4,128,128]{4,3,2,1,0:T(8,128)S(1)}, f32[1,3,4,128,128]{4,3,2,1,0:T(8,128)}, u32[]{:S(2)}) copy-start(f32[1,3,4,128,128]{4,3,2,1,0:T(8,128)} %param.14) | copy-start | bytes 2359300
  1.4 28.4 %collective-permute-start = (f16[1,128,1024]{2,1,0:T(8,128)(2,1)S(1)}, f16[1,128,1024]{2,1,0:T(8,128)(2,1)S(1)}, u32[]{:S(2)}, u32[]{:S(2)}) collective-permute-start(f16[1,128,1024]{2,1,0:T(8,128)(2,1)S(1)} %get-tuple-element.20), channel_id=1, source_target_pairs={{0,16},{1,17},{2,18},{3,19},{4,20},{5,21},{6,22},{7,23},{8,24},{9,... | collective-permute-start | bytes 786440 | tf_op jit(solution)/shard_map/ppermute | solution.py:31
  5.2 29.0 %collective-permute-start.5 = (f16[1,128,1024]{2,1,0:T(8,128)(2,1)S(1)}, f16[1,128,1024]{2,1,0:T(8,128)(2,1)S(1)}, u32[]{:S(2)}, u32[]{:S(2)}) collective-permute-start(f16[1,128,1024]{2,1,0:T(8,128)(2,1)S(1)} %get-tuple-element.20), channel_id=1, source_target_pairs={{0,31},{1,18},{2,17},{3,20},{4,19},{5,22},{6,21},{7,24},{8,23},{9,... | collective-permute-start | bytes 786440 | tf_op jit(solution)/shard_map/ppermute | solution.py:31
  6.8 28.2 %collective-permute-start.4 = (f16[1,128,1024]{2,1,0:T(8,128)(2,1)S(1)}, f16[1,128,1024]{2,1,0:T(8,128)(2,1)S(1)}, u32[]{:S(2)}, u32[]{:S(2)}) collective-permute-start(f16[1,128,1024]{2,1,0:T(8,128)(2,1)S(1)} %get-tuple-element.20), channel_id=1, source_target_pairs={{0,15},{1,2},{2,1},{3,4},{4,3},{5,6},{6,5},{7,8},{8,7},{9,10},{10,... | collective-permute-start | bytes 786440 | tf_op jit(solution)/shard_map/ppermute | solution.py:31
  6.8 18.4 %collective-permute-start.1 = (f16[1,128,1024]{2,1,0:T(8,128)(2,1)S(1)}, f16[1,128,1024]{2,1,0:T(8,128)(2,1)S(1)}, u32[]{:S(2)}, u32[]{:S(2)}) collective-permute-start(f16[1,128,1024]{2,1,0:T(8,128)(2,1)S(1)} %get-tuple-element.19), channel_id=1, source_target_pairs={{0,16},{1,17},{2,18},{3,19},{4,20},{5,21},{6,22},{7,23},{8,24},{9,... | collective-permute-start | bytes 786440 | tf_op jit(solution)/shard_map/ppermute | solution.py:31
  25.4 19.7 %collective-permute-start.6 = (f16[2,128,1024]{2,1,0:T(8,128)(2,1)S(1)}, f16[2,128,1024]{2,1,0:T(8,128)(2,1)S(1)}, u32[]{:S(2)}, u32[]{:S(2)}) collective-permute-start(f16[2,128,1024]{2,1,0:T(8,128)(2,1)S(1)} %pad_maximum_fusion.5), channel_id=1, source_target_pairs={{0,1},{1,0},{2,3},{3,2},{4,5},{5,4},{6,7},{7,6},{8,9},{9,8},{10,11... | collective-permute-start | bytes 1572872 | tf_op jit(solution)/shard_map/ppermute | solution.py:31
  25.4 10.5 %collective-permute-start.3 = (f16[1,128,1024]{2,1,0:T(8,128)(2,1)S(1)}, f16[1,128,1024]{2,1,0:T(8,128)(2,1)S(1)}, u32[]{:S(2)}, u32[]{:S(2)}) collective-permute-start(f16[1,128,1024]{2,1,0:T(8,128)(2,1)S(1)} %collective-permute-done.1), channel_id=1, source_target_pairs={{0,32},{1,33},{2,34},{3,35},{4,36},{5,37},{6,38},{7,39},{8,40},{9,... | collective-permute-start | bytes 786440 | tf_op jit(solution)/shard_map/ppermute | solution.py:31
  29.8 9.9 %collective-permute-start.2 = (f16[1,128,1024]{2,1,0:T(8,128)(2,1)S(1)}, f16[1,128,1024]{2,1,0:T(8,128)(2,1)S(1)}, u32[]{:S(2)}, u32[]{:S(2)}) collective-permute-start(f16[1,128,1024]{2,1,0:T(8,128)(2,1)S(1)} %collective-permute-done), channel_id=1, source_target_pairs={{0,32},{1,33},{2,34},{3,35},{4,36},{5,37},{6,38},{7,39},{8,40},{9,... | collective-permute-start | bytes 786440 | tf_op jit(solution)/shard_map/ppermute | solution.py:31
  35.9 8.3 %collective-permute-start.8 = (f16[1,128,1024]{2,1,0:T(8,128)(2,1)S(1)}, f16[1,128,1024]{2,1,0:T(8,128)(2,1)S(1)}, u32[]{:S(2)}, u32[]{:S(2)}) collective-permute-start(f16[1,128,1024]{2,1,0:T(8,128)(2,1)S(1)} %collective-permute-done.3), channel_id=1, source_target_pairs={{0,1},{1,0},{2,3},{3,2},{4,5},{5,4},{6,7},{7,6},{8,9},{9,8},{10,11... | collective-permute-start | bytes 786440 | tf_op jit(solution)/shard_map/ppermute | solution.py:31
  39.7 10.5 %collective-permute-start.7 = (f16[1,128,1024]{2,1,0:T(8,128)(2,1)S(1)}, f16[1,128,1024]{2,1,0:T(8,128)(2,1)S(1)}, u32[]{:S(2)}, u32[]{:S(2)}) collective-permute-start(f16[1,128,1024]{2,1,0:T(8,128)(2,1)S(1)} %collective-permute-done.2), channel_id=1, source_target_pairs={{0,15},{1,2},{2,1},{3,4},{4,3},{5,6},{6,5},{7,8},{8,7},{9,10},{10,... | collective-permute-start | bytes 786440 | tf_op jit(solution)/shard_map/ppermute | solution.py:31
  58.8 16.9 %collective-permute-start.9 = (bf16[1,128,1024]{2,1,0:T(8,128)(2,1)}, bf16[1,128,1024]{2,1,0:T(8,128)(2,1)S(1)}, u32[]{:S(2)}, u32[]{:S(2)}) collective-permute-start(bf16[1,128,1024]{2,1,0:T(8,128)(2,1)} %get-tuple-element.12), channel_id=1, source_target_pairs={{0,16},{1,17},{2,18},{3,19},{4,20},{5,21},{6,22},{7,23},{8,24},{9,... | collective-permute-start | bytes 786440 | tf_op jit(solution)/shard_map/ppermute | solution.py:31
  61.5 41.8 %collective-permute-start.15 = (bf16[1,128,1024]{2,1,0:T(8,128)(2,1)}, bf16[1,128,1024]{2,1,0:T(8,128)(2,1)S(1)}, u32[]{:S(2)}, u32[]{:S(2)}) collective-permute-start(bf16[1,128,1024]{2,1,0:T(8,128)(2,1)} %get-tuple-element.12), channel_id=1, source_target_pairs={{0,15},{1,2},{2,1},{3,4},{4,3},{5,6},{6,5},{7,8},{8,7},{9,10},{10,... | collective-permute-start | bytes 786440 | tf_op jit(solution)/shard_map/ppermute | solution.py:31
  62.9 40.3 %collective-permute-start.16 = (bf16[1,128,1024]{2,1,0:T(8,128)(2,1)}, bf16[1,128,1024]{2,1,0:T(8,128)(2,1)S(1)}, u32[]{:S(2)}, u32[]{:S(2)}) collective-permute-start(bf16[1,128,1024]{2,1,0:T(8,128)(2,1)} %get-tuple-element.12), channel_id=1, source_target_pairs={{0,31},{1,18},{2,17},{3,20},{4,19},{5,22},{6,21},{7,24},{8,23},{9,... | collective-permute-start | bytes 786440 | tf_op jit(solution)/shard_map/ppermute | solution.py:31
  63.3 21.7 %collective-permute-start.11 = (bf16[1,128,1024]{2,1,0:T(8,128)(2,1)}, bf16[1,128,1024]{2,1,0:T(8,128)(2,1)S(1)}, u32[]{:S(2)}, u32[]{:S(2)}) collective-permute-start(bf16[1,128,1024]{2,1,0:T(8,128)(2,1)} %get-tuple-element.14), channel_id=1, source_target_pairs={{0,16},{1,17},{2,18},{3,19},{4,20},{5,21},{6,22},{7,23},{8,24},{9,... | collective-permute-start | bytes 786440 | tf_op jit(solution)/shard_map/ppermute | solution.py:31
  65.0 24.3 %collective-permute-start.10 = (bf16[1,128,1024]{2,1,0:T(8,128)(2,1)}, bf16[1,128,1024]{2,1,0:T(8,128)(2,1)S(1)}, u32[]{:S(2)}, u32[]{:S(2)}) collective-permute-start(bf16[1,128,1024]{2,1,0:T(8,128)(2,1)} %get-tuple-element.13), channel_id=1, source_target_pairs={{0,16},{1,17},{2,18},{3,19},{4,20},{5,21},{6,22},{7,23},{8,24},{9,... | collective-permute-start | bytes 786440 | tf_op jit(solution)/shard_map/ppermute | solution.py:31
  66.3 26.5 %slice-start = ((s8[6291456]{0:T(1024)(128)(4,1)}), s8[4194304]{0:T(1024)(128)(4,1)S(1)}, s32[]{:S(2)}) async-start(s8[6291456]{0:T(1024)(128)(4,1)} %bitcast.125), calls=%async_computation | async-start | bytes 8388608
  67.7 25.2 %slice-start.1 = ((s8[6291456]{0:T(1024)(128)(4,1)}), s8[2097152]{0:T(1024)(128)(4,1)S(1)}, s32[]{:S(2)}) async-start(s8[6291456]{0:T(1024)(128)(4,1)} %bitcast.125), calls=%async_computation.1 | async-start | bytes 4194304
  75.7 20.2 %collective-permute-start.12 = (bf16[1,128,1024]{2,1,0:T(8,128)(2,1)S(1)}, bf16[1,128,1024]{2,1,0:T(8,128)(2,1)S(1)}, u32[]{:S(2)}, u32[]{:S(2)}) collective-permute-start(bf16[1,128,1024]{2,1,0:T(8,128)(2,1)S(1)} %collective-permute-done.9), channel_id=1, source_target_pairs={{0,32},{1,33},{2,34},{3,35},{4,36},{5,37},{6,38},{7,39},{8,40},{9,... | collective-permute-start | bytes 786440 | tf_op jit(solution)/shard_map/ppermute | solution.py:31
  85.0 11.0 %collective-permute-start.14 = (bf16[1,128,1024]{2,1,0:T(8,128)(2,1)S(1)}, bf16[1,128,1024]{2,1,0:T(8,128)(2,1)S(1)}, u32[]{:S(2)}, u32[]{:S(2)}) collective-permute-start(bf16[1,128,1024]{2,1,0:T(8,128)(2,1)S(1)} %collective-permute-done.11), channel_id=1, source_target_pairs={{0,32},{1,33},{2,34},{3,35},{4,36},{5,37},{6,38},{7,39},{8,40},{9,... | collective-permute-start | bytes 786440 | tf_op jit(solution)/shard_map/ppermute | solution.py:31
  89.3 8.9 %collective-permute-start.13 = (bf16[1,128,1024]{2,1,0:T(8,128)(2,1)S(1)}, bf16[1,128,1024]{2,1,0:T(8,128)(2,1)S(1)}, u32[]{:S(2)}, u32[]{:S(2)}) collective-permute-start(bf16[1,128,1024]{2,1,0:T(8,128)(2,1)S(1)} %collective-permute-done.10), channel_id=1, source_target_pairs={{0,32},{1,33},{2,34},{3,35},{4,36},{5,37},{6,38},{7,39},{8,40},{9,... | collective-permute-start | bytes 786440 | tf_op jit(solution)/shard_map/ppermute | solution.py:31
  92.8 3.0 %copy-start.2 = (bf16[1,128,1024]{2,1,0:T(8,128)(2,1)S(1)}, bf16[1,128,1024]{2,1,0:T(8,128)(2,1)}, u32[]{:S(2)}) copy-start(bf16[1,128,1024]{2,1,0:T(8,128)(2,1)} %get-tuple-element.14) | copy-start | bytes 786436
  95.9 7.3 %collective-permute-start.17 = (bf16[2,128,1024]{2,1,0:T(8,128)(2,1)S(1)}, bf16[2,128,1024]{2,1,0:T(8,128)(2,1)S(1)}, u32[]{:S(2)}, u32[]{:S(2)}) collective-permute-start(bf16[2,128,1024]{2,1,0:T(8,128)(2,1)S(1)} %pad_maximum_fusion.6), channel_id=1, source_target_pairs={{0,1},{1,0},{2,3},{3,2},{4,5},{5,4},{6,7},{7,6},{8,9},{9,8},{10,11... | collective-permute-start | bytes 1572872 | tf_op jit(solution)/shard_map/ppermute | solution.py:31
  96.0 11.0 %collective-permute-start.18 = (bf16[1,128,1024]{2,1,0:T(8,128)(2,1)S(1)}, bf16[1,128,1024]{2,1,0:T(8,128)(2,1)S(1)}, u32[]{:S(2)}, u32[]{:S(2)}) collective-permute-start(bf16[1,128,1024]{2,1,0:T(8,128)(2,1)S(1)} %collective-permute-done.12), channel_id=1, source_target_pairs={{0,15},{1,2},{2,1},{3,4},{4,3},{5,6},{6,5},{7,8},{8,7},{9,10},{10,... | collective-permute-start | bytes 786440 | tf_op jit(solution)/shard_map/ppermute | solution.py:31
  98.2 8.8 %collective-permute-start.19 = (bf16[1,128,1024]{2,1,0:T(8,128)(2,1)S(1)}, bf16[1,128,1024]{2,1,0:T(8,128)(2,1)S(1)}, u32[]{:S(2)}, u32[]{:S(2)}) collective-permute-start(bf16[1,128,1024]{2,1,0:T(8,128)(2,1)S(1)} %collective-permute-done.14), channel_id=1, source_target_pairs={{0,1},{1,0},{2,3},{3,2},{4,5},{5,4},{6,7},{7,6},{8,9},{9,8},{10,11... | collective-permute-start | bytes 786440 | tf_op jit(solution)/shard_map/ppermute | solution.py:31
  109.3 44.2 %copy-start.4 = (f32[1,2,4,128,128]{4,3,2,1,0:T(8,128)S(1)}, f32[1,2,4,128,128]{4,3,2,1,0:T(8,128)}, u32[]{:S(2)}) copy-start(f32[1,2,4,128,128]{4,3,2,1,0:T(8,128)} %param.23) | copy-start | bytes 1572868
  109.3 52.1 %copy-start.14 = (s32[1,2,4]{2,1,0:T(2,128)S(1)}, s32[1,2,4]{2,1,0:T(2,128)}, u32[]{:S(2)}) copy-start(s32[1,2,4]{2,1,0:T(2,128)} %param.22) | copy-start | bytes 100
  129.9 12.5 %collective-permute-start.20 = (bf16[1,128,1024]{2,1,0:T(8,128)(2,1)}, bf16[1,128,1024]{2,1,0:T(8,128)(2,1)S(1)}, u32[]{:S(2)}, u32[]{:S(2)}) collective-permute-start(bf16[1,128,1024]{2,1,0:T(8,128)(2,1)} %get-tuple-element.16.refs_1_), channel_id=1, source_target_pairs={{0,16},{1,17},{2,18},{3,19},{4,20},{5,21},{6,22},{7,23},{8,24},{9,... | collective-permute-start | bytes 786440 | tf_op jit(solution)/shard_map/ppermute | solution.py:31
  130.0 18.0 %collective-permute-start.22 = (bf16[1,128,1024]{2,1,0:T(8,128)(2,1)}, bf16[1,128,1024]{2,1,0:T(8,128)(2,1)S(1)}, u32[]{:S(2)}, u32[]{:S(2)}) collective-permute-start(bf16[1,128,1024]{2,1,0:T(8,128)(2,1)} %get-tuple-element.18.refs_3_), channel_id=1, source_target_pairs={{0,16},{1,17},{2,18},{3,19},{4,20},{5,21},{6,22},{7,23},{8,24},{9,... | collective-permute-start | bytes 786440 | tf_op jit(solution)/shard_map/ppermute | solution.py:31
  132.9 23.6 %collective-permute-start.26 = (bf16[1,128,1024]{2,1,0:T(8,128)(2,1)}, bf16[1,128,1024]{2,1,0:T(8,128)(2,1)S(1)}, u32[]{:S(2)}, u32[]{:S(2)}) collective-permute-start(bf16[1,128,1024]{2,1,0:T(8,128)(2,1)} %get-tuple-element.16.refs_1_), channel_id=1, source_target_pairs={{0,15},{1,2},{2,1},{3,4},{4,3},{5,6},{6,5},{7,8},{8,7},{9,10},{10,... | collective-permute-start | bytes 786440 | tf_op jit(solution)/shard_map/ppermute | solution.py:31
  133.0 23.6 %collective-permute-start.21 = (bf16[1,128,1024]{2,1,0:T(8,128)(2,1)}, bf16[1,128,1024]{2,1,0:T(8,128)(2,1)S(1)}, u32[]{:S(2)}, u32[]{:S(2)}) collective-permute-start(bf16[1,128,1024]{2,1,0:T(8,128)(2,1)} %get-tuple-element.17.refs_2_), channel_id=1, source_target_pairs={{0,16},{1,17},{2,18},{3,19},{4,20},{5,21},{6,22},{7,23},{8,24},{9,... | collective-permute-start | bytes 786440 | tf_op jit(solution)/shard_map/ppermute | solution.py:31
  142.4 27.3 %copy-start.5 = (bf16[1,128,1024]{2,1,0:T(8,128)(2,1)}, bf16[1,128,1024]{2,1,0:T(8,128)(2,1)S(1)}, u32[]{:S(2)}) copy-start(bf16[1,128,1024]{2,1,0:T(8,128)(2,1)S(1)} %collective-permute-done.20.refs_4_) | copy-start | bytes 786436
  142.4 17.2 %collective-permute-start.23 = (bf16[1,128,1024]{2,1,0:T(8,128)(2,1)S(1)}, bf16[1,128,1024]{2,1,0:T(8,128)(2,1)S(1)}, u32[]{:S(2)}, u32[]{:S(2)}) collective-permute-start(bf16[1,128,1024]{2,1,0:T(8,128)(2,1)S(1)} %collective-permute-done.20.refs_4_), channel_id=1, source_target_pairs={{0,32},{1,33},{2,34},{3,35},{4,36},{5,37},{6,38},{7,39},{8,40},{9,... | collective-permute-start | bytes 786440 | tf_op jit(solution)/shard_map/ppermute | solution.py:31
  148.0 21.7 %copy-start.1 = (bf16[1,128,1024]{2,1,0:T(8,128)(2,1)}, bf16[1,128,1024]{2,1,0:T(8,128)(2,1)S(1)}, u32[]{:S(2)}) copy-start(bf16[1,128,1024]{2,1,0:T(8,128)(2,1)S(1)} %collective-permute-done.22.refs_6_) | copy-start | bytes 786436
  148.0 12.0 %collective-permute-start.25 = (bf16[1,128,1024]{2,1,0:T(8,128)(2,1)S(1)}, bf16[1,128,1024]{2,1,0:T(8,128)(2,1)S(1)}, u32[]{:S(2)}, u32[]{:S(2)}) collective-permute-start(bf16[1,128,1024]{2,1,0:T(8,128)(2,1)S(1)} %collective-permute-done.22.refs_6_), channel_id=1, source_target_pairs={{0,32},{1,33},{2,34},{3,35},{4,36},{5,37},{6,38},{7,39},{8,40},{9,... | collective-permute-start | bytes 786440 | tf_op jit(solution)/shard_map/ppermute | solution.py:31
  151.9 17.8 %collective-permute-start.28 = (bf16[2,128,1024]{2,1,0:T(8,128)(2,1)S(1)}, bf16[2,128,1024]{2,1,0:T(8,128)(2,1)S(1)}, u32[]{:S(2)}, u32[]{:S(2)}) collective-permute-start(bf16[2,128,1024]{2,1,0:T(8,128)(2,1)S(1)} %pad_maximum_fusion.8), channel_id=1, source_target_pairs={{0,1},{1,0},{2,3},{3,2},{4,5},{5,4},{6,7},{7,6},{8,9},{9,8},{10,11... | collective-permute-start | bytes 1572872 | tf_op jit(solution)/shard_map/ppermute | solution.py:31
  156.6 13.1 %copy-start.7 = (bf16[1,128,1024]{2,1,0:T(8,128)(2,1)}, bf16[1,128,1024]{2,1,0:T(8,128)(2,1)S(1)}, u32[]{:S(2)}) copy-start(bf16[1,128,1024]{2,1,0:T(8,128)(2,1)S(1)} %collective-permute-done.21.refs_5_) | copy-start | bytes 786436
  156.6 10.1 %collective-permute-start.27 = (bf16[1,128,1024]{2,1,0:T(8,128)(2,1)}, bf16[1,128,1024]{2,1,0:T(8,128)(2,1)S(1)}, u32[]{:S(2)}, u32[]{:S(2)}) collective-permute-start(bf16[1,128,1024]{2,1,0:T(8,128)(2,1)} %get-tuple-element.16.refs_1_), channel_id=1, source_target_pairs={{0,31},{1,18},{2,17},{3,20},{4,19},{5,22},{6,21},{7,24},{8,23},{9,... | collective-permute-start | bytes 786440 | tf_op jit(solution)/shard_map/ppermute | solution.py:31
  156.6 13.1 %copy-start.6 = (bf16[1,128,1024]{2,1,0:T(8,128)(2,1)}, bf16[1,128,1024]{2,1,0:T(8,128)(2,1)S(1)}, u32[]{:S(2)}) copy-start(bf16[1,128,1024]{2,1,0:T(8,128)(2,1)S(1)} %collective-permute-done.26.refs_10_) | copy-start | bytes 786436
  156.6 10.1 %collective-permute-start.24 = (bf16[1,128,1024]{2,1,0:T(8,128)(2,1)S(1)}, bf16[1,128,1024]{2,1,0:T(8,128)(2,1)S(1)}, u32[]{:S(2)}, u32[]{:S(2)}) collective-permute-start(bf16[1,128,1024]{2,1,0:T(8,128)(2,1)S(1)} %collective-permute-done.21.refs_5_), channel_id=1, source_target_pairs={{0,32},{1,33},{2,34},{3,35},{4,36},{5,37},{6,38},{7,39},{8,40},{9,... | collective-permute-start | bytes 786440 | tf_op jit(solution)/shard_map/ppermute | solution.py:31
  159.6 10.1 %copy-start.8 = (bf16[1,128,1024]{2,1,0:T(8,128)(2,1)}, bf16[1,128,1024]{2,1,0:T(8,128)(2,1)S(1)}, u32[]{:S(2)}) copy-start(bf16[1,128,1024]{2,1,0:T(8,128)(2,1)S(1)} %collective-permute-done.23.refs_7_) | copy-start | bytes 786436
  159.6 8.7 %collective-permute-start.29 = (bf16[1,128,1024]{2,1,0:T(8,128)(2,1)S(1)}, bf16[1,128,1024]{2,1,0:T(8,128)(2,1)S(1)}, u32[]{:S(2)}, u32[]{:S(2)}) collective-permute-start(bf16[1,128,1024]{2,1,0:T(8,128)(2,1)S(1)} %collective-permute-done.23.refs_7_), channel_id=1, source_target_pairs={{0,15},{1,2},{2,1},{3,4},{4,3},{5,6},{6,5},{7,8},{8,7},{9,10},{10,... | collective-permute-start | bytes 786440 | tf_op jit(solution)/shard_map/ppermute | solution.py:31
  159.9 9.8 %copy-start.9 = (bf16[1,128,1024]{2,1,0:T(8,128)(2,1)}, bf16[1,128,1024]{2,1,0:T(8,128)(2,1)S(1)}, u32[]{:S(2)}) copy-start(bf16[1,128,1024]{2,1,0:T(8,128)(2,1)S(1)} %collective-permute-done.25.refs_9_) | copy-start | bytes 786436
  159.9 8.3 %collective-permute-start.30 = (bf16[1,128,1024]{2,1,0:T(8,128)(2,1)S(1)}, bf16[1,128,1024]{2,1,0:T(8,128)(2,1)S(1)}, u32[]{:S(2)}, u32[]{:S(2)}) collective-permute-start(bf16[1,128,1024]{2,1,0:T(8,128)(2,1)S(1)} %collective-permute-done.25.refs_9_), channel_id=1, source_target_pairs={{0,1},{1,0},{2,3},{3,2},{4,5},{5,4},{6,7},{7,6},{8,9},{9,8},{10,11... | collective-permute-start | bytes 786440 | tf_op jit(solution)/shard_map/ppermute | solution.py:31
  166.7 3.0 %copy-start.10 = (bf16[1,128,1024]{2,1,0:T(8,128)(2,1)}, bf16[1,128,1024]{2,1,0:T(8,128)(2,1)S(1)}, u32[]{:S(2)}) copy-start(bf16[1,128,1024]{2,1,0:T(8,128)(2,1)S(1)} %collective-permute-done.27.refs_11_) | copy-start | bytes 786436
  166.7 3.0 %copy-start.11 = (bf16[1,128,1024]{2,1,0:T(8,128)(2,1)}, bf16[1,128,1024]{2,1,0:T(8,128)(2,1)S(1)}, u32[]{:S(2)}) copy-start(bf16[1,128,1024]{2,1,0:T(8,128)(2,1)S(1)} %collective-permute-done.24.refs_8_) | copy-start | bytes 786436
  168.3 0.7 copy-start.12
  169.0 0.7 copy-start.13
  169.7 0.8 copy-start.3

commit v3 on v2

--- a/solution.py
+++ b/solution.py
@@ -10,6 +10,7 @@
 EPSILON = 1e-05
 AXES = ("lat", "lon")
 GRID_SCALE = 8192.0
+MEBI = 1024 * 1024
 
 
 def relay_band(band):
@@ -183,16 +184,24 @@
                 at = width + h * wide
                 values[h, j * rows:(j + 1) * rows, 0:wide] = table[slot, :, at:at + wide]
         bias = jnp.where(key_block < counts[source], 0.0, -1e30)
-        for h in range(HEADS // 2):
+
+        def score(h):
             at = h * wide
             query = queries[m, :, at:at + wide] * jnp.asarray(head_size ** (-0.5), jnp.bfloat16)
             none = jnp.zeros_like(query)
             pair_rows = jnp.concatenate(
                 [jnp.where(low_half, query, none), jnp.where(low_half, none, query)], axis=0
             )
-            scores = lax.dot_general(
+            return lax.dot_general(
                 pair_rows, keys[:, at:at + wide], (((1,), (1,)), ((), ())), preferred_element_type=jnp.float32
             )
+
+        following = score(0)
+        for h in range(HEADS // 2):
+            at = h * wide
+            scores = following
+            if h + 1 < HEADS // 2:
+                following = score(h + 1)
             first, second = scores[:, :certain], scores[:, certain:] + bias
             highest = jnp.maximum(
                 jnp.max(first, axis=-1, keepdims=True), jnp.max(second, axis=-1, keepdims=True)
@@ -278,6 +287,7 @@
         out_shape=[
             jax.ShapeDtypeStruct((mesh_blocks, rows, width), f32),
         ] + part_shapes,
+        compiler_params=pltpu.CompilerParams(vmem_limit_bytes=20 * MEBI),
         name="lift",
     )(lift_slots, even, *grid_pieces, stacked_weights(lift_weight[0]), norm_gains)
 
@@ -321,6 +331,7 @@
             ],
         ),
         out_shape=part_shapes,
+        compiler_params=pltpu.CompilerParams(vmem_limit_bytes=42 * MEBI),
         name="layer",
     )(
         window_slots, window_count[0], even, *kv_pieces, queries, mesh_in, norm_gains,
@@ -343,6 +354,7 @@
             ],
         ),
         out_shape=jax.ShapeDtypeStruct((grid_blocks, rows, width), f32),
+        compiler_params=pltpu.CompilerParams(vmem_limit_bytes=16 * MEBI),
         name="give_back",
     )(return_slots, *mesh_pieces, stacked_weights(return_weight[0]))
     return grid_out.reshape(1, grid_blocks, rows, width)

time: 177 us -> 157 us (0.89)
  waiting for transfers between devices: 45.5 us -> 59.4 us
  Pallas kernels: 33.9 us -> 20.7 us
  other arithmetic: 18 us -> 6.62 us
  matrix products: 17.7 us -> 10.2 us
  local copies, waits for them, and re-layouts: 4.47 us -> 0.23 us
  starting transfers between devices: 56.2 us -> 59.2 us
    ppermute x31, waiting for transfers between devices: 45.5 us -> 59.4 us  [move(): return lax.ppermute(values, AXES, pairs)]
    mul x9, other arithmetic: 7.91 us -> 1.47 us  [decode(): return [piece.astype(f32) * (1.0 / GRID_SCALE) for piece in pieces]]
    pallas_call x1, Pallas kernels: 20.6 us -> 15.1 us  [shards(): pl.pallas_call(lambda *refs: layer_kernel(*refs, piece_count=len(kv_piece...]
    pallas_call x1, Pallas kernels: 7.73 us -> 2.91 us  [shards(): pl.pallas_call(lambda *refs: lift_kernel(*refs, piece_count=len(grid_piec...]
    dot_general x4, matrix products: 11.9 us -> 7.3 us  [project(): jnp.dot(stacked.reshape(-1, width), kv_weight, preferred_element_type=f32)]
    ppermute x31, starting transfers between devices: 56.2 us -> 59.2 us  [move(): return lax.ppermute(values, AXES, pairs)]
    pallas_call x1, Pallas kernels: 5.58 us -> 2.68 us  [shards(): pl.pallas_call(lambda *refs: return_kernel(*refs, piece_count=len(mesh_pi...]
    dot_general x1, matrix products: 5.77 us -> 2.88 us  [shards(): jnp.dot(normed.reshape(-1, width), qkv_weight, preferred_element_type=f32)]
  transfers between devices with their start and end apart: 31 -> 31, of which waited for: 10 -> 13; matrix products, arithmetic and copies ran while one was open for 19% -> 9% of each run, Pallas kernels for 0% -> 0%
where the time goes in v3:
time: 157 us
  waiting for transfers between devices  59.4 us (38%)
  starting transfers between devices  59.2 us (38%)
  Pallas kernels  20.7 us (13%)
  matrix products  10.2 us (6%)
  other arithmetic  6.62 us (4%)
    ppermute x31, waiting for transfers between devices, move(): return lax.ppermute(values, AXES, pairs)  59.4 us
    ppermute x31, starting transfers between devices, move(): return lax.ppermute(values, AXES, pairs)  59.2 us
    pallas_call x1, Pallas kernels, shards(): pl.pallas_call(lambda *refs: layer_kernel(*refs, piece_count=len(kv_piece...  15.1 us
    dot_general x4, matrix products, project(): jnp.dot(stacked.reshape(-1, width), kv_weight, preferred_element_type=f32)  7.3 us
  transfers between devices with their start and end apart: 31, of which 13 were waited for; matrix products, arithmetic and copies ran while one was open for 9% of the time, Pallas kernels for 0%

profile of v3, /device:TPU:1, one launch (start us, length us, event | category | flops | bytes accessed | tf_op | source)
XLA Modules:
  0.0 157.1 jit_solution(11851230699823688314)
XLA Ops:
  0.0 2.1 %fusion.11 = (f16[1,128,1024]{2,1,0:T(8,128)(2,1)S(1)}, f16[1,128,1024]{2,1,0:T(8,128)(2,1)}) fusion(f32[1,2,128,1024]{3,2,1,0:T(8,128)} %param.12, pred[]{:T(512)S(6)} %eq.89), kind=kLoop, calls=%fused_computation.38 | loop fusion | flops 786432 | bytes 1572865 | tf_op jit(solution)/shard_map/convert_element_type | solution.py:264
  2.1 3.7 %collective-permute-start = (f16[1,128,1024]{2,1,0:T(8,128)(2,1)}, f16[1,128,1024]{2,1,0:T(8,128)(2,1)S(1)}, u32[]{:S(2)}, u32[]{:S(2)}) collective-permute-start(f16[1,128,1024]{2,1,0:T(8,128)(2,1)} %get-tuple-element.20), channel_id=1, source_target_pairs={{0,16},{1,17},{2,18},{3,19},{4,20},{5,21},{6,22},{7,23},{8,24},{9,... | collective-permute-start | bytes 786440 | tf_op jit(solution)/shard_map/ppermute | solution.py:32
  5.8 1.6 %collective-permute-start.5 = (f16[1,128,1024]{2,1,0:T(8,128)(2,1)}, f16[1,128,1024]{2,1,0:T(8,128)(2,1)}, u32[]{:S(2)}, u32[]{:S(2)}) collective-permute-start(f16[1,128,1024]{2,1,0:T(8,128)(2,1)} %get-tuple-element.20), channel_id=1, source_target_pairs={{0,31},{1,18},{2,17},{3,20},{4,19},{5,22},{6,21},{7,24},{8,23},{9,... | collective-permute-start | bytes 786440 | tf_op jit(solution)/shard_map/ppermute | solution.py:32
  7.5 2.5 %collective-permute-start.1 = (f16[1,128,1024]{2,1,0:T(8,128)(2,1)S(1)}, f16[1,128,1024]{2,1,0:T(8,128)(2,1)S(1)}, u32[]{:S(2)}, u32[]{:S(2)}) collective-permute-start(f16[1,128,1024]{2,1,0:T(8,128)(2,1)S(1)} %get-tuple-element.19), channel_id=1, source_target_pairs={{0,16},{1,17},{2,18},{3,19},{4,20},{5,21},{6,22},{7,23},{8,24},{9,... | collective-permute-start | bytes 786440 | tf_op jit(solution)/shard_map/ppermute | solution.py:32
  10.0 0.7 broadcast_remainder_fusion
  10.7 0.7 sign_compare_fusion
  11.4 0.1 reduce-precision_convert_fusion
  11.5 0.7 fusion.21.refs_0_
  12.3 13.7 %collective-permute-done.1 = f16[1,128,1024]{2,1,0:T(8,128)(2,1)S(1)} collective-permute-done((f16[1,128,1024]{2,1,0:T(8,128)(2,1)S(1)}, f16[1,128,1024]{2,1,0:T(8,128)(2,1)S(1)}, u32[]{:S(2)}, u32[]{:S(2)}) %collective-permute-start.1) | collective-permute-done | bytes 262176 | tf_op jit(solution)/shard_map/ppermute | solution.py:32
  26.0 0.1 pad_maximum_fusion.5
  26.2 0.1 collective-permute-start.6
  26.3 3.7 %collective-permute-start.3 = (f16[1,128,1024]{2,1,0:T(8,128)(2,1)S(1)}, f16[1,128,1024]{2,1,0:T(8,128)(2,1)S(1)}, u32[]{:S(2)}, u32[]{:S(2)}) collective-permute-start(f16[1,128,1024]{2,1,0:T(8,128)(2,1)S(1)} %collective-permute-done.1), channel_id=1, source_target_pairs={{0,32},{1,33},{2,34},{3,35},{4,36},{5,37},{6,38},{7,39},{8,40},{9,... | collective-permute-start | bytes 786440 | tf_op jit(solution)/shard_map/ppermute | solution.py:32
  30.0 3.5 %collective-permute-start.2 = (f16[1,128,1024]{2,1,0:T(8,128)(2,1)S(1)}, f16[1,128,1024]{2,1,0:T(8,128)(2,1)S(1)}, u32[]{:S(2)}, u32[]{:S(2)}) collective-permute-start(f16[1,128,1024]{2,1,0:T(8,128)(2,1)S(1)} %collective-permute-done), channel_id=1, source_target_pairs={{0,32},{1,33},{2,34},{3,35},{4,36},{5,37},{6,38},{7,39},{8,40},{9,... | collective-permute-start | bytes 786440 | tf_op jit(solution)/shard_map/ppermute | solution.py:32
  33.6 1.0 convert_multiply_fusion.3.refs_8_
  34.7 0.5 collective-permute-done.3
  35.2 2.0 %collective-permute-start.8 = (f16[1,128,1024]{2,1,0:T(8,128)(2,1)S(1)}, f16[1,128,1024]{2,1,0:T(8,128)(2,1)S(1)}, u32[]{:S(2)}, u32[]{:S(2)}) collective-permute-start(f16[1,128,1024]{2,1,0:T(8,128)(2,1)S(1)} %collective-permute-done.3), channel_id=1, source_target_pairs={{0,1},{1,0},{2,3},{3,2},{4,5},{5,4},{6,7},{7,6},{8,9},{9,8},{10,11... | collective-permute-start | bytes 786440 | tf_op jit(solution)/shard_map/ppermute | solution.py:32
  37.3 3.5 %collective-permute-done.2 = f16[1,128,1024]{2,1,0:T(8,128)(2,1)S(1)} collective-permute-done((f16[1,128,1024]{2,1,0:T(8,128)(2,1)S(1)}, f16[1,128,1024]{2,1,0:T(8,128)(2,1)S(1)}, u32[]{:S(2)}, u32[]{:S(2)}) %collective-permute-start.2) | collective-permute-done | bytes 262176 | tf_op jit(solution)/shard_map/ppermute | solution.py:32
  40.8 3.4 %collective-permute-start.7 = (f16[1,128,1024]{2,1,0:T(8,128)(2,1)S(1)}, f16[1,128,1024]{2,1,0:T(8,128)(2,1)S(1)}, u32[]{:S(2)}, u32[]{:S(2)}) collective-permute-start(f16[1,128,1024]{2,1,0:T(8,128)(2,1)S(1)} %collective-permute-done.2), channel_id=1, source_target_pairs={{0,15},{1,2},{2,1},{3,4},{4,3},{5,6},{6,5},{7,8},{8,7},{9,10},{10,... | collective-permute-start | bytes 786440 | tf_op jit(solution)/shard_map/ppermute | solution.py:32
  44.4 0.1 convert_multiply_fusion.refs_9_
  44.5 6.6 %collective-permute-done.7 = f16[1,128,1024]{2,1,0:T(8,128)(2,1)S(1)} collective-permute-done((f16[1,128,1024]{2,1,0:T(8,128)(2,1)S(1)}, f16[1,128,1024]{2,1,0:T(8,128)(2,1)S(1)}, u32[]{:S(2)}, u32[]{:S(2)}) %collective-permute-start.7) | collective-permute-done | bytes 262176 | tf_op jit(solution)/shard_map/ppermute | solution.py:32
  51.2 2.9 %lift.1 = (f32[3,128,1024]{2,1,0:T(8,128)S(1)}, bf16[1,128,1024]{2,1,0:T(8,128)(2,1)S(1)}, bf16[1,128,1024]{2,1,0:T(8,128)(2,1)S(1)}, bf16[1,128,1024]{2,1,0:T(8,128)(2,1)S(1)}) custom-call(s32[3,4]{1,0:T(4,128)S(1)} %fusion.21.refs_0_, s32[1]{0:T(128)} %bitcast.4.refs_1_.refs_2_, f32[2,128,1024]{2,1,0:T(8,128)S(1)} %bitcast.113, ...), custom_call_target="tpu_custom_call" | custom-call | tf_op jit(solution)/shard_map/lift/pallas_call | solution.py:274
  54.1 2.7 %collective-permute-start.9 = (bf16[1,128,1024]{2,1,0:T(8,128)(2,1)S(1)}, bf16[1,128,1024]{2,1,0:T(8,128)(2,1)S(1)}, u32[]{:S(2)}, u32[]{:S(2)}) collective-permute-start(bf16[1,128,1024]{2,1,0:T(8,128)(2,1)S(1)} %get-tuple-element.12), channel_id=1, source_target_pairs={{0,16},{1,17},{2,18},{3,19},{4,20},{5,21},{6,22},{7,23},{8,24},{9,... | collective-permute-start | bytes 786440 | tf_op jit(solution)/shard_map/ppermute | solution.py:32
  56.8 1.3 collective-permute-start.15
  58.1 0.5 collective-permute-start.16
  58.6 1.8 %collective-permute-start.11 = (bf16[1,128,1024]{2,1,0:T(8,128)(2,1)S(1)}, bf16[1,128,1024]{2,1,0:T(8,128)(2,1)S(1)}, u32[]{:S(2)}, u32[]{:S(2)}) collective-permute-start(bf16[1,128,1024]{2,1,0:T(8,128)(2,1)S(1)} %get-tuple-element.14), channel_id=1, source_target_pairs={{0,16},{1,17},{2,18},{3,19},{4,20},{5,21},{6,22},{7,23},{8,24},{9,... | collective-permute-start | bytes 786440 | tf_op jit(solution)/shard_map/ppermute | solution.py:32
  60.4 1.2 collective-permute-start.10
  61.6 0.1 pad_maximum_fusion.2
  61.7 2.9 %convolution_convert_fusion = bf16[384,3072]{1,0:T(8,128)(2,1)S(1)} fusion(bf16[384,1024]{1,0:T(8,128)(2,1)S(1)} %bitcast.122, bf16[1024,3072]{1,0:T(8,128)(2,1)S(1)} %bitcast.126), kind=kOutput, calls=%fused_computation | convolution fusion | flops 2417098752 | bytes 9437184 | tf_op jit(solution)/shard_map/dot_general | solution.py:296
  64.6 0.1 slice.24
  64.8 4.3 %collective-permute-done.9 = bf16[1,128,1024]{2,1,0:T(8,128)(2,1)S(1)} collective-permute-done((bf16[1,128,1024]{2,1,0:T(8,128)(2,1)S(1)}, bf16[1,128,1024]{2,1,0:T(8,128)(2,1)S(1)}, u32[]{:S(2)}, u32[]{:S(2)}) %collective-permute-start.9) | collective-permute-done | bytes 262176 | tf_op jit(solution)/shard_map/ppermute | solution.py:32
  69.1 4.7 %collective-permute-start.12 = (bf16[1,128,1024]{2,1,0:T(8,128)(2,1)S(1)}, bf16[1,128,1024]{2,1,0:T(8,128)(2,1)S(1)}, u32[]{:S(2)}, u32[]{:S(2)}) collective-permute-start(bf16[1,128,1024]{2,1,0:T(8,128)(2,1)S(1)} %collective-permute-done.9), channel_id=1, source_target_pairs={{0,32},{1,33},{2,34},{3,35},{4,36},{5,37},{6,38},{7,39},{8,40},{9,... | collective-permute-start | bytes 786440 | tf_op jit(solution)/shard_map/ppermute | solution.py:32
  73.8 6.2 %collective-permute-done.11 = bf16[1,128,1024]{2,1,0:T(8,128)(2,1)S(1)} collective-permute-done((bf16[1,128,1024]{2,1,0:T(8,128)(2,1)S(1)}, bf16[1,128,1024]{2,1,0:T(8,128)(2,1)S(1)}, u32[]{:S(2)}, u32[]{:S(2)}) %collective-permute-start.11) | collective-permute-done | bytes 262176 | tf_op jit(solution)/shard_map/ppermute | solution.py:32
  80.0 4.6 %collective-permute-start.14 = (bf16[1,128,1024]{2,1,0:T(8,128)(2,1)S(1)}, bf16[1,128,1024]{2,1,0:T(8,128)(2,1)S(1)}, u32[]{:S(2)}, u32[]{:S(2)}) collective-permute-start(bf16[1,128,1024]{2,1,0:T(8,128)(2,1)S(1)} %collective-permute-done.11), channel_id=1, source_target_pairs={{0,32},{1,33},{2,34},{3,35},{4,36},{5,37},{6,38},{7,39},{8,40},{9,... | collective-permute-start | bytes 786440 | tf_op jit(solution)/shard_map/ppermute | solution.py:32
  84.6 3.3 %collective-permute-start.13 = (bf16[1,128,1024]{2,1,0:T(8,128)(2,1)S(1)}, bf16[1,128,1024]{2,1,0:T(8,128)(2,1)S(1)}, u32[]{:S(2)}, u32[]{:S(2)}) collective-permute-start(bf16[1,128,1024]{2,1,0:T(8,128)(2,1)S(1)} %collective-permute-done.10), channel_id=1, source_target_pairs={{0,32},{1,33},{2,34},{3,35},{4,36},{5,37},{6,38},{7,39},{8,40},{9,... | collective-permute-start | bytes 786440 | tf_op jit(solution)/shard_map/ppermute | solution.py:32
  87.9 0.1 pad_maximum_fusion.3
  88.0 1.8 %convolution_convert_fusion.3 = bf16[384,2048]{1,0:T(8,128)(2,1)S(1)} fusion(bf16[384,1024]{1,0:T(8,128)(2,1)S(1)} %bitcast.123, bf16[1024,3072]{1,0:T(8,128)(2,1)S(1)} %bitcast.126), kind=kOutput, calls=%fused_computation.3 | convolution fusion | flops 1611399168 | bytes 6553600 | tf_op jit(solution)/shard_map/dot_general | solution.py:304
  89.9 0.1 collective-permute-start.17
  90.0 0.1 collective-permute-start.18
  90.1 3.4 %collective-permute-done.13 = bf16[1,128,1024]{2,1,0:T(8,128)(2,1)S(1)} collective-permute-done((bf16[1,128,1024]{2,1,0:T(8,128)(2,1)S(1)}, bf16[1,128,1024]{2,1,0:T(8,128)(2,1)S(1)}, u32[]{:S(2)}, u32[]{:S(2)}) %collective-permute-start.13) | collective-permute-done | bytes 262176 | tf_op jit(solution)/shard_map/ppermute | solution.py:32
  93.5 0.6 collective-permute-start.19
  94.0 0.1 pad_maximum_fusion.4
  94.1 1.8 %convolution_convert_fusion.2 = bf16[384,2048]{1,0:T(8,128)(2,1)S(1)} fusion(bf16[384,1024]{1,0:T(8,128)(2,1)S(1)} %bitcast.121, bf16[1024,3072]{1,0:T(8,128)(2,1)S(1)} %bitcast.126), kind=kOutput, calls=%fused_computation.2 | convolution fusion | flops 1611399168 | bytes 6553600 | tf_op jit(solution)/shard_map/dot_general | solution.py:304
  96.0 0.1 pad_maximum_fusion
  96.1 2.4 %convolution_convert_fusion.1 = bf16[512,2048]{1,0:T(8,128)(2,1)S(1)} fusion(bf16[512,1024]{1,0:T(8,128)(2,1)S(1)} %bitcast.120, bf16[1024,3072]{1,0:T(8,128)(2,1)S(1)} %bitcast.126), kind=kOutput, calls=%fused_computation.1 | convolution fusion | flops 2148532224 | bytes 7340032 | tf_op jit(solution)/shard_map/dot_general | solution.py:304
  98.5 0.2 collective-permute-done.18
  98.7 1.3 fusion.5
  100.1 15.1 %layer.1 = (bf16[1,128,1024]{2,1,0:T(8,128)(2,1)S(1)}, bf16[1,128,1024]{2,1,0:T(8,128)(2,1)S(1)}, bf16[1,128,1024]{2,1,0:T(8,128)(2,1)S(1)}) custom-call(s32[3,8]{1,0:T(4,128)S(1)} %add_select_fusion.6.refs_0_, s32[3]{0:T(128)S(1)} %bitcast.119, s32[1]{0:T(128)} %bitcast.4.refs_1_.refs_2_, bf16[3,128,2048]{2,1,0:T(8,128)(2,1)S(1)} %bitcast.112, ...), custom_call_target="tpu_custom_call" | custom-call | tf_op jit(solution)/shard_map/layer/pallas_call | solution.py:316
  115.2 0.5 collective-permute-start.20
  115.7 2.6 %collective-permute-start.22 = (bf16[1,128,1024]{2,1,0:T(8,128)(2,1)S(1)}, bf16[1,128,1024]{2,1,0:T(8,128)(2,1)S(1)}, u32[]{:S(2)}, u32[]{:S(2)}) collective-permute-start(bf16[1,128,1024]{2,1,0:T(8,128)(2,1)S(1)} %get-tuple-element.18.refs_3_), channel_id=1, source_target_pairs={{0,16},{1,17},{2,18},{3,19},{4,20},{5,21},{6,22},{7,23},{8,24},{9,... | collective-permute-start | bytes 786440 | tf_op jit(solution)/shard_map/ppermute | solution.py:32
  118.3 0.6 collective-permute-start.26
  118.8 0.4 collective-permute-start.21
  119.2 8.4 %collective-permute-done.20.refs_4_ = bf16[1,128,1024]{2,1,0:T(8,128)(2,1)S(1)} collective-permute-done((bf16[1,128,1024]{2,1,0:T(8,128)(2,1)S(1)}, bf16[1,128,1024]{2,1,0:T(8,128)(2,1)S(1)}, u32[]{:S(2)}, u32[]{:S(2)}) %collective-permute-start.20) | collective-permute-done | bytes 262176 | tf_op jit(solution)/shard_map/ppermute | solution.py:32
  127.6 3.9 %collective-permute-start.23 = (bf16[1,128,1024]{2,1,0:T(8,128)(2,1)S(1)}, bf16[1,128,1024]{2,1,0:T(8,128)(2,1)S(1)}, u32[]{:S(2)}, u32[]{:S(2)}) collective-permute-start(bf16[1,128,1024]{2,1,0:T(8,128)(2,1)S(1)} %collective-permute-done.20.refs_4_), channel_id=1, source_target_pairs={{0,32},{1,33},{2,34},{3,35},{4,36},{5,37},{6,38},{7,39},{8,40},{9,... | collective-permute-start | bytes 786440 | tf_op jit(solution)/shard_map/ppermute | solution.py:32
  131.6 1.7 %collective-permute-done.22.refs_6_ = bf16[1,128,1024]{2,1,0:T(8,128)(2,1)S(1)} collective-permute-done((bf16[1,128,1024]{2,1,0:T(8,128)(2,1)S(1)}, bf16[1,128,1024]{2,1,0:T(8,128)(2,1)S(1)}, u32[]{:S(2)}, u32[]{:S(2)}) %collective-permute-start.22) | collective-permute-done | bytes 262176 | tf_op jit(solution)/shard_map/ppermute | solution.py:32
  133.2 3.9 %collective-permute-start.25 = (bf16[1,128,1024]{2,1,0:T(8,128)(2,1)S(1)}, bf16[1,128,1024]{2,1,0:T(8,128)(2,1)S(1)}, u32[]{:S(2)}, u32[]{:S(2)}) collective-permute-start(bf16[1,128,1024]{2,1,0:T(8,128)(2,1)S(1)} %collective-permute-done.22.refs_6_), channel_id=1, source_target_pairs={{0,32},{1,33},{2,34},{3,35},{4,36},{5,37},{6,38},{7,39},{8,40},{9,... | collective-permute-start | bytes 786440 | tf_op jit(solution)/shard_map/ppermute | solution.py:32
  137.2 1.2 collective-permute-start.28
  138.4 0.1 reduce-precision_convert_fusion.1
  138.5 3.2 %collective-permute-done.21.refs_5_ = bf16[1,128,1024]{2,1,0:T(8,128)(2,1)S(1)} collective-permute-done((bf16[1,128,1024]{2,1,0:T(8,128)(2,1)S(1)}, bf16[1,128,1024]{2,1,0:T(8,128)(2,1)S(1)}, u32[]{:S(2)}, u32[]{:S(2)}) %collective-permute-start.21) | collective-permute-done | bytes 262176 | tf_op jit(solution)/shard_map/ppermute | solution.py:32
  141.7 3.8 %collective-permute-start.24 = (bf16[1,128,1024]{2,1,0:T(8,128)(2,1)S(1)}, bf16[1,128,1024]{2,1,0:T(8,128)(2,1)S(1)}, u32[]{:S(2)}, u32[]{:S(2)}) collective-permute-start(bf16[1,128,1024]{2,1,0:T(8,128)(2,1)S(1)} %collective-permute-done.21.refs_5_), channel_id=1, source_target_pairs={{0,32},{1,33},{2,34},{3,35},{4,36},{5,37},{6,38},{7,39},{8,40},{9,... | collective-permute-start | bytes 786440 | tf_op jit(solution)/shard_map/ppermute | solution.py:32
  145.5 0.3 collective-permute-start.29
  145.9 0.6 collective-permute-start.30
  146.5 4.9 %collective-permute-done.27.refs_11_ = bf16[1,128,1024]{2,1,0:T(8,128)(2,1)S(1)} collective-permute-done((bf16[1,128,1024]{2,1,0:T(8,128)(2,1)S(1)}, bf16[1,128,1024]{2,1,0:T(8,128)(2,1)S(1)}, u32[]{:S(2)}, u32[]{:S(2)}) %collective-permute-start.27) | collective-permute-done | bytes 262176 | tf_op jit(solution)/shard_map/ppermute | solution.py:32
  151.4 2.8 %collective-permute-done.29.refs_13_ = bf16[1,128,1024]{2,1,0:T(8,128)(2,1)S(1)} collective-permute-done((bf16[1,128,1024]{2,1,0:T(8,128)(2,1)S(1)}, bf16[1,128,1024]{2,1,0:T(8,128)(2,1)S(1)}, u32[]{:S(2)}, u32[]{:S(2)}) %collective-permute-start.29) | collective-permute-done | bytes 262176 | tf_op jit(solution)/shard_map/ppermute | solution.py:32
  154.2 2.7 %give_back.1 = f32[2,128,1024]{2,1,0:T(8,128)} custom-call(s32[2,4]{1,0:T(2,128)S(1)} %and_select_fusion.refs_0_, bf16[1,128,1024]{2,1,0:T(8,128)(2,1)S(1)} %get-tuple-element.16.refs_1_, bf16[1,128,1024]{2,1,0:T(8,128)(2,1)S(1)} %get-tuple-element.17.refs_2_, bf16[1,128,1024]{2,1,0:T(8,128)(2,1)S(1)} %get-tuple-element.18.refs_3_, ...), custom_call_target="tpu_custom_call" | custom-call | tf_op jit(solution)/shard_map/give_back/pallas_call | solution.py:344
  (52 shorter events, 0.8 us)
Async XLA Ops:
  0.0 11.4 %copy-start = (f32[1,3,4,128,128]{4,3,2,1,0:T(8,128)S(1)}, f32[1,3,4,128,128]{4,3,2,1,0:T(8,128)}, u32[]{:S(2)}) copy-start(f32[1,3,4,128,128]{4,3,2,1,0:T(8,128)} %param.14) | copy-start | bytes 2359300
  2.1 27.9 %collective-permute-start = (f16[1,128,1024]{2,1,0:T(8,128)(2,1)}, f16[1,128,1024]{2,1,0:T(8,128)(2,1)S(1)}, u32[]{:S(2)}, u32[]{:S(2)}) collective-permute-start(f16[1,128,1024]{2,1,0:T(8,128)(2,1)} %get-tuple-element.20), channel_id=1, source_target_pairs={{0,16},{1,17},{2,18},{3,19},{4,20},{5,21},{6,22},{7,23},{8,24},{9,... | collective-permute-start | bytes 786440 | tf_op jit(solution)/shard_map/ppermute | solution.py:32
  5.8 27.8 %collective-permute-start.5 = (f16[1,128,1024]{2,1,0:T(8,128)(2,1)}, f16[1,128,1024]{2,1,0:T(8,128)(2,1)}, u32[]{:S(2)}, u32[]{:S(2)}) collective-permute-start(f16[1,128,1024]{2,1,0:T(8,128)(2,1)} %get-tuple-element.20), channel_id=1, source_target_pairs={{0,31},{1,18},{2,17},{3,20},{4,19},{5,22},{6,21},{7,24},{8,23},{9,... | collective-permute-start | bytes 786440 | tf_op jit(solution)/shard_map/ppermute | solution.py:32
  7.5 27.2 %collective-permute-start.4 = (f16[1,128,1024]{2,1,0:T(8,128)(2,1)}, f16[1,128,1024]{2,1,0:T(8,128)(2,1)S(1)}, u32[]{:S(2)}, u32[]{:S(2)}) collective-permute-start(f16[1,128,1024]{2,1,0:T(8,128)(2,1)} %get-tuple-element.20), channel_id=1, source_target_pairs={{0,15},{1,2},{2,1},{3,4},{4,3},{5,6},{6,5},{7,8},{8,7},{9,10},{10,... | collective-permute-start | bytes 786440 | tf_op jit(solution)/shard_map/ppermute | solution.py:32
  7.5 18.6 %collective-permute-start.1 = (f16[1,128,1024]{2,1,0:T(8,128)(2,1)S(1)}, f16[1,128,1024]{2,1,0:T(8,128)(2,1)S(1)}, u32[]{:S(2)}, u32[]{:S(2)}) collective-permute-start(f16[1,128,1024]{2,1,0:T(8,128)(2,1)S(1)} %get-tuple-element.19), channel_id=1, source_target_pairs={{0,16},{1,17},{2,18},{3,19},{4,20},{5,21},{6,22},{7,23},{8,24},{9,... | collective-permute-start | bytes 786440 | tf_op jit(solution)/shard_map/ppermute | solution.py:32
  26.2 25.0 %copy-start.1 = (f32[1,2,128,1024]{3,2,1,0:T(8,128)S(1)}, f32[1,2,128,1024]{3,2,1,0:T(8,128)}, u32[]{:S(2)}) copy-start(f32[1,2,128,1024]{3,2,1,0:T(8,128)} %param.12) | copy-start | bytes 3145732
  26.2 25.0 %copy-start.2 = (f32[2,1024]{1,0:T(2,128)S(1)}, f32[2,1024]{1,0:T(2,128)}, u32[]{:S(2)}) copy-start(f32[2,1024]{1,0:T(2,128)} %refs_10_.1) | copy-start | bytes 24580
  26.2 18.2 %collective-permute-start.6 = (f16[2,128,1024]{2,1,0:T(8,128)(2,1)S(1)}, f16[2,128,1024]{2,1,0:T(8,128)(2,1)S(1)}, u32[]{:S(2)}, u32[]{:S(2)}) collective-permute-start(f16[2,128,1024]{2,1,0:T(8,128)(2,1)S(1)} %pad_maximum_fusion.5), channel_id=1, source_target_pairs={{0,1},{1,0},{2,3},{3,2},{4,5},{5,4},{6,7},{7,6},{8,9},{9,8},{10,11... | collective-permute-start | bytes 1572872 | tf_op jit(solution)/shard_map/ppermute | solution.py:32
  26.3 8.9 %collective-permute-start.3 = (f16[1,128,1024]{2,1,0:T(8,128)(2,1)S(1)}, f16[1,128,1024]{2,1,0:T(8,128)(2,1)S(1)}, u32[]{:S(2)}, u32[]{:S(2)}) collective-permute-start(f16[1,128,1024]{2,1,0:T(8,128)(2,1)S(1)} %collective-permute-done.1), channel_id=1, source_target_pairs={{0,32},{1,33},{2,34},{3,35},{4,36},{5,37},{6,38},{7,39},{8,40},{9,... | collective-permute-start | bytes 786440 | tf_op jit(solution)/shard_map/ppermute | solution.py:32
  30.0 10.8 %collective-permute-start.2 = (f16[1,128,1024]{2,1,0:T(8,128)(2,1)S(1)}, f16[1,128,1024]{2,1,0:T(8,128)(2,1)S(1)}, u32[]{:S(2)}, u32[]{:S(2)}) collective-permute-start(f16[1,128,1024]{2,1,0:T(8,128)(2,1)S(1)} %collective-permute-done), channel_id=1, source_target_pairs={{0,32},{1,33},{2,34},{3,35},{4,36},{5,37},{6,38},{7,39},{8,40},{9,... | collective-permute-start | bytes 786440 | tf_op jit(solution)/shard_map/ppermute | solution.py:32
  35.2 9.1 %collective-permute-start.8 = (f16[1,128,1024]{2,1,0:T(8,128)(2,1)S(1)}, f16[1,128,1024]{2,1,0:T(8,128)(2,1)S(1)}, u32[]{:S(2)}, u32[]{:S(2)}) collective-permute-start(f16[1,128,1024]{2,1,0:T(8,128)(2,1)S(1)} %collective-permute-done.3), channel_id=1, source_target_pairs={{0,1},{1,0},{2,3},{3,2},{4,5},{5,4},{6,7},{7,6},{8,9},{9,8},{10,11... | collective-permute-start | bytes 786440 | tf_op jit(solution)/shard_map/ppermute | solution.py:32
  40.8 10.3 %collective-permute-start.7 = (f16[1,128,1024]{2,1,0:T(8,128)(2,1)S(1)}, f16[1,128,1024]{2,1,0:T(8,128)(2,1)S(1)}, u32[]{:S(2)}, u32[]{:S(2)}) collective-permute-start(f16[1,128,1024]{2,1,0:T(8,128)(2,1)S(1)} %collective-permute-done.2), channel_id=1, source_target_pairs={{0,15},{1,2},{2,1},{3,4},{4,3},{5,6},{6,5},{7,8},{8,7},{9,10},{10,... | collective-permute-start | bytes 786440 | tf_op jit(solution)/shard_map/ppermute | solution.py:32
  44.3 17.4 %slice-start = ((s8[6291456]{0:T(1024)(128)(4,1)}), s8[4194304]{0:T(1024)(128)(4,1)S(1)}, s32[]{:S(2)}) async-start(s8[6291456]{0:T(1024)(128)(4,1)} %bitcast.125), calls=%async_computation | async-start | bytes 8388608
  51.2 10.5 %slice-start.1 = ((s8[6291456]{0:T(1024)(128)(4,1)}), s8[2097152]{0:T(1024)(128)(4,1)S(1)}, s32[]{:S(2)}) async-start(s8[6291456]{0:T(1024)(128)(4,1)} %bitcast.125), calls=%async_computation.1 | async-start | bytes 4194304
  54.1 15.0 %collective-permute-start.9 = (bf16[1,128,1024]{2,1,0:T(8,128)(2,1)S(1)}, bf16[1,128,1024]{2,1,0:T(8,128)(2,1)S(1)}, u32[]{:S(2)}, u32[]{:S(2)}) collective-permute-start(bf16[1,128,1024]{2,1,0:T(8,128)(2,1)S(1)} %get-tuple-element.12), channel_id=1, source_target_pairs={{0,16},{1,17},{2,18},{3,19},{4,20},{5,21},{6,22},{7,23},{8,24},{9,... | collective-permute-start | bytes 786440 | tf_op jit(solution)/shard_map/ppermute | solution.py:32
  56.8 39.1 %collective-permute-start.15 = (bf16[1,128,1024]{2,1,0:T(8,128)(2,1)S(1)}, bf16[1,128,1024]{2,1,0:T(8,128)(2,1)S(1)}, u32[]{:S(2)}, u32[]{:S(2)}) collective-permute-start(bf16[1,128,1024]{2,1,0:T(8,128)(2,1)S(1)} %get-tuple-element.12), channel_id=1, source_target_pairs={{0,15},{1,2},{2,1},{3,4},{4,3},{5,6},{6,5},{7,8},{8,7},{9,10},{10,... | collective-permute-start | bytes 786440 | tf_op jit(solution)/shard_map/ppermute | solution.py:32
  58.1 37.8 %collective-permute-start.16 = (bf16[1,128,1024]{2,1,0:T(8,128)(2,1)S(1)}, bf16[1,128,1024]{2,1,0:T(8,128)(2,1)S(1)}, u32[]{:S(2)}, u32[]{:S(2)}) collective-permute-start(bf16[1,128,1024]{2,1,0:T(8,128)(2,1)S(1)} %get-tuple-element.12), channel_id=1, source_target_pairs={{0,31},{1,18},{2,17},{3,20},{4,19},{5,22},{6,21},{7,24},{8,23},{9,... | collective-permute-start | bytes 786440 | tf_op jit(solution)/shard_map/ppermute | solution.py:32
  58.6 21.4 %collective-permute-start.11 = (bf16[1,128,1024]{2,1,0:T(8,128)(2,1)S(1)}, bf16[1,128,1024]{2,1,0:T(8,128)(2,1)S(1)}, u32[]{:S(2)}, u32[]{:S(2)}) collective-permute-start(bf16[1,128,1024]{2,1,0:T(8,128)(2,1)S(1)} %get-tuple-element.14), channel_id=1, source_target_pairs={{0,16},{1,17},{2,18},{3,19},{4,20},{5,21},{6,22},{7,23},{8,24},{9,... | collective-permute-start | bytes 786440 | tf_op jit(solution)/shard_map/ppermute | solution.py:32
  60.4 24.2 %collective-permute-start.10 = (bf16[1,128,1024]{2,1,0:T(8,128)(2,1)S(1)}, bf16[1,128,1024]{2,1,0:T(8,128)(2,1)S(1)}, u32[]{:S(2)}, u32[]{:S(2)}) collective-permute-start(bf16[1,128,1024]{2,1,0:T(8,128)(2,1)S(1)} %get-tuple-element.13), channel_id=1, source_target_pairs={{0,16},{1,17},{2,18},{3,19},{4,20},{5,21},{6,22},{7,23},{8,24},{9,... | collective-permute-start | bytes 786440 | tf_op jit(solution)/shard_map/ppermute | solution.py:32
  69.1 20.8 %collective-permute-start.12 = (bf16[1,128,1024]{2,1,0:T(8,128)(2,1)S(1)}, bf16[1,128,1024]{2,1,0:T(8,128)(2,1)S(1)}, u32[]{:S(2)}, u32[]{:S(2)}) collective-permute-start(bf16[1,128,1024]{2,1,0:T(8,128)(2,1)S(1)} %collective-permute-done.9), channel_id=1, source_target_pairs={{0,32},{1,33},{2,34},{3,35},{4,36},{5,37},{6,38},{7,39},{8,40},{9,... | collective-permute-start | bytes 786440 | tf_op jit(solution)/shard_map/ppermute | solution.py:32
  80.0 10.0 %collective-permute-start.14 = (bf16[1,128,1024]{2,1,0:T(8,128)(2,1)S(1)}, bf16[1,128,1024]{2,1,0:T(8,128)(2,1)S(1)}, u32[]{:S(2)}, u32[]{:S(2)}) collective-permute-start(bf16[1,128,1024]{2,1,0:T(8,128)(2,1)S(1)} %collective-permute-done.11), channel_id=1, source_target_pairs={{0,32},{1,33},{2,34},{3,35},{4,36},{5,37},{6,38},{7,39},{8,40},{9,... | collective-permute-start | bytes 786440 | tf_op jit(solution)/shard_map/ppermute | solution.py:32
  84.6 8.9 %collective-permute-start.13 = (bf16[1,128,1024]{2,1,0:T(8,128)(2,1)S(1)}, bf16[1,128,1024]{2,1,0:T(8,128)(2,1)S(1)}, u32[]{:S(2)}, u32[]{:S(2)}) collective-permute-start(bf16[1,128,1024]{2,1,0:T(8,128)(2,1)S(1)} %collective-permute-done.10), channel_id=1, source_target_pairs={{0,32},{1,33},{2,34},{3,35},{4,36},{5,37},{6,38},{7,39},{8,40},{9,... | collective-permute-start | bytes 786440 | tf_op jit(solution)/shard_map/ppermute | solution.py:32
  89.9 6.1 %collective-permute-start.17 = (bf16[2,128,1024]{2,1,0:T(8,128)(2,1)S(1)}, bf16[2,128,1024]{2,1,0:T(8,128)(2,1)S(1)}, u32[]{:S(2)}, u32[]{:S(2)}) collective-permute-start(bf16[2,128,1024]{2,1,0:T(8,128)(2,1)S(1)} %pad_maximum_fusion.6), channel_id=1, source_target_pairs={{0,1},{1,0},{2,3},{3,2},{4,5},{5,4},{6,7},{7,6},{8,9},{9,8},{10,11... | collective-permute-start | bytes 1572872 | tf_op jit(solution)/shard_map/ppermute | solution.py:32
  90.0 8.7 %collective-permute-start.18 = (bf16[1,128,1024]{2,1,0:T(8,128)(2,1)S(1)}, bf16[1,128,1024]{2,1,0:T(8,128)(2,1)S(1)}, u32[]{:S(2)}, u32[]{:S(2)}) collective-permute-start(bf16[1,128,1024]{2,1,0:T(8,128)(2,1)S(1)} %collective-permute-done.12), channel_id=1, source_target_pairs={{0,15},{1,2},{2,1},{3,4},{4,3},{5,6},{6,5},{7,8},{8,7},{9,10},{10,... | collective-permute-start | bytes 786440 | tf_op jit(solution)/shard_map/ppermute | solution.py:32
  93.5 5.2 %collective-permute-start.19 = (bf16[1,128,1024]{2,1,0:T(8,128)(2,1)S(1)}, bf16[1,128,1024]{2,1,0:T(8,128)(2,1)S(1)}, u32[]{:S(2)}, u32[]{:S(2)}) collective-permute-start(bf16[1,128,1024]{2,1,0:T(8,128)(2,1)S(1)} %collective-permute-done.14), channel_id=1, source_target_pairs={{0,1},{1,0},{2,3},{3,2},{4,5},{5,4},{6,7},{7,6},{8,9},{9,8},{10,11... | collective-permute-start | bytes 786440 | tf_op jit(solution)/shard_map/ppermute | solution.py:32
  98.7 1.3 copy-start.3
  100.0 38.4 %copy-start.4 = (f32[1,2,4,128,128]{4,3,2,1,0:T(8,128)S(1)}, f32[1,2,4,128,128]{4,3,2,1,0:T(8,128)}, u32[]{:S(2)}) copy-start(f32[1,2,4,128,128]{4,3,2,1,0:T(8,128)} %param.23) | copy-start | bytes 1572868
  100.1 46.4 %copy-start.5 = (s32[1,2,4]{2,1,0:T(2,128)S(1)}, s32[1,2,4]{2,1,0:T(2,128)}, u32[]{:S(2)}) copy-start(s32[1,2,4]{2,1,0:T(2,128)} %param.22) | copy-start | bytes 100
  115.2 12.4 %collective-permute-start.20 = (bf16[1,128,1024]{2,1,0:T(8,128)(2,1)S(1)}, bf16[1,128,1024]{2,1,0:T(8,128)(2,1)S(1)}, u32[]{:S(2)}, u32[]{:S(2)}) collective-permute-start(bf16[1,128,1024]{2,1,0:T(8,128)(2,1)S(1)} %get-tuple-element.16.refs_1_), channel_id=1, source_target_pairs={{0,16},{1,17},{2,18},{3,19},{4,20},{5,21},{6,22},{7,23},{8,24},{9,... | collective-permute-start | bytes 786440 | tf_op jit(solution)/shard_map/ppermute | solution.py:32
  115.7 17.6 %collective-permute-start.22 = (bf16[1,128,1024]{2,1,0:T(8,128)(2,1)S(1)}, bf16[1,128,1024]{2,1,0:T(8,128)(2,1)S(1)}, u32[]{:S(2)}, u32[]{:S(2)}) collective-permute-start(bf16[1,128,1024]{2,1,0:T(8,128)(2,1)S(1)} %get-tuple-element.18.refs_3_), channel_id=1, source_target_pairs={{0,16},{1,17},{2,18},{3,19},{4,20},{5,21},{6,22},{7,23},{8,24},{9,... | collective-permute-start | bytes 786440 | tf_op jit(solution)/shard_map/ppermute | solution.py:32
  118.3 23.4 %collective-permute-start.26 = (bf16[1,128,1024]{2,1,0:T(8,128)(2,1)S(1)}, bf16[1,128,1024]{2,1,0:T(8,128)(2,1)S(1)}, u32[]{:S(2)}, u32[]{:S(2)}) collective-permute-start(bf16[1,128,1024]{2,1,0:T(8,128)(2,1)S(1)} %get-tuple-element.16.refs_1_), channel_id=1, source_target_pairs={{0,15},{1,2},{2,1},{3,4},{4,3},{5,6},{6,5},{7,8},{8,7},{9,10},{10,... | collective-permute-start | bytes 786440 | tf_op jit(solution)/shard_map/ppermute | solution.py:32
  118.8 22.9 %collective-permute-start.21 = (bf16[1,128,1024]{2,1,0:T(8,128)(2,1)S(1)}, bf16[1,128,1024]{2,1,0:T(8,128)(2,1)S(1)}, u32[]{:S(2)}, u32[]{:S(2)}) collective-permute-start(bf16[1,128,1024]{2,1,0:T(8,128)(2,1)S(1)} %get-tuple-element.17.refs_2_), channel_id=1, source_target_pairs={{0,16},{1,17},{2,18},{3,19},{4,20},{5,21},{6,22},{7,23},{8,24},{9,... | collective-permute-start | bytes 786440 | tf_op jit(solution)/shard_map/ppermute | solution.py:32
  127.6 17.9 %collective-permute-start.23 = (bf16[1,128,1024]{2,1,0:T(8,128)(2,1)S(1)}, bf16[1,128,1024]{2,1,0:T(8,128)(2,1)S(1)}, u32[]{:S(2)}, u32[]{:S(2)}) collective-permute-start(bf16[1,128,1024]{2,1,0:T(8,128)(2,1)S(1)} %collective-permute-done.20.refs_4_), channel_id=1, source_target_pairs={{0,32},{1,33},{2,34},{3,35},{4,36},{5,37},{6,38},{7,39},{8,40},{9,... | collective-permute-start | bytes 786440 | tf_op jit(solution)/shard_map/ppermute | solution.py:32
  133.2 12.6 %collective-permute-start.25 = (bf16[1,128,1024]{2,1,0:T(8,128)(2,1)S(1)}, bf16[1,128,1024]{2,1,0:T(8,128)(2,1)S(1)}, u32[]{:S(2)}, u32[]{:S(2)}) collective-permute-start(bf16[1,128,1024]{2,1,0:T(8,128)(2,1)S(1)} %collective-permute-done.22.refs_6_), channel_id=1, source_target_pairs={{0,32},{1,33},{2,34},{3,35},{4,36},{5,37},{6,38},{7,39},{8,40},{9,... | collective-permute-start | bytes 786440 | tf_op jit(solution)/shard_map/ppermute | solution.py:32
  137.2 17.0 %collective-permute-start.28 = (bf16[2,128,1024]{2,1,0:T(8,128)(2,1)S(1)}, bf16[2,128,1024]{2,1,0:T(8,128)(2,1)S(1)}, u32[]{:S(2)}, u32[]{:S(2)}) collective-permute-start(bf16[2,128,1024]{2,1,0:T(8,128)(2,1)S(1)} %pad_maximum_fusion.8), channel_id=1, source_target_pairs={{0,1},{1,0},{2,3},{3,2},{4,5},{5,4},{6,7},{7,6},{8,9},{9,8},{10,11... | collective-permute-start | bytes 1572872 | tf_op jit(solution)/shard_map/ppermute | solution.py:32
  141.7 9.7 %collective-permute-start.27 = (bf16[1,128,1024]{2,1,0:T(8,128)(2,1)S(1)}, bf16[1,128,1024]{2,1,0:T(8,128)(2,1)S(1)}, u32[]{:S(2)}, u32[]{:S(2)}) collective-permute-start(bf16[1,128,1024]{2,1,0:T(8,128)(2,1)S(1)} %get-tuple-element.16.refs_1_), channel_id=1, source_target_pairs={{0,31},{1,18},{2,17},{3,20},{4,19},{5,22},{6,21},{7,24},{8,23},{9,... | collective-permute-start | bytes 786440 | tf_op jit(solution)/shard_map/ppermute | solution.py:32
  141.7 9.7 %collective-permute-start.24 = (bf16[1,128,1024]{2,1,0:T(8,128)(2,1)S(1)}, bf16[1,128,1024]{2,1,0:T(8,128)(2,1)S(1)}, u32[]{:S(2)}, u32[]{:S(2)}) collective-permute-start(bf16[1,128,1024]{2,1,0:T(8,128)(2,1)S(1)} %collective-permute-done.21.refs_5_), channel_id=1, source_target_pairs={{0,32},{1,33},{2,34},{3,35},{4,36},{5,37},{6,38},{7,39},{8,40},{9,... | collective-permute-start | bytes 786440 | tf_op jit(solution)/shard_map/ppermute | solution.py:32
  145.5 8.7 %collective-permute-start.29 = (bf16[1,128,1024]{2,1,0:T(8,128)(2,1)S(1)}, bf16[1,128,1024]{2,1,0:T(8,128)(2,1)S(1)}, u32[]{:S(2)}, u32[]{:S(2)}) collective-permute-start(bf16[1,128,1024]{2,1,0:T(8,128)(2,1)S(1)} %collective-permute-done.23.refs_7_), channel_id=1, source_target_pairs={{0,15},{1,2},{2,1},{3,4},{4,3},{5,6},{6,5},{7,8},{8,7},{9,10},{10,... | collective-permute-start | bytes 786440 | tf_op jit(solution)/shard_map/ppermute | solution.py:32
  145.9 8.4 %collective-permute-start.30 = (bf16[1,128,1024]{2,1,0:T(8,128)(2,1)S(1)}, bf16[1,128,1024]{2,1,0:T(8,128)(2,1)S(1)}, u32[]{:S(2)}, u32[]{:S(2)}) collective-permute-start(bf16[1,128,1024]{2,1,0:T(8,128)(2,1)S(1)} %collective-permute-done.25.refs_9_), channel_id=1, source_target_pairs={{0,1},{1,0},{2,3},{3,2},{4,5},{5,4},{6,7},{7,6},{8,9},{9,8},{10,11... | collective-permute-start | bytes 786440 | tf_op jit(solution)/shard_map/ppermute | solution.py:32

commit v4 on v3

--- a/solution.py
+++ b/solution.py
@@ -43,14 +43,8 @@
 def exchange(blocks):
     near = [move(block, pair, same) for block in blocks]
     far = [move(block, relay_band, same) for block in near]
-    outer = [
-        move(blocks[0], same, outer_sector),
-        move(blocks[0], pair, outer_sector),
-        move(far[0], same, outer_sector),
-    ]
-    inner = [
-        move(jnp.concatenate([blocks[-1], near[-1]], axis=0), same, pair), move(far[-1], same, pair)
-    ]
+    outer = [move(blocks[0], same, outer_sector), move(blocks[0], pair, outer_sector), move(far[0], same, outer_sector)]
+    inner = [move(jnp.concatenate([blocks[1], near[1]], axis=0), same, pair), move(far[1], same, pair)]
     return near, far, outer[:2] + inner[:1], outer[2:] + inner[1:]
 
 
@@ -63,7 +57,9 @@
     group = jnp.where(band_step == 0, 0, jnp.where(band_step == near_step, 1, 2))
     even = sector_here % 2 == 0
     outer_column = jnp.where(even, 0, blocks_here + 1)
-    outer_first = jnp.where(even, column - 1, blocks_here - column)
+    inner_column = jnp.where(even, blocks_here, 1)
+    at_outer = column == jnp.where(even, 1, blocks_here)
+    outer_first = jnp.where(at_outer, 0, jnp.where(column == inner_column, 1, column))
     if own_in_order:
         outer_first = jnp.where(group == 0, column - 1, outer_first)
     inside = group * blocks_here + outer_first
@@ -119,7 +115,8 @@
 
 
 def block_at(place, count, even):
-    return jnp.where(even[0] == 1, place, count - 1 - place)
+    first = jnp.where(even[0] == 1, 0, count - 1)
+    return jnp.where(place == 0, first, jnp.where(place == 1, count - 1 - first, place - 1))
 
 
 def lift_kernel(slots, even, *refs, piece_count):
@@ -154,35 +151,55 @@
 def layer_kernel(slots, counts, even, *refs, piece_count):
     pieces = refs[:piece_count]
     queries, mesh_in, gains, out_hbm, up_hbm, down_hbm, *rest = refs[piece_count:]
-    table, keys, values, mixed, out_weight, up_weight, down_weight, sems = rest[-8:]
-    parts = rest[:-8]
-    copies = fill_table(pieces, table, sems)
+    window, mixed, out_weight, up_weight, down_weight, sems, window_sems = rest[-7:]
+    parts = rest[:-7]
+    mesh_blocks, rows, width = mesh_in.shape
+    neighbours = window.shape[1] // rows
+
+    def place(slot, j):
+        return window.at[slot, pl.ds(j * rows, rows)]
+
+    def fetch(m, buffer):
+        source = block_at(m, mesh_blocks, even)
+        for j in range(neighbours):
+            slot = slots[source, j]
+            start = 0
+            for piece in pieces:
+                count = piece.shape[0]
+
+                @pl.when(jnp.logical_and(slot >= start, slot < start + count))
+                def _(piece=piece, start=start):
+                    pltpu.make_async_copy(
+                        piece.at[slot - start], place(buffer, j), window_sems.at[buffer, j]
+                    ).start()
+
+                start += count
+
+    fetch(0, 0)
     weights = [
-        pltpu.make_async_copy(out_hbm, out_weight, sems.at[piece_count]),
-        pltpu.make_async_copy(up_hbm, up_weight, sems.at[piece_count + 1]),
-        pltpu.make_async_copy(down_hbm, down_weight, sems.at[piece_count + 2]),
+        pltpu.make_async_copy(out_hbm, out_weight, sems.at[0]),
+        pltpu.make_async_copy(up_hbm, up_weight, sems.at[1]),
+        pltpu.make_async_copy(down_hbm, down_weight, sems.at[2]),
     ]
-    for copy in copies + weights:
+    for copy in weights:
         copy.start()
-    for copy in copies:
-        copy.wait()
-    mesh_blocks, rows, width = mesh_in.shape
-    neighbours = keys.shape[0] // rows
     head_size = width // HEADS
     wide = 2 * head_size
     certain = neighbours // 2 * rows
     low_half = lax.broadcasted_iota(jnp.int32, (rows, wide), 1) < head_size
     key_block = lax.broadcasted_iota(jnp.int32, (1, neighbours * rows - certain), 1) // rows + neighbours // 2
-    values[:, :, wide:] = jnp.ones((HEADS // 2, neighbours * rows, wide), jnp.bfloat16)
+    ones = jnp.ones((neighbours * rows, wide), jnp.bfloat16)
 
     def attend(m, carry):
         source = block_at(m, mesh_blocks, even)
+        buffer = lax.rem(m, 2)
         for j in range(neighbours):
-            slot = slots[source, j]
-            keys[j * rows:(j + 1) * rows, :] = table[slot, :, 0:width]
-            for h in range(HEADS // 2):
-                at = width + h * wide
-                values[h, j * rows:(j + 1) * rows, 0:wide] = table[slot, :, at:at + wide]
+            pltpu.make_async_copy(pieces[0].at[0], place(buffer, j), window_sems.at[buffer, j]).wait()
+
+        @pl.when(m + 1 < mesh_blocks)
+        def _():
+            fetch(m + 1, 1 - buffer)
+
         bias = jnp.where(key_block < counts[source], 0.0, -1e30)
 
         def score(h):
@@ -193,7 +210,7 @@
                 [jnp.where(low_half, query, none), jnp.where(low_half, none, query)], axis=0
             )
             return lax.dot_general(
-                pair_rows, keys[:, at:at + wide], (((1,), (1,)), ((), ())), preferred_element_type=jnp.float32
+                pair_rows, window[buffer, :, at:at + wide], (((1,), (1,)), ((), ())), preferred_element_type=jnp.float32
             )
 
         following = score(0)
@@ -210,7 +227,8 @@
                 [jnp.exp(first - highest).astype(jnp.bfloat16), jnp.exp(second - highest).astype(jnp.bfloat16)],
                 axis=1,
             )
-            summed = jnp.dot(raw, values[h], preferred_element_type=jnp.float32)
+            columns = jnp.concatenate([window[buffer, :, width + at:width + at + wide], ones], axis=1)
+            summed = jnp.dot(raw, columns, preferred_element_type=jnp.float32)
             part = summed[:, :wide] / summed[:, wide:]
             mixed[pl.ds(m * rows, rows), at:at + wide] = jnp.where(
                 low_half, part[:rows], part[rows:]
@@ -320,14 +338,13 @@
             in_specs=any_specs(len(kv_pieces)) + [VMEM_SPEC] * 3 + any_specs(3),
             out_specs=[VMEM_SPEC] * mesh_blocks,
             scratch_shapes=[
-                pltpu.VMEM((mesh_table, rows, 2 * width), bf16),
-                pltpu.VMEM((neighbours * rows, width), bf16),
-                pltpu.VMEM((HEADS // 2, neighbours * rows, 4 * (width // HEADS)), bf16),
+                pltpu.VMEM((2, neighbours * rows, 2 * width), bf16),
                 pltpu.VMEM((mesh_blocks * rows, width), bf16),
                 pltpu.VMEM((width, width), bf16),
                 pltpu.VMEM((width, hidden_width), bf16),
                 pltpu.VMEM((hidden_width, width), bf16),
-                pltpu.SemaphoreType.DMA((len(kv_pieces) + 3,)),
+                pltpu.SemaphoreType.DMA((3,)),
+                pltpu.SemaphoreType.DMA((2, neighbours)),
             ],
         ),
         out_shape=part_shapes,
@@ -376,6 +393,4 @@
         P("lat", "lon", None, None, None),
     )
 
-    return jax.shard_map(
-        shards, mesh=mesh, in_specs=placed, out_specs=P("lat", "lon", None, None), check_vma=False
-    )
+    return jax.shard_map(shards, mesh=mesh, in_specs=placed, out_specs=P("lat", "lon", None, None), check_vma=False)

time: 157 us -> 158 us (level)
  no operation moved by 1% of the time
where the time goes in v4:
time: 158 us; the launch traced here: 157 us
  waiting for transfers between devices  59.5 us (38%)
  starting transfers between devices  59.1 us (37%)
  Pallas kernels  20.8 us (13%)
  matrix products  10.2 us (6%)
  other arithmetic  6.62 us (4%)
    ppermute x31, waiting for transfers between devices, move(): return lax.ppermute(values, AXES, pairs)  59.5 us
    ppermute x31, starting transfers between devices, move(): return lax.ppermute(values, AXES, pairs)  59.1 us
    pallas_call x1, Pallas kernels, shards(): pl.pallas_call(lambda *refs: layer_kernel(*refs, piece_count=len(kv_piece...  15.2 us
    dot_general x4, matrix products, project(): jnp.dot(stacked.reshape(-1, width), kv_weight, preferred_element_type=f32)  7.31 us
  transfers between devices with their start and end apart: 31, of which 13 were waited for; matrix products, arithmetic and copies ran while one was open for 9% of the time, Pallas kernels for 0%

profile of v4, /device:TPU:1, one launch (start us, length us, event | category | flops | bytes accessed | tf_op | source)
XLA Modules:
  0.0 157.2 jit_solution(7870038545730762712)
XLA Ops:
  0.0 2.1 %fusion.11 = (f16[1,128,1024]{2,1,0:T(8,128)(2,1)S(1)}, f16[1,128,1024]{2,1,0:T(8,128)(2,1)}) fusion(f32[1,2,128,1024]{3,2,1,0:T(8,128)} %param.12, pred[]{:T(512)S(6)} %eq.125), kind=kLoop, calls=%fused_computation.38 | loop fusion | flops 786432 | bytes 1572865 | tf_op jit(solution)/shard_map/convert_element_type | solution.py:282
  2.1 3.7 %collective-permute-start = (f16[1,128,1024]{2,1,0:T(8,128)(2,1)}, f16[1,128,1024]{2,1,0:T(8,128)(2,1)S(1)}, u32[]{:S(2)}, u32[]{:S(2)}) collective-permute-start(f16[1,128,1024]{2,1,0:T(8,128)(2,1)} %get-tuple-element.20), channel_id=1, source_target_pairs={{0,16},{1,17},{2,18},{3,19},{4,20},{5,21},{6,22},{7,23},{8,24},{9,... | collective-permute-start | bytes 786440 | tf_op jit(solution)/shard_map/ppermute | solution.py:32
  5.8 1.6 %collective-permute-start.5 = (f16[1,128,1024]{2,1,0:T(8,128)(2,1)}, f16[1,128,1024]{2,1,0:T(8,128)(2,1)}, u32[]{:S(2)}, u32[]{:S(2)}) collective-permute-start(f16[1,128,1024]{2,1,0:T(8,128)(2,1)} %get-tuple-element.20), channel_id=1, source_target_pairs={{0,31},{1,18},{2,17},{3,20},{4,19},{5,22},{6,21},{7,24},{8,23},{9,... | collective-permute-start | bytes 786440 | tf_op jit(solution)/shard_map/ppermute | solution.py:32
  7.5 2.5 %collective-permute-start.1 = (f16[1,128,1024]{2,1,0:T(8,128)(2,1)S(1)}, f16[1,128,1024]{2,1,0:T(8,128)(2,1)S(1)}, u32[]{:S(2)}, u32[]{:S(2)}) collective-permute-start(f16[1,128,1024]{2,1,0:T(8,128)(2,1)S(1)} %get-tuple-element.19), channel_id=1, source_target_pairs={{0,16},{1,17},{2,18},{3,19},{4,20},{5,21},{6,22},{7,23},{8,24},{9,... | collective-permute-start | bytes 786440 | tf_op jit(solution)/shard_map/ppermute | solution.py:32
  10.0 0.7 broadcast_remainder_fusion
  10.7 0.7 sign_compare_fusion
  11.4 0.1 reduce-precision_convert_fusion
  11.5 0.7 fusion.26.refs_0_
  12.3 13.7 %collective-permute-done.1 = f16[1,128,1024]{2,1,0:T(8,128)(2,1)S(1)} collective-permute-done((f16[1,128,1024]{2,1,0:T(8,128)(2,1)S(1)}, f16[1,128,1024]{2,1,0:T(8,128)(2,1)S(1)}, u32[]{:S(2)}, u32[]{:S(2)}) %collective-permute-start.1) | collective-permute-done | bytes 262176 | tf_op jit(solution)/shard_map/ppermute | solution.py:32
  26.0 0.1 pad_maximum_fusion.5
  26.2 0.1 collective-permute-start.6
  26.3 3.7 %collective-permute-start.3 = (f16[1,128,1024]{2,1,0:T(8,128)(2,1)S(1)}, f16[1,128,1024]{2,1,0:T(8,128)(2,1)S(1)}, u32[]{:S(2)}, u32[]{:S(2)}) collective-permute-start(f16[1,128,1024]{2,1,0:T(8,128)(2,1)S(1)} %collective-permute-done.1), channel_id=1, source_target_pairs={{0,32},{1,33},{2,34},{3,35},{4,36},{5,37},{6,38},{7,39},{8,40},{9,... | collective-permute-start | bytes 786440 | tf_op jit(solution)/shard_map/ppermute | solution.py:32
  30.0 3.5 %collective-permute-start.2 = (f16[1,128,1024]{2,1,0:T(8,128)(2,1)S(1)}, f16[1,128,1024]{2,1,0:T(8,128)(2,1)S(1)}, u32[]{:S(2)}, u32[]{:S(2)}) collective-permute-start(f16[1,128,1024]{2,1,0:T(8,128)(2,1)S(1)} %collective-permute-done), channel_id=1, source_target_pairs={{0,32},{1,33},{2,34},{3,35},{4,36},{5,37},{6,38},{7,39},{8,40},{9,... | collective-permute-start | bytes 786440 | tf_op jit(solution)/shard_map/ppermute | solution.py:32
  33.6 1.0 convert_multiply_fusion.3.refs_8_
  34.7 0.5 collective-permute-done.3
  35.2 2.0 %collective-permute-start.8 = (f16[1,128,1024]{2,1,0:T(8,128)(2,1)S(1)}, f16[1,128,1024]{2,1,0:T(8,128)(2,1)S(1)}, u32[]{:S(2)}, u32[]{:S(2)}) collective-permute-start(f16[1,128,1024]{2,1,0:T(8,128)(2,1)S(1)} %collective-permute-done.3), channel_id=1, source_target_pairs={{0,1},{1,0},{2,3},{3,2},{4,5},{5,4},{6,7},{7,6},{8,9},{9,8},{10,11... | collective-permute-start | bytes 786440 | tf_op jit(solution)/shard_map/ppermute | solution.py:32
  37.3 3.5 %collective-permute-done.2 = f16[1,128,1024]{2,1,0:T(8,128)(2,1)S(1)} collective-permute-done((f16[1,128,1024]{2,1,0:T(8,128)(2,1)S(1)}, f16[1,128,1024]{2,1,0:T(8,128)(2,1)S(1)}, u32[]{:S(2)}, u32[]{:S(2)}) %collective-permute-start.2) | collective-permute-done | bytes 262176 | tf_op jit(solution)/shard_map/ppermute | solution.py:32
  40.8 3.4 %collective-permute-start.7 = (f16[1,128,1024]{2,1,0:T(8,128)(2,1)S(1)}, f16[1,128,1024]{2,1,0:T(8,128)(2,1)S(1)}, u32[]{:S(2)}, u32[]{:S(2)}) collective-permute-start(f16[1,128,1024]{2,1,0:T(8,128)(2,1)S(1)} %collective-permute-done.2), channel_id=1, source_target_pairs={{0,15},{1,2},{2,1},{3,4},{4,3},{5,6},{6,5},{7,8},{8,7},{9,10},{10,... | collective-permute-start | bytes 786440 | tf_op jit(solution)/shard_map/ppermute | solution.py:32
  44.4 0.1 convert_multiply_fusion.refs_9_
  44.5 6.6 %collective-permute-done.7 = f16[1,128,1024]{2,1,0:T(8,128)(2,1)S(1)} collective-permute-done((f16[1,128,1024]{2,1,0:T(8,128)(2,1)S(1)}, f16[1,128,1024]{2,1,0:T(8,128)(2,1)S(1)}, u32[]{:S(2)}, u32[]{:S(2)}) %collective-permute-start.7) | collective-permute-done | bytes 262176 | tf_op jit(solution)/shard_map/ppermute | solution.py:32
  51.2 2.9 %lift.1 = (f32[3,128,1024]{2,1,0:T(8,128)S(1)}, bf16[1,128,1024]{2,1,0:T(8,128)(2,1)S(1)}, bf16[1,128,1024]{2,1,0:T(8,128)(2,1)S(1)}, bf16[1,128,1024]{2,1,0:T(8,128)(2,1)S(1)}) custom-call(s32[3,4]{1,0:T(4,128)S(1)} %fusion.26.refs_0_, s32[1]{0:T(128)} %bitcast.4.refs_1_.refs_2_, f32[2,128,1024]{2,1,0:T(8,128)S(1)} %bitcast.113, ...), custom_call_target="tpu_custom_call" | custom-call | tf_op jit(solution)/shard_map/lift/pallas_call | solution.py:292
  54.1 2.7 %collective-permute-start.9 = (bf16[1,128,1024]{2,1,0:T(8,128)(2,1)S(1)}, bf16[1,128,1024]{2,1,0:T(8,128)(2,1)S(1)}, u32[]{:S(2)}, u32[]{:S(2)}) collective-permute-start(bf16[1,128,1024]{2,1,0:T(8,128)(2,1)S(1)} %get-tuple-element.12), channel_id=1, source_target_pairs={{0,16},{1,17},{2,18},{3,19},{4,20},{5,21},{6,22},{7,23},{8,24},{9,... | collective-permute-start | bytes 786440 | tf_op jit(solution)/shard_map/ppermute | solution.py:32
  56.8 1.3 collective-permute-start.15
  58.1 0.5 collective-permute-start.16
  58.6 1.8 %collective-permute-start.10 = (bf16[1,128,1024]{2,1,0:T(8,128)(2,1)S(1)}, bf16[1,128,1024]{2,1,0:T(8,128)(2,1)S(1)}, u32[]{:S(2)}, u32[]{:S(2)}) collective-permute-start(bf16[1,128,1024]{2,1,0:T(8,128)(2,1)S(1)} %get-tuple-element.13), channel_id=1, source_target_pairs={{0,16},{1,17},{2,18},{3,19},{4,20},{5,21},{6,22},{7,23},{8,24},{9,... | collective-permute-start | bytes 786440 | tf_op jit(solution)/shard_map/ppermute | solution.py:32
  60.4 1.2 collective-permute-start.11
  61.6 0.1 pad_maximum_fusion.2
  61.7 2.9 %convolution_convert_fusion = bf16[384,3072]{1,0:T(8,128)(2,1)S(1)} fusion(bf16[384,1024]{1,0:T(8,128)(2,1)S(1)} %bitcast.122, bf16[1024,3072]{1,0:T(8,128)(2,1)S(1)} %bitcast.126), kind=kOutput, calls=%fused_computation | convolution fusion | flops 2417098752 | bytes 9437184 | tf_op jit(solution)/shard_map/dot_general | solution.py:314
  64.6 0.1 slice.24
  64.8 4.3 %collective-permute-done.9 = bf16[1,128,1024]{2,1,0:T(8,128)(2,1)S(1)} collective-permute-done((bf16[1,128,1024]{2,1,0:T(8,128)(2,1)S(1)}, bf16[1,128,1024]{2,1,0:T(8,128)(2,1)S(1)}, u32[]{:S(2)}, u32[]{:S(2)}) %collective-permute-start.9) | collective-permute-done | bytes 262176 | tf_op jit(solution)/shard_map/ppermute | solution.py:32
  69.1 4.7 %collective-permute-start.12 = (bf16[1,128,1024]{2,1,0:T(8,128)(2,1)S(1)}, bf16[1,128,1024]{2,1,0:T(8,128)(2,1)S(1)}, u32[]{:S(2)}, u32[]{:S(2)}) collective-permute-start(bf16[1,128,1024]{2,1,0:T(8,128)(2,1)S(1)} %collective-permute-done.9), channel_id=1, source_target_pairs={{0,32},{1,33},{2,34},{3,35},{4,36},{5,37},{6,38},{7,39},{8,40},{9,... | collective-permute-start | bytes 786440 | tf_op jit(solution)/shard_map/ppermute | solution.py:32
  73.8 6.2 %collective-permute-done.10 = bf16[1,128,1024]{2,1,0:T(8,128)(2,1)S(1)} collective-permute-done((bf16[1,128,1024]{2,1,0:T(8,128)(2,1)S(1)}, bf16[1,128,1024]{2,1,0:T(8,128)(2,1)S(1)}, u32[]{:S(2)}, u32[]{:S(2)}) %collective-permute-start.10) | collective-permute-done | bytes 262176 | tf_op jit(solution)/shard_map/ppermute | solution.py:32
  80.0 4.6 %collective-permute-start.13 = (bf16[1,128,1024]{2,1,0:T(8,128)(2,1)S(1)}, bf16[1,128,1024]{2,1,0:T(8,128)(2,1)S(1)}, u32[]{:S(2)}, u32[]{:S(2)}) collective-permute-start(bf16[1,128,1024]{2,1,0:T(8,128)(2,1)S(1)} %collective-permute-done.10), channel_id=1, source_target_pairs={{0,32},{1,33},{2,34},{3,35},{4,36},{5,37},{6,38},{7,39},{8,40},{9,... | collective-permute-start | bytes 786440 | tf_op jit(solution)/shard_map/ppermute | solution.py:32
  84.6 3.3 %collective-permute-start.14 = (bf16[1,128,1024]{2,1,0:T(8,128)(2,1)S(1)}, bf16[1,128,1024]{2,1,0:T(8,128)(2,1)S(1)}, u32[]{:S(2)}, u32[]{:S(2)}) collective-permute-start(bf16[1,128,1024]{2,1,0:T(8,128)(2,1)S(1)} %collective-permute-done.11), channel_id=1, source_target_pairs={{0,32},{1,33},{2,34},{3,35},{4,36},{5,37},{6,38},{7,39},{8,40},{9,... | collective-permute-start | bytes 786440 | tf_op jit(solution)/shard_map/ppermute | solution.py:32
  87.9 0.1 pad_maximum_fusion.3
  88.0 1.8 %convolution_convert_fusion.3 = bf16[384,2048]{1,0:T(8,128)(2,1)S(1)} fusion(bf16[384,1024]{1,0:T(8,128)(2,1)S(1)} %bitcast.123, bf16[1024,3072]{1,0:T(8,128)(2,1)S(1)} %bitcast.126), kind=kOutput, calls=%fused_computation.3 | convolution fusion | flops 1611399168 | bytes 6553600 | tf_op jit(solution)/shard_map/dot_general | solution.py:322
  89.9 0.1 collective-permute-start.17
  90.0 0.1 collective-permute-start.18
  90.1 3.4 %collective-permute-done.14 = bf16[1,128,1024]{2,1,0:T(8,128)(2,1)S(1)} collective-permute-done((bf16[1,128,1024]{2,1,0:T(8,128)(2,1)S(1)}, bf16[1,128,1024]{2,1,0:T(8,128)(2,1)S(1)}, u32[]{:S(2)}, u32[]{:S(2)}) %collective-permute-start.14) | collective-permute-done | bytes 262176 | tf_op jit(solution)/shard_map/ppermute | solution.py:32
  93.5 0.6 collective-permute-start.19
  94.1 0.1 pad_maximum_fusion.4
  94.1 1.8 %convolution_convert_fusion.2 = bf16[384,2048]{1,0:T(8,128)(2,1)S(1)} fusion(bf16[384,1024]{1,0:T(8,128)(2,1)S(1)} %bitcast.121, bf16[1024,3072]{1,0:T(8,128)(2,1)S(1)} %bitcast.126), kind=kOutput, calls=%fused_computation.2 | convolution fusion | flops 1611399168 | bytes 6553600 | tf_op jit(solution)/shard_map/dot_general | solution.py:322
  96.0 0.1 pad_maximum_fusion
  96.1 2.4 %convolution_convert_fusion.1 = bf16[512,2048]{1,0:T(8,128)(2,1)S(1)} fusion(bf16[512,1024]{1,0:T(8,128)(2,1)S(1)} %bitcast.120, bf16[1024,3072]{1,0:T(8,128)(2,1)S(1)} %bitcast.126), kind=kOutput, calls=%fused_computation.1 | convolution fusion | flops 2148532224 | bytes 7340032 | tf_op jit(solution)/shard_map/dot_general | solution.py:322
  98.5 0.2 collective-permute-done.18
  98.8 1.3 fusion.5
  100.1 15.2 %layer.1 = (bf16[1,128,1024]{2,1,0:T(8,128)(2,1)S(1)}, bf16[1,128,1024]{2,1,0:T(8,128)(2,1)S(1)}, bf16[1,128,1024]{2,1,0:T(8,128)(2,1)S(1)}) custom-call(s32[3,8]{1,0:T(4,128)S(1)} %fusion.22.refs_0_, s32[3]{0:T(128)S(1)} %bitcast.119, s32[1]{0:T(128)} %bitcast.4.refs_1_.refs_2_, bf16[3,128,2048]{2,1,0:T(8,128)(2,1)S(1)} %bitcast.112, ...), custom_call_target="tpu_custom_call" | custom-call | tf_op jit(solution)/shard_map/layer/pallas_call | solution.py:334
  115.3 0.5 collective-permute-start.20
  115.8 2.6 %collective-permute-start.21 = (bf16[1,128,1024]{2,1,0:T(8,128)(2,1)S(1)}, bf16[1,128,1024]{2,1,0:T(8,128)(2,1)S(1)}, u32[]{:S(2)}, u32[]{:S(2)}) collective-permute-start(bf16[1,128,1024]{2,1,0:T(8,128)(2,1)S(1)} %get-tuple-element.17.refs_2_), channel_id=1, source_target_pairs={{0,16},{1,17},{2,18},{3,19},{4,20},{5,21},{6,22},{7,23},{8,24},{9,... | collective-permute-start | bytes 786440 | tf_op jit(solution)/shard_map/ppermute | solution.py:32
  118.4 0.6 collective-permute-start.26
  118.9 0.4 collective-permute-start.22
  119.3 8.4 %collective-permute-done.20.refs_4_ = bf16[1,128,1024]{2,1,0:T(8,128)(2,1)S(1)} collective-permute-done((bf16[1,128,1024]{2,1,0:T(8,128)(2,1)S(1)}, bf16[1,128,1024]{2,1,0:T(8,128)(2,1)S(1)}, u32[]{:S(2)}, u32[]{:S(2)}) %collective-permute-start.20) | collective-permute-done | bytes 262176 | tf_op jit(solution)/shard_map/ppermute | solution.py:32
  127.7 3.9 %collective-permute-start.23 = (bf16[1,128,1024]{2,1,0:T(8,128)(2,1)S(1)}, bf16[1,128,1024]{2,1,0:T(8,128)(2,1)S(1)}, u32[]{:S(2)}, u32[]{:S(2)}) collective-permute-start(bf16[1,128,1024]{2,1,0:T(8,128)(2,1)S(1)} %collective-permute-done.20.refs_4_), channel_id=1, source_target_pairs={{0,32},{1,33},{2,34},{3,35},{4,36},{5,37},{6,38},{7,39},{8,40},{9,... | collective-permute-start | bytes 786440 | tf_op jit(solution)/shard_map/ppermute | solution.py:32
  131.6 1.7 %collective-permute-done.21.refs_5_ = bf16[1,128,1024]{2,1,0:T(8,128)(2,1)S(1)} collective-permute-done((bf16[1,128,1024]{2,1,0:T(8,128)(2,1)S(1)}, bf16[1,128,1024]{2,1,0:T(8,128)(2,1)S(1)}, u32[]{:S(2)}, u32[]{:S(2)}) %collective-permute-start.21) | collective-permute-done | bytes 262176 | tf_op jit(solution)/shard_map/ppermute | solution.py:32
  133.4 3.9 %collective-permute-start.24 = (bf16[1,128,1024]{2,1,0:T(8,128)(2,1)S(1)}, bf16[1,128,1024]{2,1,0:T(8,128)(2,1)S(1)}, u32[]{:S(2)}, u32[]{:S(2)}) collective-permute-start(bf16[1,128,1024]{2,1,0:T(8,128)(2,1)S(1)} %collective-permute-done.21.refs_5_), channel_id=1, source_target_pairs={{0,32},{1,33},{2,34},{3,35},{4,36},{5,37},{6,38},{7,39},{8,40},{9,... | collective-permute-start | bytes 786440 | tf_op jit(solution)/shard_map/ppermute | solution.py:32
  137.3 1.2 collective-permute-start.28
  138.5 0.1 reduce-precision_convert_fusion.1
  138.6 3.2 %collective-permute-done.22.refs_6_ = bf16[1,128,1024]{2,1,0:T(8,128)(2,1)S(1)} collective-permute-done((bf16[1,128,1024]{2,1,0:T(8,128)(2,1)S(1)}, bf16[1,128,1024]{2,1,0:T(8,128)(2,1)S(1)}, u32[]{:S(2)}, u32[]{:S(2)}) %collective-permute-start.22) | collective-permute-done | bytes 262176 | tf_op jit(solution)/shard_map/ppermute | solution.py:32
  141.8 3.8 %collective-permute-start.25 = (bf16[1,128,1024]{2,1,0:T(8,128)(2,1)S(1)}, bf16[1,128,1024]{2,1,0:T(8,128)(2,1)S(1)}, u32[]{:S(2)}, u32[]{:S(2)}) collective-permute-start(bf16[1,128,1024]{2,1,0:T(8,128)(2,1)S(1)} %collective-permute-done.22.refs_6_), channel_id=1, source_target_pairs={{0,32},{1,33},{2,34},{3,35},{4,36},{5,37},{6,38},{7,39},{8,40},{9,... | collective-permute-start | bytes 786440 | tf_op jit(solution)/shard_map/ppermute | solution.py:32
  145.6 0.3 collective-permute-start.29
  145.9 0.6 collective-permute-start.30
  146.6 4.9 %collective-permute-done.27.refs_11_ = bf16[1,128,1024]{2,1,0:T(8,128)(2,1)S(1)} collective-permute-done((bf16[1,128,1024]{2,1,0:T(8,128)(2,1)S(1)}, bf16[1,128,1024]{2,1,0:T(8,128)(2,1)S(1)}, u32[]{:S(2)}, u32[]{:S(2)}) %collective-permute-start.27) | collective-permute-done | bytes 262176 | tf_op jit(solution)/shard_map/ppermute | solution.py:32
  151.5 2.8 %collective-permute-done.29.refs_13_ = bf16[1,128,1024]{2,1,0:T(8,128)(2,1)S(1)} collective-permute-done((bf16[1,128,1024]{2,1,0:T(8,128)(2,1)S(1)}, bf16[1,128,1024]{2,1,0:T(8,128)(2,1)S(1)}, u32[]{:S(2)}, u32[]{:S(2)}) %collective-permute-start.29) | collective-permute-done | bytes 262176 | tf_op jit(solution)/shard_map/ppermute | solution.py:32
  154.3 2.7 %give_back.1 = f32[2,128,1024]{2,1,0:T(8,128)} custom-call(s32[2,4]{1,0:T(2,128)S(1)} %and_select_fusion.refs_0_, bf16[1,128,1024]{2,1,0:T(8,128)(2,1)S(1)} %get-tuple-element.16.refs_1_, bf16[1,128,1024]{2,1,0:T(8,128)(2,1)S(1)} %get-tuple-element.17.refs_2_, bf16[1,128,1024]{2,1,0:T(8,128)(2,1)S(1)} %get-tuple-element.18.refs_3_, ...), custom_call_target="tpu_custom_call" | custom-call | tf_op jit(solution)/shard_map/give_back/pallas_call | solution.py:361
  (52 shorter events, 0.8 us)
Async XLA Ops:
  0.0 11.4 %copy-start = (f32[1,3,4,128,128]{4,3,2,1,0:T(8,128)S(1)}, f32[1,3,4,128,128]{4,3,2,1,0:T(8,128)}, u32[]{:S(2)}) copy-start(f32[1,3,4,128,128]{4,3,2,1,0:T(8,128)} %param.14) | copy-start | bytes 2359300
  2.1 27.9 %collective-permute-start = (f16[1,128,1024]{2,1,0:T(8,128)(2,1)}, f16[1,128,1024]{2,1,0:T(8,128)(2,1)S(1)}, u32[]{:S(2)}, u32[]{:S(2)}) collective-permute-start(f16[1,128,1024]{2,1,0:T(8,128)(2,1)} %get-tuple-element.20), channel_id=1, source_target_pairs={{0,16},{1,17},{2,18},{3,19},{4,20},{5,21},{6,22},{7,23},{8,24},{9,... | collective-permute-start | bytes 786440 | tf_op jit(solution)/shard_map/ppermute | solution.py:32
  5.8 27.8 %collective-permute-start.5 = (f16[1,128,1024]{2,1,0:T(8,128)(2,1)}, f16[1,128,1024]{2,1,0:T(8,128)(2,1)}, u32[]{:S(2)}, u32[]{:S(2)}) collective-permute-start(f16[1,128,1024]{2,1,0:T(8,128)(2,1)} %get-tuple-element.20), channel_id=1, source_target_pairs={{0,31},{1,18},{2,17},{3,20},{4,19},{5,22},{6,21},{7,24},{8,23},{9,... | collective-permute-start | bytes 786440 | tf_op jit(solution)/shard_map/ppermute | solution.py:32
  7.5 27.2 %collective-permute-start.4 = (f16[1,128,1024]{2,1,0:T(8,128)(2,1)}, f16[1,128,1024]{2,1,0:T(8,128)(2,1)S(1)}, u32[]{:S(2)}, u32[]{:S(2)}) collective-permute-start(f16[1,128,1024]{2,1,0:T(8,128)(2,1)} %get-tuple-element.20), channel_id=1, source_target_pairs={{0,15},{1,2},{2,1},{3,4},{4,3},{5,6},{6,5},{7,8},{8,7},{9,10},{10,... | collective-permute-start | bytes 786440 | tf_op jit(solution)/shard_map/ppermute | solution.py:32
  7.5 18.6 %collective-permute-start.1 = (f16[1,128,1024]{2,1,0:T(8,128)(2,1)S(1)}, f16[1,128,1024]{2,1,0:T(8,128)(2,1)S(1)}, u32[]{:S(2)}, u32[]{:S(2)}) collective-permute-start(f16[1,128,1024]{2,1,0:T(8,128)(2,1)S(1)} %get-tuple-element.19), channel_id=1, source_target_pairs={{0,16},{1,17},{2,18},{3,19},{4,20},{5,21},{6,22},{7,23},{8,24},{9,... | collective-permute-start | bytes 786440 | tf_op jit(solution)/shard_map/ppermute | solution.py:32
  26.2 25.0 %copy-start.1 = (f32[1,2,128,1024]{3,2,1,0:T(8,128)S(1)}, f32[1,2,128,1024]{3,2,1,0:T(8,128)}, u32[]{:S(2)}) copy-start(f32[1,2,128,1024]{3,2,1,0:T(8,128)} %param.12) | copy-start | bytes 3145732
  26.2 25.0 %copy-start.2 = (f32[2,1024]{1,0:T(2,128)S(1)}, f32[2,1024]{1,0:T(2,128)}, u32[]{:S(2)}) copy-start(f32[2,1024]{1,0:T(2,128)} %refs_10_.1) | copy-start | bytes 24580
  26.2 18.2 %collective-permute-start.6 = (f16[2,128,1024]{2,1,0:T(8,128)(2,1)S(1)}, f16[2,128,1024]{2,1,0:T(8,128)(2,1)S(1)}, u32[]{:S(2)}, u32[]{:S(2)}) collective-permute-start(f16[2,128,1024]{2,1,0:T(8,128)(2,1)S(1)} %pad_maximum_fusion.5), channel_id=1, source_target_pairs={{0,1},{1,0},{2,3},{3,2},{4,5},{5,4},{6,7},{7,6},{8,9},{9,8},{10,11... | collective-permute-start | bytes 1572872 | tf_op jit(solution)/shard_map/ppermute | solution.py:32
  26.3 8.9 %collective-permute-start.3 = (f16[1,128,1024]{2,1,0:T(8,128)(2,1)S(1)}, f16[1,128,1024]{2,1,0:T(8,128)(2,1)S(1)}, u32[]{:S(2)}, u32[]{:S(2)}) collective-permute-start(f16[1,128,1024]{2,1,0:T(8,128)(2,1)S(1)} %collective-permute-done.1), channel_id=1, source_target_pairs={{0,32},{1,33},{2,34},{3,35},{4,36},{5,37},{6,38},{7,39},{8,40},{9,... | collective-permute-start | bytes 786440 | tf_op jit(solution)/shard_map/ppermute | solution.py:32
  30.0 10.8 %collective-permute-start.2 = (f16[1,128,1024]{2,1,0:T(8,128)(2,1)S(1)}, f16[1,128,1024]{2,1,0:T(8,128)(2,1)S(1)}, u32[]{:S(2)}, u32[]{:S(2)}) collective-permute-start(f16[1,128,1024]{2,1,0:T(8,128)(2,1)S(1)} %collective-permute-done), channel_id=1, source_target_pairs={{0,32},{1,33},{2,34},{3,35},{4,36},{5,37},{6,38},{7,39},{8,40},{9,... | collective-permute-start | bytes 786440 | tf_op jit(solution)/shard_map/ppermute | solution.py:32
  35.2 9.1 %collective-permute-start.8 = (f16[1,128,1024]{2,1,0:T(8,128)(2,1)S(1)}, f16[1,128,1024]{2,1,0:T(8,128)(2,1)S(1)}, u32[]{:S(2)}, u32[]{:S(2)}) collective-permute-start(f16[1,128,1024]{2,1,0:T(8,128)(2,1)S(1)} %collective-permute-done.3), channel_id=1, source_target_pairs={{0,1},{1,0},{2,3},{3,2},{4,5},{5,4},{6,7},{7,6},{8,9},{9,8},{10,11... | collective-permute-start | bytes 786440 | tf_op jit(solution)/shard_map/ppermute | solution.py:32
  40.8 10.3 %collective-permute-start.7 = (f16[1,128,1024]{2,1,0:T(8,128)(2,1)S(1)}, f16[1,128,1024]{2,1,0:T(8,128)(2,1)S(1)}, u32[]{:S(2)}, u32[]{:S(2)}) collective-permute-start(f16[1,128,1024]{2,1,0:T(8,128)(2,1)S(1)} %collective-permute-done.2), channel_id=1, source_target_pairs={{0,15},{1,2},{2,1},{3,4},{4,3},{5,6},{6,5},{7,8},{8,7},{9,10},{10,... | collective-permute-start | bytes 786440 | tf_op jit(solution)/shard_map/ppermute | solution.py:32
  44.3 17.4 %slice-start = ((s8[6291456]{0:T(1024)(128)(4,1)}), s8[4194304]{0:T(1024)(128)(4,1)S(1)}, s32[]{:S(2)}) async-start(s8[6291456]{0:T(1024)(128)(4,1)} %bitcast.125), calls=%async_computation | async-start | bytes 8388608
  51.2 10.5 %slice-start.1 = ((s8[6291456]{0:T(1024)(128)(4,1)}), s8[2097152]{0:T(1024)(128)(4,1)S(1)}, s32[]{:S(2)}) async-start(s8[6291456]{0:T(1024)(128)(4,1)} %bitcast.125), calls=%async_computation.1 | async-start | bytes 4194304
  54.1 15.0 %collective-permute-start.9 = (bf16[1,128,1024]{2,1,0:T(8,128)(2,1)S(1)}, bf16[1,128,1024]{2,1,0:T(8,128)(2,1)S(1)}, u32[]{:S(2)}, u32[]{:S(2)}) collective-permute-start(bf16[1,128,1024]{2,1,0:T(8,128)(2,1)S(1)} %get-tuple-element.12), channel_id=1, source_target_pairs={{0,16},{1,17},{2,18},{3,19},{4,20},{5,21},{6,22},{7,23},{8,24},{9,... | collective-permute-start | bytes 786440 | tf_op jit(solution)/shard_map/ppermute | solution.py:32
  56.8 39.1 %collective-permute-start.15 = (bf16[1,128,1024]{2,1,0:T(8,128)(2,1)S(1)}, bf16[1,128,1024]{2,1,0:T(8,128)(2,1)S(1)}, u32[]{:S(2)}, u32[]{:S(2)}) collective-permute-start(bf16[1,128,1024]{2,1,0:T(8,128)(2,1)S(1)} %get-tuple-element.12), channel_id=1, source_target_pairs={{0,15},{1,2},{2,1},{3,4},{4,3},{5,6},{6,5},{7,8},{8,7},{9,10},{10,... | collective-permute-start | bytes 786440 | tf_op jit(solution)/shard_map/ppermute | solution.py:32
  58.1 37.9 %collective-permute-start.16 = (bf16[1,128,1024]{2,1,0:T(8,128)(2,1)S(1)}, bf16[1,128,1024]{2,1,0:T(8,128)(2,1)S(1)}, u32[]{:S(2)}, u32[]{:S(2)}) collective-permute-start(bf16[1,128,1024]{2,1,0:T(8,128)(2,1)S(1)} %get-tuple-element.12), channel_id=1, source_target_pairs={{0,31},{1,18},{2,17},{3,20},{4,19},{5,22},{6,21},{7,24},{8,23},{9,... | collective-permute-start | bytes 786440 | tf_op jit(solution)/shard_map/ppermute | solution.py:32
  58.6 21.3 %collective-permute-start.10 = (bf16[1,128,1024]{2,1,0:T(8,128)(2,1)S(1)}, bf16[1,128,1024]{2,1,0:T(8,128)(2,1)S(1)}, u32[]{:S(2)}, u32[]{:S(2)}) collective-permute-start(bf16[1,128,1024]{2,1,0:T(8,128)(2,1)S(1)} %get-tuple-element.13), channel_id=1, source_target_pairs={{0,16},{1,17},{2,18},{3,19},{4,20},{5,21},{6,22},{7,23},{8,24},{9,... | collective-permute-start | bytes 786440 | tf_op jit(solution)/shard_map/ppermute | solution.py:32
  60.4 24.2 %collective-permute-start.11 = (bf16[1,128,1024]{2,1,0:T(8,128)(2,1)S(1)}, bf16[1,128,1024]{2,1,0:T(8,128)(2,1)S(1)}, u32[]{:S(2)}, u32[]{:S(2)}) collective-permute-start(bf16[1,128,1024]{2,1,0:T(8,128)(2,1)S(1)} %get-tuple-element.14), channel_id=1, source_target_pairs={{0,16},{1,17},{2,18},{3,19},{4,20},{5,21},{6,22},{7,23},{8,24},{9,... | collective-permute-start | bytes 786440 | tf_op jit(solution)/shard_map/ppermute | solution.py:32
  69.1 20.8 %collective-permute-start.12 = (bf16[1,128,1024]{2,1,0:T(8,128)(2,1)S(1)}, bf16[1,128,1024]{2,1,0:T(8,128)(2,1)S(1)}, u32[]{:S(2)}, u32[]{:S(2)}) collective-permute-start(bf16[1,128,1024]{2,1,0:T(8,128)(2,1)S(1)} %collective-permute-done.9), channel_id=1, source_target_pairs={{0,32},{1,33},{2,34},{3,35},{4,36},{5,37},{6,38},{7,39},{8,40},{9,... | collective-permute-start | bytes 786440 | tf_op jit(solution)/shard_map/ppermute | solution.py:32
  80.0 10.0 %collective-permute-start.13 = (bf16[1,128,1024]{2,1,0:T(8,128)(2,1)S(1)}, bf16[1,128,1024]{2,1,0:T(8,128)(2,1)S(1)}, u32[]{:S(2)}, u32[]{:S(2)}) collective-permute-start(bf16[1,128,1024]{2,1,0:T(8,128)(2,1)S(1)} %collective-permute-done.10), channel_id=1, source_target_pairs={{0,32},{1,33},{2,34},{3,35},{4,36},{5,37},{6,38},{7,39},{8,40},{9,... | collective-permute-start | bytes 786440 | tf_op jit(solution)/shard_map/ppermute | solution.py:32
  84.6 8.9 %collective-permute-start.14 = (bf16[1,128,1024]{2,1,0:T(8,128)(2,1)S(1)}, bf16[1,128,1024]{2,1,0:T(8,128)(2,1)S(1)}, u32[]{:S(2)}, u32[]{:S(2)}) collective-permute-start(bf16[1,128,1024]{2,1,0:T(8,128)(2,1)S(1)} %collective-permute-done.11), channel_id=1, source_target_pairs={{0,32},{1,33},{2,34},{3,35},{4,36},{5,37},{6,38},{7,39},{8,40},{9,... | collective-permute-start | bytes 786440 | tf_op jit(solution)/shard_map/ppermute | solution.py:32
  89.9 6.1 %collective-permute-start.17 = (bf16[2,128,1024]{2,1,0:T(8,128)(2,1)S(1)}, bf16[2,128,1024]{2,1,0:T(8,128)(2,1)S(1)}, u32[]{:S(2)}, u32[]{:S(2)}) collective-permute-start(bf16[2,128,1024]{2,1,0:T(8,128)(2,1)S(1)} %pad_maximum_fusion.6), channel_id=1, source_target_pairs={{0,1},{1,0},{2,3},{3,2},{4,5},{5,4},{6,7},{7,6},{8,9},{9,8},{10,11... | collective-permute-start | bytes 1572872 | tf_op jit(solution)/shard_map/ppermute | solution.py:32
  90.0 8.7 %collective-permute-start.18 = (bf16[1,128,1024]{2,1,0:T(8,128)(2,1)S(1)}, bf16[1,128,1024]{2,1,0:T(8,128)(2,1)S(1)}, u32[]{:S(2)}, u32[]{:S(2)}) collective-permute-start(bf16[1,128,1024]{2,1,0:T(8,128)(2,1)S(1)} %collective-permute-done.12), channel_id=1, source_target_pairs={{0,15},{1,2},{2,1},{3,4},{4,3},{5,6},{6,5},{7,8},{8,7},{9,10},{10,... | collective-permute-start | bytes 786440 | tf_op jit(solution)/shard_map/ppermute | solution.py:32
  93.5 5.2 %collective-permute-start.19 = (bf16[1,128,1024]{2,1,0:T(8,128)(2,1)S(1)}, bf16[1,128,1024]{2,1,0:T(8,128)(2,1)S(1)}, u32[]{:S(2)}, u32[]{:S(2)}) collective-permute-start(bf16[1,128,1024]{2,1,0:T(8,128)(2,1)S(1)} %collective-permute-done.13), channel_id=1, source_target_pairs={{0,1},{1,0},{2,3},{3,2},{4,5},{5,4},{6,7},{7,6},{8,9},{9,8},{10,11... | collective-permute-start | bytes 786440 | tf_op jit(solution)/shard_map/ppermute | solution.py:32
  98.7 1.3 copy-start.3
  100.1 38.4 %copy-start.4 = (f32[1,2,4,128,128]{4,3,2,1,0:T(8,128)S(1)}, f32[1,2,4,128,128]{4,3,2,1,0:T(8,128)}, u32[]{:S(2)}) copy-start(f32[1,2,4,128,128]{4,3,2,1,0:T(8,128)} %param.23) | copy-start | bytes 1572868
  100.1 46.5 %copy-start.5 = (s32[1,2,4]{2,1,0:T(2,128)S(1)}, s32[1,2,4]{2,1,0:T(2,128)}, u32[]{:S(2)}) copy-start(s32[1,2,4]{2,1,0:T(2,128)} %param.22) | copy-start | bytes 100
  115.3 12.4 %collective-permute-start.20 = (bf16[1,128,1024]{2,1,0:T(8,128)(2,1)S(1)}, bf16[1,128,1024]{2,1,0:T(8,128)(2,1)S(1)}, u32[]{:S(2)}, u32[]{:S(2)}) collective-permute-start(bf16[1,128,1024]{2,1,0:T(8,128)(2,1)S(1)} %get-tuple-element.16.refs_1_), channel_id=1, source_target_pairs={{0,16},{1,17},{2,18},{3,19},{4,20},{5,21},{6,22},{7,23},{8,24},{9,... | collective-permute-start | bytes 786440 | tf_op jit(solution)/shard_map/ppermute | solution.py:32
  115.8 17.6 %collective-permute-start.21 = (bf16[1,128,1024]{2,1,0:T(8,128)(2,1)S(1)}, bf16[1,128,1024]{2,1,0:T(8,128)(2,1)S(1)}, u32[]{:S(2)}, u32[]{:S(2)}) collective-permute-start(bf16[1,128,1024]{2,1,0:T(8,128)(2,1)S(1)} %get-tuple-element.17.refs_2_), channel_id=1, source_target_pairs={{0,16},{1,17},{2,18},{3,19},{4,20},{5,21},{6,22},{7,23},{8,24},{9,... | collective-permute-start | bytes 786440 | tf_op jit(solution)/shard_map/ppermute | solution.py:32
  118.4 23.4 %collective-permute-start.26 = (bf16[1,128,1024]{2,1,0:T(8,128)(2,1)S(1)}, bf16[1,128,1024]{2,1,0:T(8,128)(2,1)S(1)}, u32[]{:S(2)}, u32[]{:S(2)}) collective-permute-start(bf16[1,128,1024]{2,1,0:T(8,128)(2,1)S(1)} %get-tuple-element.16.refs_1_), channel_id=1, source_target_pairs={{0,15},{1,2},{2,1},{3,4},{4,3},{5,6},{6,5},{7,8},{8,7},{9,10},{10,... | collective-permute-start | bytes 786440 | tf_op jit(solution)/shard_map/ppermute | solution.py:32
  118.9 22.9 %collective-permute-start.22 = (bf16[1,128,1024]{2,1,0:T(8,128)(2,1)S(1)}, bf16[1,128,1024]{2,1,0:T(8,128)(2,1)S(1)}, u32[]{:S(2)}, u32[]{:S(2)}) collective-permute-start(bf16[1,128,1024]{2,1,0:T(8,128)(2,1)S(1)} %get-tuple-element.18.refs_3_), channel_id=1, source_target_pairs={{0,16},{1,17},{2,18},{3,19},{4,20},{5,21},{6,22},{7,23},{8,24},{9,... | collective-permute-start | bytes 786440 | tf_op jit(solution)/shard_map/ppermute | solution.py:32
  127.7 17.9 %collective-permute-start.23 = (bf16[1,128,1024]{2,1,0:T(8,128)(2,1)S(1)}, bf16[1,128,1024]{2,1,0:T(8,128)(2,1)S(1)}, u32[]{:S(2)}, u32[]{:S(2)}) collective-permute-start(bf16[1,128,1024]{2,1,0:T(8,128)(2,1)S(1)} %collective-permute-done.20.refs_4_), channel_id=1, source_target_pairs={{0,32},{1,33},{2,34},{3,35},{4,36},{5,37},{6,38},{7,39},{8,40},{9,... | collective-permute-start | bytes 786440 | tf_op jit(solution)/shard_map/ppermute | solution.py:32
  133.4 12.6 %collective-permute-start.24 = (bf16[1,128,1024]{2,1,0:T(8,128)(2,1)S(1)}, bf16[1,128,1024]{2,1,0:T(8,128)(2,1)S(1)}, u32[]{:S(2)}, u32[]{:S(2)}) collective-permute-start(bf16[1,128,1024]{2,1,0:T(8,128)(2,1)S(1)} %collective-permute-done.21.refs_5_), channel_id=1, source_target_pairs={{0,32},{1,33},{2,34},{3,35},{4,36},{5,37},{6,38},{7,39},{8,40},{9,... | collective-permute-start | bytes 786440 | tf_op jit(solution)/shard_map/ppermute | solution.py:32
  137.3 17.0 %collective-permute-start.28 = (bf16[2,128,1024]{2,1,0:T(8,128)(2,1)S(1)}, bf16[2,128,1024]{2,1,0:T(8,128)(2,1)S(1)}, u32[]{:S(2)}, u32[]{:S(2)}) collective-permute-start(bf16[2,128,1024]{2,1,0:T(8,128)(2,1)S(1)} %pad_maximum_fusion.8), channel_id=1, source_target_pairs={{0,1},{1,0},{2,3},{3,2},{4,5},{5,4},{6,7},{7,6},{8,9},{9,8},{10,11... | collective-permute-start | bytes 1572872 | tf_op jit(solution)/shard_map/ppermute | solution.py:32
  141.8 9.7 %collective-permute-start.27 = (bf16[1,128,1024]{2,1,0:T(8,128)(2,1)S(1)}, bf16[1,128,1024]{2,1,0:T(8,128)(2,1)S(1)}, u32[]{:S(2)}, u32[]{:S(2)}) collective-permute-start(bf16[1,128,1024]{2,1,0:T(8,128)(2,1)S(1)} %get-tuple-element.16.refs_1_), channel_id=1, source_target_pairs={{0,31},{1,18},{2,17},{3,20},{4,19},{5,22},{6,21},{7,24},{8,23},{9,... | collective-permute-start | bytes 786440 | tf_op jit(solution)/shard_map/ppermute | solution.py:32
  141.8 9.7 %collective-permute-start.25 = (bf16[1,128,1024]{2,1,0:T(8,128)(2,1)S(1)}, bf16[1,128,1024]{2,1,0:T(8,128)(2,1)S(1)}, u32[]{:S(2)}, u32[]{:S(2)}) collective-permute-start(bf16[1,128,1024]{2,1,0:T(8,128)(2,1)S(1)} %collective-permute-done.22.refs_6_), channel_id=1, source_target_pairs={{0,32},{1,33},{2,34},{3,35},{4,36},{5,37},{6,38},{7,39},{8,40},{9,... | collective-permute-start | bytes 786440 | tf_op jit(solution)/shard_map/ppermute | solution.py:32
  145.6 8.7 %collective-permute-start.29 = (bf16[1,128,1024]{2,1,0:T(8,128)(2,1)S(1)}, bf16[1,128,1024]{2,1,0:T(8,128)(2,1)S(1)}, u32[]{:S(2)}, u32[]{:S(2)}) collective-permute-start(bf16[1,128,1024]{2,1,0:T(8,128)(2,1)S(1)} %collective-permute-done.23.refs_7_), channel_id=1, source_target_pairs={{0,15},{1,2},{2,1},{3,4},{4,3},{5,6},{6,5},{7,8},{8,7},{9,10},{10,... | collective-permute-start | bytes 786440 | tf_op jit(solution)/shard_map/ppermute | solution.py:32
  145.9 8.4 %collective-permute-start.30 = (bf16[1,128,1024]{2,1,0:T(8,128)(2,1)S(1)}, bf16[1,128,1024]{2,1,0:T(8,128)(2,1)S(1)}, u32[]{:S(2)}, u32[]{:S(2)}) collective-permute-start(bf16[1,128,1024]{2,1,0:T(8,128)(2,1)S(1)} %collective-permute-done.24.refs_8_), channel_id=1, source_target_pairs={{0,1},{1,0},{2,3},{3,2},{4,5},{5,4},{6,7},{7,6},{8,9},{9,8},{10,11... | collective-permute-start | bytes 786440 | tf_op jit(solution)/shard_map/ppermute | solution.py:32

commit v5 on v3

--- a/solution.py
+++ b/solution.py
@@ -11,6 +11,10 @@
 AXES = ("lat", "lon")
 GRID_SCALE = 8192.0
 MEBI = 1024 * 1024
+
+
+def far_band(band):
+    return band - 1 if band % 2 == 0 else band + 1
 
 
 def relay_band(band):
@@ -41,15 +45,22 @@
 
 
 def exchange(blocks):
+    half = blocks[0].shape[1] // 2
     near = [move(block, pair, same) for block in blocks]
     far = [move(block, relay_band, same) for block in near]
     outer = [
         move(blocks[0], same, outer_sector),
         move(blocks[0], pair, outer_sector),
-        move(far[0], same, outer_sector),
+        jnp.concatenate(
+            [
+                move(far[0][:, :half], same, outer_sector),
+                move(blocks[0][:, half:], far_band, outer_sector),
+            ],
+            axis=1,
+        ),
     ]
     inner = [
-        move(jnp.concatenate([blocks[-1], near[-1]], axis=0), same, pair), move(far[-1], same, pair)
+        move(jnp.concatenate([blocks[1], near[1]], axis=0), same, pair), move(far[1], same, pair)
     ]
     return near, far, outer[:2] + inner[:1], outer[2:] + inner[1:]
 
@@ -63,7 +74,9 @@
     group = jnp.where(band_step == 0, 0, jnp.where(band_step == near_step, 1, 2))
     even = sector_here % 2 == 0
     outer_column = jnp.where(even, 0, blocks_here + 1)
-    outer_first = jnp.where(even, column - 1, blocks_here - column)
+    inner_column = jnp.where(even, blocks_here, 1)
+    at_outer = column == jnp.where(even, 1, blocks_here)
+    outer_first = jnp.where(at_outer, 0, jnp.where(column == inner_column, 1, column))
     if own_in_order:
         outer_first = jnp.where(group == 0, column - 1, outer_first)
     inside = group * blocks_here + outer_first
@@ -119,7 +132,8 @@
 
 
 def block_at(place, count, even):
-    return jnp.where(even[0] == 1, place, count - 1 - place)
+    first = jnp.where(even[0] == 1, 0, count - 1)
+    return jnp.where(place == 0, first, jnp.where(place == 1, count - 1 - first, place - 1))
 
 
 def lift_kernel(slots, even, *refs, piece_count):
@@ -170,9 +184,10 @@
     neighbours = keys.shape[0] // rows
     head_size = width // HEADS
     wide = 2 * head_size
-    certain = neighbours // 2 * rows
     low_half = lax.broadcasted_iota(jnp.int32, (rows, wide), 1) < head_size
-    key_block = lax.broadcasted_iota(jnp.int32, (1, neighbours * rows - certain), 1) // rows + neighbours // 2
+    key_block = lax.broadcasted_iota(jnp.int32, (neighbours * rows, wide), 0) // rows
+    first_lane = lax.broadcasted_iota(jnp.int32, (2 * rows, wide), 1) == 0
+    marker = jnp.where(first_lane, 1.0, 0.0).astype(jnp.bfloat16)
     values[:, :, wide:] = jnp.ones((HEADS // 2, neighbours * rows, wide), jnp.bfloat16)
 
     def attend(m, carry):
@@ -183,7 +198,7 @@
             for h in range(HEADS // 2):
                 at = width + h * wide
                 values[h, j * rows:(j + 1) * rows, 0:wide] = table[slot, :, at:at + wide]
-        bias = jnp.where(key_block < counts[source], 0.0, -1e30)
+        bias = jnp.where(key_block < counts[source], 0.0, -1e30).astype(jnp.bfloat16)
 
         def score(h):
             at = h * wide
@@ -193,7 +208,10 @@
                 [jnp.where(low_half, query, none), jnp.where(low_half, none, query)], axis=0
             )
             return lax.dot_general(
-                pair_rows, keys[:, at:at + wide], (((1,), (1,)), ((), ())), preferred_element_type=jnp.float32
+                jnp.concatenate([pair_rows, marker], axis=1),
+                jnp.concatenate([keys[:, at:at + wide], bias], axis=1),
+                (((1,), (1,)), ((), ())),
+                preferred_element_type=jnp.float32,
             )
 
         following = score(0)
@@ -202,14 +220,8 @@
             scores = following
             if h + 1 < HEADS // 2:
                 following = score(h + 1)
-            first, second = scores[:, :certain], scores[:, certain:] + bias
-            highest = jnp.maximum(
-                jnp.max(first, axis=-1, keepdims=True), jnp.max(second, axis=-1, keepdims=True)
-            )
-            raw = jnp.concatenate(
-                [jnp.exp(first - highest).astype(jnp.bfloat16), jnp.exp(second - highest).astype(jnp.bfloat16)],
-                axis=1,
-            )
+            highest = jnp.max(scores, axis=-1, keepdims=True)
+            raw = jnp.exp(scores - highest).astype(jnp.bfloat16)
             summed = jnp.dot(raw, values[h], preferred_element_type=jnp.float32)
             part = summed[:, :wide] / summed[:, wide:]
             mixed[pl.ds(m * rows, rows), at:at + wide] = jnp.where(

time: 157 us -> 158 us (level)
  the two profiles are of different devices: /device:TPU:1 before, /device:TPU:32 now
where the time goes in v5:
time: 158 us
  starting transfers between devices  87.7 us (56%)
  waiting for transfers between devices  32.4 us (21%)
  Pallas kernels  21.6 us (14%)
  matrix products  10.2 us (6%)
  other arithmetic  5 us (3%)
    ppermute x34, starting transfers between devices, move(): return lax.ppermute(values, AXES, pairs)  87.7 us
    ppermute x34, waiting for transfers between devices, move(): return lax.ppermute(values, AXES, pairs)  32.4 us
    pallas_call x1, Pallas kernels, shards(): pl.pallas_call(lambda *refs: layer_kernel(*refs, piece_count=len(kv_piece...  16 us
    dot_general x4, matrix products, project(): jnp.dot(stacked.reshape(-1, width), kv_weight, preferred_element_type=f32)  7.3 us
  transfers between devices with their start and end apart: 34, of which 11 were waited for; matrix products, arithmetic and copies ran while one was open for 8% of the time, Pallas kernels for 0%

profile of v5, /device:TPU:32, one launch (start us, length us, event | category | flops | bytes accessed | tf_op | source)
XLA Modules:
  0.0 158.0 jit_solution(326852254105185521)
XLA Ops:
  0.0 1.4 fusion.11
  1.4 3.3 %collective-permute-start = (f16[1,128,1024]{2,1,0:T(8,128)(2,1)S(1)}, f16[1,128,1024]{2,1,0:T(8,128)(2,1)S(1)}, u32[]{:S(2)}, u32[]{:S(2)}) collective-permute-start(f16[1,128,1024]{2,1,0:T(8,128)(2,1)S(1)} %get-tuple-element.20), channel_id=1, source_target_pairs={{0,16},{1,17},{2,18},{3,19},{4,20},{5,21},{6,22},{7,23},{8,24},{9,... | collective-permute-start | bytes 786440 | tf_op jit(solution)/shard_map/ppermute | solution.py:36
  4.7 2.4 %collective-permute-start.5 = (f16[1,128,1024]{2,1,0:T(8,128)(2,1)S(1)}, f16[1,128,1024]{2,1,0:T(8,128)(2,1)S(1)}, u32[]{:S(2)}, u32[]{:S(2)}) collective-permute-start(f16[1,128,1024]{2,1,0:T(8,128)(2,1)S(1)} %get-tuple-element.20), channel_id=1, source_target_pairs={{0,31},{1,18},{2,17},{3,20},{4,19},{5,22},{6,21},{7,24},{8,23},{9,... | collective-permute-start | bytes 786440 | tf_op jit(solution)/shard_map/ppermute | solution.py:36
  7.1 4.1 %collective-permute-start.1 = (f16[1,128,1024]{2,1,0:T(8,128)(2,1)S(1)}, f16[1,128,1024]{2,1,0:T(8,128)(2,1)S(1)}, u32[]{:S(2)}, u32[]{:S(2)}) collective-permute-start(f16[1,128,1024]{2,1,0:T(8,128)(2,1)S(1)} %get-tuple-element.19), channel_id=1, source_target_pairs={{0,16},{1,17},{2,18},{3,19},{4,20},{5,21},{6,22},{7,23},{8,24},{9,... | collective-permute-start | bytes 786440 | tf_op jit(solution)/shard_map/ppermute | solution.py:36
  11.2 3.6 %collective-permute-start.8 = (f16[1,64,1024]{2,1,0:T(8,128)(2,1)S(1)}, f16[1,64,1024]{2,1,0:T(8,128)(2,1)S(1)}, u32[]{:S(2)}, u32[]{:S(2)}) collective-permute-start(f16[1,64,1024]{2,1,0:T(8,128)(2,1)S(1)} %slice.49), channel_id=1, source_target_pairs={{16,47},{17,34},{18,33},{19,36},{20,35},{21,38},{22,37},{23,40},{2... | collective-permute-start | bytes 393224 | tf_op jit(solution)/shard_map/ppermute | solution.py:36
  14.9 0.7 broadcast_remainder_fusion
  15.6 0.7 sign_compare_fusion
  16.2 0.1 reduce-precision_convert_fusion
  16.4 0.7 fusion.26.refs_0_
  17.2 5.2 %collective-permute-done.1 = f16[1,128,1024]{2,1,0:T(8,128)(2,1)S(1)} collective-permute-done((f16[1,128,1024]{2,1,0:T(8,128)(2,1)S(1)}, f16[1,128,1024]{2,1,0:T(8,128)(2,1)S(1)}, u32[]{:S(2)}, u32[]{:S(2)}) %collective-permute-start.1) | collective-permute-done | bytes 262176 | tf_op jit(solution)/shard_map/ppermute | solution.py:36
  22.4 0.1 pad_maximum_fusion.5
  22.5 1.9 %collective-permute-start.6 = (f16[2,128,1024]{2,1,0:T(8,128)(2,1)S(1)}, f16[2,128,1024]{2,1,0:T(8,128)(2,1)S(1)}, u32[]{:S(2)}, u32[]{:S(2)}) collective-permute-start(f16[2,128,1024]{2,1,0:T(8,128)(2,1)S(1)} %pad_maximum_fusion.5), channel_id=1, source_target_pairs={{0,1},{1,0},{2,3},{3,2},{4,5},{5,4},{6,7},{7,6},{8,9},{9,8},{10,11... | collective-permute-start | bytes 1572872 | tf_op jit(solution)/shard_map/ppermute | solution.py:36
  24.4 3.8 %collective-permute-start.2 = (f16[1,128,1024]{2,1,0:T(8,128)(2,1)S(1)}, f16[1,128,1024]{2,1,0:T(8,128)(2,1)S(1)}, u32[]{:S(2)}, u32[]{:S(2)}) collective-permute-start(f16[1,128,1024]{2,1,0:T(8,128)(2,1)S(1)} %collective-permute-done), channel_id=1, source_target_pairs={{0,32},{1,33},{2,34},{3,35},{4,36},{5,37},{6,38},{7,39},{8,40},{9,... | collective-permute-start | bytes 786440 | tf_op jit(solution)/shard_map/ppermute | solution.py:36
  28.4 3.5 %collective-permute-start.3 = (f16[1,128,1024]{2,1,0:T(8,128)(2,1)S(1)}, f16[1,128,1024]{2,1,0:T(8,128)(2,1)S(1)}, u32[]{:S(2)}, u32[]{:S(2)}) collective-permute-start(f16[1,128,1024]{2,1,0:T(8,128)(2,1)S(1)} %collective-permute-done.1), channel_id=1, source_target_pairs={{0,32},{1,33},{2,34},{3,35},{4,36},{5,37},{6,38},{7,39},{8,40},{9,... | collective-permute-start | bytes 786440 | tf_op jit(solution)/shard_map/ppermute | solution.py:36
  32.0 3.4 %collective-permute-done.2 = f16[1,128,1024]{2,1,0:T(8,128)(2,1)S(1)} collective-permute-done((f16[1,128,1024]{2,1,0:T(8,128)(2,1)S(1)}, f16[1,128,1024]{2,1,0:T(8,128)(2,1)S(1)}, u32[]{:S(2)}, u32[]{:S(2)}) %collective-permute-start.2) | collective-permute-done | bytes 262176 | tf_op jit(solution)/shard_map/ppermute | solution.py:36
  35.5 2.8 %collective-permute-start.7 = (f16[1,64,1024]{2,1,0:T(8,128)(2,1)S(1)}, f16[1,64,1024]{2,1,0:T(8,128)(2,1)S(1)}, u32[]{:S(2)}, u32[]{:S(2)}) collective-permute-start(f16[1,64,1024]{2,1,0:T(8,128)(2,1)S(1)} %slice.48), channel_id=1, source_target_pairs={{0,15},{1,2},{2,1},{3,4},{4,3},{5,6},{6,5},{7,8},{8,7},{9,10},{10,... | collective-permute-start | bytes 393224 | tf_op jit(solution)/shard_map/ppermute | solution.py:36
  38.3 2.0 %collective-permute-done.3 = f16[1,128,1024]{2,1,0:T(8,128)(2,1)S(1)} collective-permute-done((f16[1,128,1024]{2,1,0:T(8,128)(2,1)S(1)}, f16[1,128,1024]{2,1,0:T(8,128)(2,1)S(1)}, u32[]{:S(2)}, u32[]{:S(2)}) %collective-permute-start.3) | collective-permute-done | bytes 262176 | tf_op jit(solution)/shard_map/ppermute | solution.py:36
  40.4 1.8 %collective-permute-done.7 = f16[1,64,1024]{2,1,0:T(8,128)(2,1)S(1)} collective-permute-done((f16[1,64,1024]{2,1,0:T(8,128)(2,1)S(1)}, f16[1,64,1024]{2,1,0:T(8,128)(2,1)S(1)}, u32[]{:S(2)}, u32[]{:S(2)}) %collective-permute-start.7) | collective-permute-done | bytes 131104 | tf_op jit(solution)/shard_map/ppermute | solution.py:36
  42.3 0.1 convert_multiply_fusion.refs_9_
  42.5 2.9 %lift.1 = (f32[3,128,1024]{2,1,0:T(8,128)S(1)}, bf16[1,128,1024]{2,1,0:T(8,128)(2,1)S(1)}, bf16[1,128,1024]{2,1,0:T(8,128)(2,1)S(1)}, bf16[1,128,1024]{2,1,0:T(8,128)(2,1)S(1)}) custom-call(s32[3,4]{1,0:T(4,128)S(1)} %fusion.26.refs_0_, s32[1]{0:T(128)} %bitcast.4.refs_1_.refs_2_, f32[2,128,1024]{2,1,0:T(8,128)S(1)} %bitcast.113, ...), custom_call_target="tpu_custom_call" | custom-call | tf_op jit(solution)/shard_map/lift/pallas_call | solution.py:286
  45.4 3.7 %collective-permute-start.10 = (bf16[1,128,1024]{2,1,0:T(8,128)(2,1)S(1)}, bf16[1,128,1024]{2,1,0:T(8,128)(2,1)S(1)}, u32[]{:S(2)}, u32[]{:S(2)}) collective-permute-start(bf16[1,128,1024]{2,1,0:T(8,128)(2,1)S(1)} %get-tuple-element.12), channel_id=1, source_target_pairs={{0,16},{1,17},{2,18},{3,19},{4,20},{5,21},{6,22},{7,23},{8,24},{9,... | collective-permute-start | bytes 786440 | tf_op jit(solution)/shard_map/ppermute | solution.py:36
  49.1 0.8 collective-permute-start.16
  49.9 1.7 %collective-permute-start.17 = (bf16[1,128,1024]{2,1,0:T(8,128)(2,1)S(1)}, bf16[1,128,1024]{2,1,0:T(8,128)(2,1)S(1)}, u32[]{:S(2)}, u32[]{:S(2)}) collective-permute-start(bf16[1,128,1024]{2,1,0:T(8,128)(2,1)S(1)} %get-tuple-element.12), channel_id=1, source_target_pairs={{0,31},{1,18},{2,17},{3,20},{4,19},{5,22},{6,21},{7,24},{8,23},{9,... | collective-permute-start | bytes 786440 | tf_op jit(solution)/shard_map/ppermute | solution.py:36
  51.7 3.4 %collective-permute-start.11 = (bf16[1,128,1024]{2,1,0:T(8,128)(2,1)S(1)}, bf16[1,128,1024]{2,1,0:T(8,128)(2,1)S(1)}, u32[]{:S(2)}, u32[]{:S(2)}) collective-permute-start(bf16[1,128,1024]{2,1,0:T(8,128)(2,1)S(1)} %get-tuple-element.13), channel_id=1, source_target_pairs={{0,16},{1,17},{2,18},{3,19},{4,20},{5,21},{6,22},{7,23},{8,24},{9,... | collective-permute-start | bytes 786440 | tf_op jit(solution)/shard_map/ppermute | solution.py:36
  55.1 0.1 collective-permute-start.12
  55.2 0.1 pad_maximum_fusion.2
  55.3 2.9 %convolution_convert_fusion = bf16[384,3072]{1,0:T(8,128)(2,1)S(1)} fusion(bf16[384,1024]{1,0:T(8,128)(2,1)S(1)} %bitcast.122, bf16[1024,3072]{1,0:T(8,128)(2,1)S(1)} %bitcast.126), kind=kOutput, calls=%fused_computation | convolution fusion | flops 2417098752 | bytes 9437184 | tf_op jit(solution)/shard_map/dot_general | solution.py:308
  58.2 0.1 slice.50
  58.4 2.1 %collective-permute-done.10 = bf16[1,128,1024]{2,1,0:T(8,128)(2,1)S(1)} collective-permute-done((bf16[1,128,1024]{2,1,0:T(8,128)(2,1)S(1)}, bf16[1,128,1024]{2,1,0:T(8,128)(2,1)S(1)}, u32[]{:S(2)}, u32[]{:S(2)}) %collective-permute-start.10) | collective-permute-done | bytes 262176 | tf_op jit(solution)/shard_map/ppermute | solution.py:36
  60.5 3.7 %collective-permute-start.13 = (bf16[1,128,1024]{2,1,0:T(8,128)(2,1)S(1)}, bf16[1,128,1024]{2,1,0:T(8,128)(2,1)S(1)}, u32[]{:S(2)}, u32[]{:S(2)}) collective-permute-start(bf16[1,128,1024]{2,1,0:T(8,128)(2,1)S(1)} %collective-permute-done.10), channel_id=1, source_target_pairs={{0,32},{1,33},{2,34},{3,35},{4,36},{5,37},{6,38},{7,39},{8,40},{9,... | collective-permute-start | bytes 786440 | tf_op jit(solution)/shard_map/ppermute | solution.py:36
  64.3 0.9 collective-permute-done.11
  65.2 3.8 %collective-permute-start.14 = (bf16[1,128,1024]{2,1,0:T(8,128)(2,1)S(1)}, bf16[1,128,1024]{2,1,0:T(8,128)(2,1)S(1)}, u32[]{:S(2)}, u32[]{:S(2)}) collective-permute-start(bf16[1,128,1024]{2,1,0:T(8,128)(2,1)S(1)} %collective-permute-done.11), channel_id=1, source_target_pairs={{0,32},{1,33},{2,34},{3,35},{4,36},{5,37},{6,38},{7,39},{8,40},{9,... | collective-permute-start | bytes 786440 | tf_op jit(solution)/shard_map/ppermute | solution.py:36
  68.9 1.8 %collective-permute-done.12 = bf16[1,128,1024]{2,1,0:T(8,128)(2,1)S(1)} collective-permute-done((bf16[1,128,1024]{2,1,0:T(8,128)(2,1)S(1)}, bf16[1,128,1024]{2,1,0:T(8,128)(2,1)S(1)}, u32[]{:S(2)}, u32[]{:S(2)}) %collective-permute-start.12) | collective-permute-done | bytes 262176 | tf_op jit(solution)/shard_map/ppermute | solution.py:36
  70.8 3.8 %collective-permute-start.15 = (bf16[1,128,1024]{2,1,0:T(8,128)(2,1)S(1)}, bf16[1,128,1024]{2,1,0:T(8,128)(2,1)S(1)}, u32[]{:S(2)}, u32[]{:S(2)}) collective-permute-start(bf16[1,128,1024]{2,1,0:T(8,128)(2,1)S(1)} %collective-permute-done.12), channel_id=1, source_target_pairs={{0,32},{1,33},{2,34},{3,35},{4,36},{5,37},{6,38},{7,39},{8,40},{9,... | collective-permute-start | bytes 786440 | tf_op jit(solution)/shard_map/ppermute | solution.py:36
  74.6 0.1 pad_maximum_fusion.3
  74.7 1.8 %convolution_convert_fusion.3 = bf16[384,2048]{1,0:T(8,128)(2,1)S(1)} fusion(bf16[384,1024]{1,0:T(8,128)(2,1)S(1)} %bitcast.123, bf16[1024,3072]{1,0:T(8,128)(2,1)S(1)} %bitcast.126), kind=kOutput, calls=%fused_computation.3 | convolution fusion | flops 1611399168 | bytes 6553600 | tf_op jit(solution)/shard_map/dot_general | solution.py:316
  76.6 2.3 %collective-permute-start.20 = (bf16[1,64,1024]{2,1,0:T(8,128)(2,1)S(1)}, bf16[1,64,1024]{2,1,0:T(8,128)(2,1)S(1)}, u32[]{:S(2)}, u32[]{:S(2)}) collective-permute-start(bf16[1,64,1024]{2,1,0:T(8,128)(2,1)S(1)} %slice.44), channel_id=1, source_target_pairs={{16,47},{17,34},{18,33},{19,36},{20,35},{21,38},{22,37},{23,40},{2... | collective-permute-start | bytes 393224 | tf_op jit(solution)/shard_map/ppermute | solution.py:36
  78.9 2.7 %collective-permute-start.18 = (bf16[2,128,1024]{2,1,0:T(8,128)(2,1)S(1)}, bf16[2,128,1024]{2,1,0:T(8,128)(2,1)S(1)}, u32[]{:S(2)}, u32[]{:S(2)}) collective-permute-start(bf16[2,128,1024]{2,1,0:T(8,128)(2,1)S(1)} %pad_maximum_fusion.6), channel_id=1, source_target_pairs={{0,1},{1,0},{2,3},{3,2},{4,5},{5,4},{6,7},{7,6},{8,9},{9,8},{10,11... | collective-permute-start | bytes 1572872 | tf_op jit(solution)/shard_map/ppermute | solution.py:36
  81.6 5.9 %collective-permute-start.19 = (bf16[1,64,1024]{2,1,0:T(8,128)(2,1)S(1)}, bf16[1,64,1024]{2,1,0:T(8,128)(2,1)S(1)}, u32[]{:S(2)}, u32[]{:S(2)}) collective-permute-start(bf16[1,64,1024]{2,1,0:T(8,128)(2,1)S(1)} %slice.51), channel_id=1, source_target_pairs={{0,15},{1,2},{2,1},{3,4},{4,3},{5,6},{6,5},{7,8},{8,7},{9,10},{10,... | collective-permute-start | bytes 393224 | tf_op jit(solution)/shard_map/ppermute | solution.py:36
  87.5 0.1 pad_maximum_fusion.4
  87.6 1.8 %convolution_convert_fusion.2 = bf16[384,2048]{1,0:T(8,128)(2,1)S(1)} fusion(bf16[384,1024]{1,0:T(8,128)(2,1)S(1)} %bitcast.121, bf16[1024,3072]{1,0:T(8,128)(2,1)S(1)} %bitcast.126), kind=kOutput, calls=%fused_computation.2 | convolution fusion | flops 1611399168 | bytes 6553600 | tf_op jit(solution)/shard_map/dot_general | solution.py:316
  89.4 0.7 collective-permute-start.21
  90.1 0.1 pad_maximum_fusion
  90.2 2.4 %convolution_convert_fusion.1 = bf16[512,2048]{1,0:T(8,128)(2,1)S(1)} fusion(bf16[512,1024]{1,0:T(8,128)(2,1)S(1)} %bitcast.120, bf16[1024,3072]{1,0:T(8,128)(2,1)S(1)} %bitcast.126), kind=kOutput, calls=%fused_computation.1 | convolution fusion | flops 2148532224 | bytes 7340032 | tf_op jit(solution)/shard_map/dot_general | solution.py:316
  92.7 1.3 fusion.5
  94.0 16.0 %layer.1 = (bf16[1,128,1024]{2,1,0:T(8,128)(2,1)S(1)}, bf16[1,128,1024]{2,1,0:T(8,128)(2,1)S(1)}, bf16[1,128,1024]{2,1,0:T(8,128)(2,1)S(1)}) custom-call(s32[3,8]{1,0:T(4,128)S(1)} %fusion.22.refs_0_, s32[3]{0:T(128)S(1)} %bitcast.119, s32[1]{0:T(128)} %bitcast.4.refs_1_.refs_2_, bf16[3,128,2048]{2,1,0:T(8,128)(2,1)S(1)} %bitcast.112, ...), custom_call_target="tpu_custom_call" | custom-call | tf_op jit(solution)/shard_map/layer/pallas_call | solution.py:328
  110.0 2.2 %collective-permute-start.22 = (bf16[1,128,1024]{2,1,0:T(8,128)(2,1)S(1)}, bf16[1,128,1024]{2,1,0:T(8,128)(2,1)S(1)}, u32[]{:S(2)}, u32[]{:S(2)}) collective-permute-start(bf16[1,128,1024]{2,1,0:T(8,128)(2,1)S(1)} %get-tuple-element.16.refs_1_), channel_id=1, source_target_pairs={{0,16},{1,17},{2,18},{3,19},{4,20},{5,21},{6,22},{7,23},{8,24},{9,... | collective-permute-start | bytes 786440 | tf_op jit(solution)/shard_map/ppermute | solution.py:36
  112.2 1.6 %collective-permute-start.23 = (bf16[1,128,1024]{2,1,0:T(8,128)(2,1)S(1)}, bf16[1,128,1024]{2,1,0:T(8,128)(2,1)S(1)}, u32[]{:S(2)}, u32[]{:S(2)}) collective-permute-start(bf16[1,128,1024]{2,1,0:T(8,128)(2,1)S(1)} %get-tuple-element.17.refs_2_), channel_id=1, source_target_pairs={{0,16},{1,17},{2,18},{3,19},{4,20},{5,21},{6,22},{7,23},{8,24},{9,... | collective-permute-start | bytes 786440 | tf_op jit(solution)/shard_map/ppermute | solution.py:36
  113.8 7.2 %collective-permute-done.22.refs_4_ = bf16[1,128,1024]{2,1,0:T(8,128)(2,1)S(1)} collective-permute-done((bf16[1,128,1024]{2,1,0:T(8,128)(2,1)S(1)}, bf16[1,128,1024]{2,1,0:T(8,128)(2,1)S(1)}, u32[]{:S(2)}, u32[]{:S(2)}) %collective-permute-start.22) | collective-permute-done | bytes 262176 | tf_op jit(solution)/shard_map/ppermute | solution.py:36
  121.0 4.1 %collective-permute-start.25 = (bf16[1,128,1024]{2,1,0:T(8,128)(2,1)S(1)}, bf16[1,128,1024]{2,1,0:T(8,128)(2,1)S(1)}, u32[]{:S(2)}, u32[]{:S(2)}) collective-permute-start(bf16[1,128,1024]{2,1,0:T(8,128)(2,1)S(1)} %collective-permute-done.22.refs_4_), channel_id=1, source_target_pairs={{0,32},{1,33},{2,34},{3,35},{4,36},{5,37},{6,38},{7,39},{8,40},{9,... | collective-permute-start | bytes 786440 | tf_op jit(solution)/shard_map/ppermute | solution.py:36
  125.1 1.9 %collective-permute-start.32 = (bf16[1,64,1024]{2,1,0:T(8,128)(2,1)S(1)}, bf16[1,64,1024]{2,1,0:T(8,128)(2,1)S(1)}, u32[]{:S(2)}, u32[]{:S(2)}) collective-permute-start(bf16[1,64,1024]{2,1,0:T(8,128)(2,1)S(1)} %slice.47), channel_id=1, source_target_pairs={{16,47},{17,34},{18,33},{19,36},{20,35},{21,38},{22,37},{23,40},{2... | collective-permute-start | bytes 393224 | tf_op jit(solution)/shard_map/ppermute | solution.py:36
  127.0 4.2 %collective-permute-start.24 = (bf16[1,128,1024]{2,1,0:T(8,128)(2,1)S(1)}, bf16[1,128,1024]{2,1,0:T(8,128)(2,1)S(1)}, u32[]{:S(2)}, u32[]{:S(2)}) collective-permute-start(bf16[1,128,1024]{2,1,0:T(8,128)(2,1)S(1)} %get-tuple-element.18.refs_3_), channel_id=1, source_target_pairs={{0,16},{1,17},{2,18},{3,19},{4,20},{5,21},{6,22},{7,23},{8,24},{9,... | collective-permute-start | bytes 786440 | tf_op jit(solution)/shard_map/ppermute | solution.py:36
  131.2 1.9 %collective-permute-start.26 = (bf16[1,128,1024]{2,1,0:T(8,128)(2,1)S(1)}, bf16[1,128,1024]{2,1,0:T(8,128)(2,1)S(1)}, u32[]{:S(2)}, u32[]{:S(2)}) collective-permute-start(bf16[1,128,1024]{2,1,0:T(8,128)(2,1)S(1)} %collective-permute-done.23.refs_5_), channel_id=1, source_target_pairs={{0,32},{1,33},{2,34},{3,35},{4,36},{5,37},{6,38},{7,39},{8,40},{9,... | collective-permute-start | bytes 786440 | tf_op jit(solution)/shard_map/ppermute | solution.py:36
  133.2 0.1 collective-permute-start.30
  133.3 3.5 %collective-permute-start.31 = (bf16[1,64,1024]{2,1,0:T(8,128)(2,1)S(1)}, bf16[1,64,1024]{2,1,0:T(8,128)(2,1)S(1)}, u32[]{:S(2)}, u32[]{:S(2)}) collective-permute-start(bf16[1,64,1024]{2,1,0:T(8,128)(2,1)S(1)} %slice.53), channel_id=1, source_target_pairs={{0,15},{1,2},{2,1},{3,4},{4,3},{5,6},{6,5},{7,8},{8,7},{9,10},{10,... | collective-permute-start | bytes 393224 | tf_op jit(solution)/shard_map/ppermute | solution.py:36
  136.9 0.1 reduce-precision_convert_fusion.1
  136.9 0.5 collective-permute-start.28
  137.4 1.9 %collective-permute-done.24.refs_6_ = bf16[1,128,1024]{2,1,0:T(8,128)(2,1)S(1)} collective-permute-done((bf16[1,128,1024]{2,1,0:T(8,128)(2,1)S(1)}, bf16[1,128,1024]{2,1,0:T(8,128)(2,1)S(1)}, u32[]{:S(2)}, u32[]{:S(2)}) %collective-permute-start.24) | collective-permute-done | bytes 262176 | tf_op jit(solution)/shard_map/ppermute | solution.py:36
  139.3 7.6 %collective-permute-start.29 = (bf16[1,128,1024]{2,1,0:T(8,128)(2,1)S(1)}, bf16[1,128,1024]{2,1,0:T(8,128)(2,1)S(1)}, u32[]{:S(2)}, u32[]{:S(2)}) collective-permute-start(bf16[1,128,1024]{2,1,0:T(8,128)(2,1)S(1)} %get-tuple-element.16.refs_1_), channel_id=1, source_target_pairs={{0,31},{1,18},{2,17},{3,20},{4,19},{5,22},{6,21},{7,24},{8,23},{9,... | collective-permute-start | bytes 786440 | tf_op jit(solution)/shard_map/ppermute | solution.py:36
  146.9 1.9 %collective-permute-start.27 = (bf16[1,128,1024]{2,1,0:T(8,128)(2,1)S(1)}, bf16[1,128,1024]{2,1,0:T(8,128)(2,1)S(1)}, u32[]{:S(2)}, u32[]{:S(2)}) collective-permute-start(bf16[1,128,1024]{2,1,0:T(8,128)(2,1)S(1)} %collective-permute-done.24.refs_6_), channel_id=1, source_target_pairs={{0,32},{1,33},{2,34},{3,35},{4,36},{5,37},{6,38},{7,39},{8,40},{9,... | collective-permute-start | bytes 786440 | tf_op jit(solution)/shard_map/ppermute | solution.py:36
  148.8 0.1 collective-permute-start.33
  149.0 1.9 %collective-permute-done.29.refs_11_ = bf16[1,128,1024]{2,1,0:T(8,128)(2,1)S(1)} collective-permute-done((bf16[1,128,1024]{2,1,0:T(8,128)(2,1)S(1)}, bf16[1,128,1024]{2,1,0:T(8,128)(2,1)S(1)}, u32[]{:S(2)}, u32[]{:S(2)}) %collective-permute-start.29) | collective-permute-done | bytes 262176 | tf_op jit(solution)/shard_map/ppermute | solution.py:36
  150.9 4.2 %collective-permute-done.27.refs_9_ = bf16[1,128,1024]{2,1,0:T(8,128)(2,1)S(1)} collective-permute-done((bf16[1,128,1024]{2,1,0:T(8,128)(2,1)S(1)}, bf16[1,128,1024]{2,1,0:T(8,128)(2,1)S(1)}, u32[]{:S(2)}, u32[]{:S(2)}) %collective-permute-start.27) | collective-permute-done | bytes 262176 | tf_op jit(solution)/shard_map/ppermute | solution.py:36
  155.1 2.7 %give_back.1 = f32[2,128,1024]{2,1,0:T(8,128)} custom-call(s32[2,4]{1,0:T(2,128)S(1)} %and_select_fusion.refs_0_, bf16[1,128,1024]{2,1,0:T(8,128)(2,1)S(1)} %get-tuple-element.16.refs_1_, bf16[1,128,1024]{2,1,0:T(8,128)(2,1)S(1)} %get-tuple-element.17.refs_2_, bf16[1,128,1024]{2,1,0:T(8,128)(2,1)S(1)} %get-tuple-element.18.refs_3_, ...), custom_call_target="tpu_custom_call" | custom-call | tf_op jit(solution)/shard_map/give_back/pallas_call | solution.py:356
  (65 shorter events, 1.0 us)
Async XLA Ops:
  0.0 16.2 %copy-start = (f32[1,3,4,128,128]{4,3,2,1,0:T(8,128)S(1)}, f32[1,3,4,128,128]{4,3,2,1,0:T(8,128)}, u32[]{:S(2)}) copy-start(f32[1,3,4,128,128]{4,3,2,1,0:T(8,128)} %param.14) | copy-start | bytes 2359300
  1.4 23.0 %collective-permute-start = (f16[1,128,1024]{2,1,0:T(8,128)(2,1)S(1)}, f16[1,128,1024]{2,1,0:T(8,128)(2,1)S(1)}, u32[]{:S(2)}, u32[]{:S(2)}) collective-permute-start(f16[1,128,1024]{2,1,0:T(8,128)(2,1)S(1)} %get-tuple-element.20), channel_id=1, source_target_pairs={{0,16},{1,17},{2,18},{3,19},{4,20},{5,21},{6,22},{7,23},{8,24},{9,... | collective-permute-start | bytes 786440 | tf_op jit(solution)/shard_map/ppermute | solution.py:36
  4.7 23.7 %collective-permute-start.5 = (f16[1,128,1024]{2,1,0:T(8,128)(2,1)S(1)}, f16[1,128,1024]{2,1,0:T(8,128)(2,1)S(1)}, u32[]{:S(2)}, u32[]{:S(2)}) collective-permute-start(f16[1,128,1024]{2,1,0:T(8,128)(2,1)S(1)} %get-tuple-element.20), channel_id=1, source_target_pairs={{0,31},{1,18},{2,17},{3,20},{4,19},{5,22},{6,21},{7,24},{8,23},{9,... | collective-permute-start | bytes 786440 | tf_op jit(solution)/shard_map/ppermute | solution.py:36
  7.1 24.9 %collective-permute-start.4 = (f16[1,128,1024]{2,1,0:T(8,128)(2,1)S(1)}, f16[1,128,1024]{2,1,0:T(8,128)(2,1)S(1)}, u32[]{:S(2)}, u32[]{:S(2)}) collective-permute-start(f16[1,128,1024]{2,1,0:T(8,128)(2,1)S(1)} %get-tuple-element.20), channel_id=1, source_target_pairs={{0,15},{1,2},{2,1},{3,4},{4,3},{5,6},{6,5},{7,8},{8,7},{9,10},{10,... | collective-permute-start | bytes 786440 | tf_op jit(solution)/shard_map/ppermute | solution.py:36
  7.1 15.3 %collective-permute-start.1 = (f16[1,128,1024]{2,1,0:T(8,128)(2,1)S(1)}, f16[1,128,1024]{2,1,0:T(8,128)(2,1)S(1)}, u32[]{:S(2)}, u32[]{:S(2)}) collective-permute-start(f16[1,128,1024]{2,1,0:T(8,128)(2,1)S(1)} %get-tuple-element.19), channel_id=1, source_target_pairs={{0,16},{1,17},{2,18},{3,19},{4,20},{5,21},{6,22},{7,23},{8,24},{9,... | collective-permute-start | bytes 786440 | tf_op jit(solution)/shard_map/ppermute | solution.py:36
  11.2 29.2 %collective-permute-start.8 = (f16[1,64,1024]{2,1,0:T(8,128)(2,1)S(1)}, f16[1,64,1024]{2,1,0:T(8,128)(2,1)S(1)}, u32[]{:S(2)}, u32[]{:S(2)}) collective-permute-start(f16[1,64,1024]{2,1,0:T(8,128)(2,1)S(1)} %slice.49), channel_id=1, source_target_pairs={{16,47},{17,34},{18,33},{19,36},{20,35},{21,38},{22,37},{23,40},{2... | collective-permute-start | bytes 393224 | tf_op jit(solution)/shard_map/ppermute | solution.py:36
  22.5 20.0 %copy-start.1 = (f32[1,2,128,1024]{3,2,1,0:T(8,128)S(1)}, f32[1,2,128,1024]{3,2,1,0:T(8,128)}, u32[]{:S(2)}) copy-start(f32[1,2,128,1024]{3,2,1,0:T(8,128)} %param.12) | copy-start | bytes 3145732
  22.5 20.0 %copy-start.2 = (f32[2,1024]{1,0:T(2,128)S(1)}, f32[2,1024]{1,0:T(2,128)}, u32[]{:S(2)}) copy-start(f32[2,1024]{1,0:T(2,128)} %refs_10_.1) | copy-start | bytes 24580
  22.5 19.7 %collective-permute-start.6 = (f16[2,128,1024]{2,1,0:T(8,128)(2,1)S(1)}, f16[2,128,1024]{2,1,0:T(8,128)(2,1)S(1)}, u32[]{:S(2)}, u32[]{:S(2)}) collective-permute-start(f16[2,128,1024]{2,1,0:T(8,128)(2,1)S(1)} %pad_maximum_fusion.5), channel_id=1, source_target_pairs={{0,1},{1,0},{2,3},{3,2},{4,5},{5,4},{6,7},{7,6},{8,9},{9,8},{10,11... | collective-permute-start | bytes 1572872 | tf_op jit(solution)/shard_map/ppermute | solution.py:36
  24.4 11.1 %collective-permute-start.2 = (f16[1,128,1024]{2,1,0:T(8,128)(2,1)S(1)}, f16[1,128,1024]{2,1,0:T(8,128)(2,1)S(1)}, u32[]{:S(2)}, u32[]{:S(2)}) collective-permute-start(f16[1,128,1024]{2,1,0:T(8,128)(2,1)S(1)} %collective-permute-done), channel_id=1, source_target_pairs={{0,32},{1,33},{2,34},{3,35},{4,36},{5,37},{6,38},{7,39},{8,40},{9,... | collective-permute-start | bytes 786440 | tf_op jit(solution)/shard_map/ppermute | solution.py:36
  28.4 11.9 %collective-permute-start.3 = (f16[1,128,1024]{2,1,0:T(8,128)(2,1)S(1)}, f16[1,128,1024]{2,1,0:T(8,128)(2,1)S(1)}, u32[]{:S(2)}, u32[]{:S(2)}) collective-permute-start(f16[1,128,1024]{2,1,0:T(8,128)(2,1)S(1)} %collective-permute-done.1), channel_id=1, source_target_pairs={{0,32},{1,33},{2,34},{3,35},{4,36},{5,37},{6,38},{7,39},{8,40},{9,... | collective-permute-start | bytes 786440 | tf_op jit(solution)/shard_map/ppermute | solution.py:36
  35.5 6.7 %collective-permute-start.7 = (f16[1,64,1024]{2,1,0:T(8,128)(2,1)S(1)}, f16[1,64,1024]{2,1,0:T(8,128)(2,1)S(1)}, u32[]{:S(2)}, u32[]{:S(2)}) collective-permute-start(f16[1,64,1024]{2,1,0:T(8,128)(2,1)S(1)} %slice.48), channel_id=1, source_target_pairs={{0,15},{1,2},{2,1},{3,4},{4,3},{5,6},{6,5},{7,8},{8,7},{9,10},{10,... | collective-permute-start | bytes 393224 | tf_op jit(solution)/shard_map/ppermute | solution.py:36
  40.3 2.1 %collective-permute-start.9 = (f16[1,128,1024]{2,1,0:T(8,128)(2,1)S(1)}, f16[1,128,1024]{2,1,0:T(8,128)(2,1)S(1)}, u32[]{:S(2)}, u32[]{:S(2)}) collective-permute-start(f16[1,128,1024]{2,1,0:T(8,128)(2,1)S(1)} %collective-permute-done.3), channel_id=1, source_target_pairs={{0,1},{1,0},{2,3},{3,2},{4,5},{5,4},{6,7},{7,6},{8,9},{9,8},{10,11... | collective-permute-start | bytes 786440 | tf_op jit(solution)/shard_map/ppermute | solution.py:36
  42.2 13.1 %slice-start = ((s8[6291456]{0:T(1024)(128)(4,1)}), s8[4194304]{0:T(1024)(128)(4,1)S(1)}, s32[]{:S(2)}) async-start(s8[6291456]{0:T(1024)(128)(4,1)} %bitcast.125), calls=%async_computation | async-start | bytes 8388608
  42.5 12.8 %slice-start.1 = ((s8[6291456]{0:T(1024)(128)(4,1)}), s8[2097152]{0:T(1024)(128)(4,1)S(1)}, s32[]{:S(2)}) async-start(s8[6291456]{0:T(1024)(128)(4,1)} %bitcast.125), calls=%async_computation.1 | async-start | bytes 4194304
  45.4 15.1 %collective-permute-start.10 = (bf16[1,128,1024]{2,1,0:T(8,128)(2,1)S(1)}, bf16[1,128,1024]{2,1,0:T(8,128)(2,1)S(1)}, u32[]{:S(2)}, u32[]{:S(2)}) collective-permute-start(bf16[1,128,1024]{2,1,0:T(8,128)(2,1)S(1)} %get-tuple-element.12), channel_id=1, source_target_pairs={{0,16},{1,17},{2,18},{3,19},{4,20},{5,21},{6,22},{7,23},{8,24},{9,... | collective-permute-start | bytes 786440 | tf_op jit(solution)/shard_map/ppermute | solution.py:36
  49.1 40.3 %collective-permute-start.16 = (bf16[1,128,1024]{2,1,0:T(8,128)(2,1)S(1)}, bf16[1,128,1024]{2,1,0:T(8,128)(2,1)S(1)}, u32[]{:S(2)}, u32[]{:S(2)}) collective-permute-start(bf16[1,128,1024]{2,1,0:T(8,128)(2,1)S(1)} %get-tuple-element.12), channel_id=1, source_target_pairs={{0,15},{1,2},{2,1},{3,4},{4,3},{5,6},{6,5},{7,8},{8,7},{9,10},{10,... | collective-permute-start | bytes 786440 | tf_op jit(solution)/shard_map/ppermute | solution.py:36
  49.9 40.2 %collective-permute-start.17 = (bf16[1,128,1024]{2,1,0:T(8,128)(2,1)S(1)}, bf16[1,128,1024]{2,1,0:T(8,128)(2,1)S(1)}, u32[]{:S(2)}, u32[]{:S(2)}) collective-permute-start(bf16[1,128,1024]{2,1,0:T(8,128)(2,1)S(1)} %get-tuple-element.12), channel_id=1, source_target_pairs={{0,31},{1,18},{2,17},{3,20},{4,19},{5,22},{6,21},{7,24},{8,23},{9,... | collective-permute-start | bytes 786440 | tf_op jit(solution)/shard_map/ppermute | solution.py:36
  51.7 13.5 %collective-permute-start.11 = (bf16[1,128,1024]{2,1,0:T(8,128)(2,1)S(1)}, bf16[1,128,1024]{2,1,0:T(8,128)(2,1)S(1)}, u32[]{:S(2)}, u32[]{:S(2)}) collective-permute-start(bf16[1,128,1024]{2,1,0:T(8,128)(2,1)S(1)} %get-tuple-element.13), channel_id=1, source_target_pairs={{0,16},{1,17},{2,18},{3,19},{4,20},{5,21},{6,22},{7,23},{8,24},{9,... | collective-permute-start | bytes 786440 | tf_op jit(solution)/shard_map/ppermute | solution.py:36
  55.1 15.7 %collective-permute-start.12 = (bf16[1,128,1024]{2,1,0:T(8,128)(2,1)S(1)}, bf16[1,128,1024]{2,1,0:T(8,128)(2,1)S(1)}, u32[]{:S(2)}, u32[]{:S(2)}) collective-permute-start(bf16[1,128,1024]{2,1,0:T(8,128)(2,1)S(1)} %get-tuple-element.14), channel_id=1, source_target_pairs={{0,16},{1,17},{2,18},{3,19},{4,20},{5,21},{6,22},{7,23},{8,24},{9,... | collective-permute-start | bytes 786440 | tf_op jit(solution)/shard_map/ppermute | solution.py:36
  60.5 16.0 %collective-permute-start.13 = (bf16[1,128,1024]{2,1,0:T(8,128)(2,1)S(1)}, bf16[1,128,1024]{2,1,0:T(8,128)(2,1)S(1)}, u32[]{:S(2)}, u32[]{:S(2)}) collective-permute-start(bf16[1,128,1024]{2,1,0:T(8,128)(2,1)S(1)} %collective-permute-done.10), channel_id=1, source_target_pairs={{0,32},{1,33},{2,34},{3,35},{4,36},{5,37},{6,38},{7,39},{8,40},{9,... | collective-permute-start | bytes 786440 | tf_op jit(solution)/shard_map/ppermute | solution.py:36
  65.2 13.7 %collective-permute-start.14 = (bf16[1,128,1024]{2,1,0:T(8,128)(2,1)S(1)}, bf16[1,128,1024]{2,1,0:T(8,128)(2,1)S(1)}, u32[]{:S(2)}, u32[]{:S(2)}) collective-permute-start(bf16[1,128,1024]{2,1,0:T(8,128)(2,1)S(1)} %collective-permute-done.11), channel_id=1, source_target_pairs={{0,32},{1,33},{2,34},{3,35},{4,36},{5,37},{6,38},{7,39},{8,40},{9,... | collective-permute-start | bytes 786440 | tf_op jit(solution)/shard_map/ppermute | solution.py:36
  70.8 10.8 %collective-permute-start.15 = (bf16[1,128,1024]{2,1,0:T(8,128)(2,1)S(1)}, bf16[1,128,1024]{2,1,0:T(8,128)(2,1)S(1)}, u32[]{:S(2)}, u32[]{:S(2)}) collective-permute-start(bf16[1,128,1024]{2,1,0:T(8,128)(2,1)S(1)} %collective-permute-done.12), channel_id=1, source_target_pairs={{0,32},{1,33},{2,34},{3,35},{4,36},{5,37},{6,38},{7,39},{8,40},{9,... | collective-permute-start | bytes 786440 | tf_op jit(solution)/shard_map/ppermute | solution.py:36
  76.6 16.0 %collective-permute-start.20 = (bf16[1,64,1024]{2,1,0:T(8,128)(2,1)S(1)}, bf16[1,64,1024]{2,1,0:T(8,128)(2,1)S(1)}, u32[]{:S(2)}, u32[]{:S(2)}) collective-permute-start(bf16[1,64,1024]{2,1,0:T(8,128)(2,1)S(1)} %slice.44), channel_id=1, source_target_pairs={{16,47},{17,34},{18,33},{19,36},{20,35},{21,38},{22,37},{23,40},{2... | collective-permute-start | bytes 393224 | tf_op jit(solution)/shard_map/ppermute | solution.py:36
  78.9 11.2 %collective-permute-start.18 = (bf16[2,128,1024]{2,1,0:T(8,128)(2,1)S(1)}, bf16[2,128,1024]{2,1,0:T(8,128)(2,1)S(1)}, u32[]{:S(2)}, u32[]{:S(2)}) collective-permute-start(bf16[2,128,1024]{2,1,0:T(8,128)(2,1)S(1)} %pad_maximum_fusion.6), channel_id=1, source_target_pairs={{0,1},{1,0},{2,3},{3,2},{4,5},{5,4},{6,7},{7,6},{8,9},{9,8},{10,11... | collective-permute-start | bytes 1572872 | tf_op jit(solution)/shard_map/ppermute | solution.py:36
  81.6 11.0 %collective-permute-start.19 = (bf16[1,64,1024]{2,1,0:T(8,128)(2,1)S(1)}, bf16[1,64,1024]{2,1,0:T(8,128)(2,1)S(1)}, u32[]{:S(2)}, u32[]{:S(2)}) collective-permute-start(bf16[1,64,1024]{2,1,0:T(8,128)(2,1)S(1)} %slice.51), channel_id=1, source_target_pairs={{0,15},{1,2},{2,1},{3,4},{4,3},{5,6},{6,5},{7,8},{8,7},{9,10},{10,... | collective-permute-start | bytes 393224 | tf_op jit(solution)/shard_map/ppermute | solution.py:36
  89.4 3.2 %collective-permute-start.21 = (bf16[1,128,1024]{2,1,0:T(8,128)(2,1)S(1)}, bf16[1,128,1024]{2,1,0:T(8,128)(2,1)S(1)}, u32[]{:S(2)}, u32[]{:S(2)}) collective-permute-start(bf16[1,128,1024]{2,1,0:T(8,128)(2,1)S(1)} %collective-permute-done.14), channel_id=1, source_target_pairs={{0,1},{1,0},{2,3},{3,2},{4,5},{5,4},{6,7},{7,6},{8,9},{9,8},{10,11... | collective-permute-start | bytes 786440 | tf_op jit(solution)/shard_map/ppermute | solution.py:36
  92.7 1.3 copy-start.3
  94.0 42.9 %copy-start.4 = (f32[1,2,4,128,128]{4,3,2,1,0:T(8,128)S(1)}, f32[1,2,4,128,128]{4,3,2,1,0:T(8,128)}, u32[]{:S(2)}) copy-start(f32[1,2,4,128,128]{4,3,2,1,0:T(8,128)} %param.23) | copy-start | bytes 1572868
  94.0 54.9 %copy-start.5 = (s32[1,2,4]{2,1,0:T(2,128)S(1)}, s32[1,2,4]{2,1,0:T(2,128)}, u32[]{:S(2)}) copy-start(s32[1,2,4]{2,1,0:T(2,128)} %param.22) | copy-start | bytes 100
  110.0 11.0 %collective-permute-start.22 = (bf16[1,128,1024]{2,1,0:T(8,128)(2,1)S(1)}, bf16[1,128,1024]{2,1,0:T(8,128)(2,1)S(1)}, u32[]{:S(2)}, u32[]{:S(2)}) collective-permute-start(bf16[1,128,1024]{2,1,0:T(8,128)(2,1)S(1)} %get-tuple-element.16.refs_1_), channel_id=1, source_target_pairs={{0,16},{1,17},{2,18},{3,19},{4,20},{5,21},{6,22},{7,23},{8,24},{9,... | collective-permute-start | bytes 786440 | tf_op jit(solution)/shard_map/ppermute | solution.py:36
  112.2 19.0 %collective-permute-start.23 = (bf16[1,128,1024]{2,1,0:T(8,128)(2,1)S(1)}, bf16[1,128,1024]{2,1,0:T(8,128)(2,1)S(1)}, u32[]{:S(2)}, u32[]{:S(2)}) collective-permute-start(bf16[1,128,1024]{2,1,0:T(8,128)(2,1)S(1)} %get-tuple-element.17.refs_2_), channel_id=1, source_target_pairs={{0,16},{1,17},{2,18},{3,19},{4,20},{5,21},{6,22},{7,23},{8,24},{9,... | collective-permute-start | bytes 786440 | tf_op jit(solution)/shard_map/ppermute | solution.py:36
  121.0 12.4 %collective-permute-start.25 = (bf16[1,128,1024]{2,1,0:T(8,128)(2,1)S(1)}, bf16[1,128,1024]{2,1,0:T(8,128)(2,1)S(1)}, u32[]{:S(2)}, u32[]{:S(2)}) collective-permute-start(bf16[1,128,1024]{2,1,0:T(8,128)(2,1)S(1)} %collective-permute-done.22.refs_4_), channel_id=1, source_target_pairs={{0,32},{1,33},{2,34},{3,35},{4,36},{5,37},{6,38},{7,39},{8,40},{9,... | collective-permute-start | bytes 786440 | tf_op jit(solution)/shard_map/ppermute | solution.py:36
  125.1 11.8 %collective-permute-start.32 = (bf16[1,64,1024]{2,1,0:T(8,128)(2,1)S(1)}, bf16[1,64,1024]{2,1,0:T(8,128)(2,1)S(1)}, u32[]{:S(2)}, u32[]{:S(2)}) collective-permute-start(bf16[1,64,1024]{2,1,0:T(8,128)(2,1)S(1)} %slice.47), channel_id=1, source_target_pairs={{16,47},{17,34},{18,33},{19,36},{20,35},{21,38},{22,37},{23,40},{2... | collective-permute-start | bytes 393224 | tf_op jit(solution)/shard_map/ppermute | solution.py:36
  127.0 12.3 %collective-permute-start.24 = (bf16[1,128,1024]{2,1,0:T(8,128)(2,1)S(1)}, bf16[1,128,1024]{2,1,0:T(8,128)(2,1)S(1)}, u32[]{:S(2)}, u32[]{:S(2)}) collective-permute-start(bf16[1,128,1024]{2,1,0:T(8,128)(2,1)S(1)} %get-tuple-element.18.refs_3_), channel_id=1, source_target_pairs={{0,16},{1,17},{2,18},{3,19},{4,20},{5,21},{6,22},{7,23},{8,24},{9,... | collective-permute-start | bytes 786440 | tf_op jit(solution)/shard_map/ppermute | solution.py:36
  131.2 15.6 %collective-permute-start.26 = (bf16[1,128,1024]{2,1,0:T(8,128)(2,1)S(1)}, bf16[1,128,1024]{2,1,0:T(8,128)(2,1)S(1)}, u32[]{:S(2)}, u32[]{:S(2)}) collective-permute-start(bf16[1,128,1024]{2,1,0:T(8,128)(2,1)S(1)} %collective-permute-done.23.refs_5_), channel_id=1, source_target_pairs={{0,32},{1,33},{2,34},{3,35},{4,36},{5,37},{6,38},{7,39},{8,40},{9,... | collective-permute-start | bytes 786440 | tf_op jit(solution)/shard_map/ppermute | solution.py:36
  133.2 21.9 %collective-permute-start.30 = (bf16[2,128,1024]{2,1,0:T(8,128)(2,1)S(1)}, bf16[2,128,1024]{2,1,0:T(8,128)(2,1)S(1)}, u32[]{:S(2)}, u32[]{:S(2)}) collective-permute-start(bf16[2,128,1024]{2,1,0:T(8,128)(2,1)S(1)} %pad_maximum_fusion.8), channel_id=1, source_target_pairs={{0,1},{1,0},{2,3},{3,2},{4,5},{5,4},{6,7},{7,6},{8,9},{9,8},{10,11... | collective-permute-start | bytes 1572872 | tf_op jit(solution)/shard_map/ppermute | solution.py:36
  133.3 15.4 %collective-permute-start.31 = (bf16[1,64,1024]{2,1,0:T(8,128)(2,1)S(1)}, bf16[1,64,1024]{2,1,0:T(8,128)(2,1)S(1)}, u32[]{:S(2)}, u32[]{:S(2)}) collective-permute-start(bf16[1,64,1024]{2,1,0:T(8,128)(2,1)S(1)} %slice.53), channel_id=1, source_target_pairs={{0,15},{1,2},{2,1},{3,4},{4,3},{5,6},{6,5},{7,8},{8,7},{9,10},{10,... | collective-permute-start | bytes 393224 | tf_op jit(solution)/shard_map/ppermute | solution.py:36
  136.9 12.1 %collective-permute-start.28 = (bf16[1,128,1024]{2,1,0:T(8,128)(2,1)S(1)}, bf16[1,128,1024]{2,1,0:T(8,128)(2,1)S(1)}, u32[]{:S(2)}, u32[]{:S(2)}) collective-permute-start(bf16[1,128,1024]{2,1,0:T(8,128)(2,1)S(1)} %get-tuple-element.16.refs_1_), channel_id=1, source_target_pairs={{0,15},{1,2},{2,1},{3,4},{4,3},{5,6},{6,5},{7,8},{8,7},{9,10},{10,... | collective-permute-start | bytes 786440 | tf_op jit(solution)/shard_map/ppermute | solution.py:36
  139.3 11.6 %collective-permute-start.29 = (bf16[1,128,1024]{2,1,0:T(8,128)(2,1)S(1)}, bf16[1,128,1024]{2,1,0:T(8,128)(2,1)S(1)}, u32[]{:S(2)}, u32[]{:S(2)}) collective-permute-start(bf16[1,128,1024]{2,1,0:T(8,128)(2,1)S(1)} %get-tuple-element.16.refs_1_), channel_id=1, source_target_pairs={{0,31},{1,18},{2,17},{3,20},{4,19},{5,22},{6,21},{7,24},{8,23},{9,... | collective-permute-start | bytes 786440 | tf_op jit(solution)/shard_map/ppermute | solution.py:36
  146.9 8.3 %collective-permute-start.27 = (bf16[1,128,1024]{2,1,0:T(8,128)(2,1)S(1)}, bf16[1,128,1024]{2,1,0:T(8,128)(2,1)S(1)}, u32[]{:S(2)}, u32[]{:S(2)}) collective-permute-start(bf16[1,128,1024]{2,1,0:T(8,128)(2,1)S(1)} %collective-permute-done.24.refs_6_), channel_id=1, source_target_pairs={{0,32},{1,33},{2,34},{3,35},{4,36},{5,37},{6,38},{7,39},{8,40},{9,... | collective-permute-start | bytes 786440 | tf_op jit(solution)/shard_map/ppermute | solution.py:36
  148.8 6.3 %collective-permute-start.33 = (bf16[1,128,1024]{2,1,0:T(8,128)(2,1)S(1)}, bf16[1,128,1024]{2,1,0:T(8,128)(2,1)S(1)}, u32[]{:S(2)}, u32[]{:S(2)}) collective-permute-start(bf16[1,128,1024]{2,1,0:T(8,128)(2,1)S(1)} %collective-permute-done.26.refs_8_), channel_id=1, source_target_pairs={{0,1},{1,0},{2,3},{3,2},{4,5},{5,4},{6,7},{7,6},{8,9},{9,8},{10,11... | collective-permute-start | bytes 786440 | tf_op jit(solution)/shard_map/ppermute | solution.py:36
